TPU v7x, 128 devices: a whole 4x4x4 slice. The times are simulated.
128 devices in a mesh: fsdp: 16 (over x, z_lo, core), tensor: 8 (over y, z_hi).
Axes of the slice: x: 4, y: 4, z: 4 (z_hi: 2, z_lo: 2; z = z_hi * 2 + z_lo), core: 2. Of those that a mesh axis runs over, the one named last changes fastest.
Arguments:
- tokens: bfloat16 [16384, 4096], P('fsdp'), may hold values from -6 to 6
- input_source: float32 [256, 16, 4096], P('tensor', None, 'fsdp'), may hold values from -0.09375 to 0.09375
- branch_source: float32 [256, 16, 4096], P('tensor', None, 'fsdp'), may hold values from -0.09375 to 0.09375
- output_source: float32 [256, 16, 4096], P('tensor', None, 'fsdp'), may hold values from -0.09375 to 0.09375
- gates_source: float32 [2, 16, 256, 256], P(None, None, 'fsdp', 'tensor'), may hold values from -0.375 to 0.375
- decay_param: float32 [16, 256], replicated, may hold values from -9 to 1
- block_order: int32 [16], replicated, may hold values from 0 to 15, each once
Outputs:
- mixed: bfloat16 [16384, 4096], P('fsdp', 'tensor')
- input_serve: bfloat16 [4096, 4096], P(None, 'tensor')
- branch_serve: bfloat16 [4096, 4096], P(None, 'tensor')
- output_serve: bfloat16 [4096, 4096], P(None, 'tensor')
- gates_serve: bfloat16 [2, 16, 256, 256], P(None, 'tensor')
Inputs may be any that keep to these rules, and one draw needn't show every extreme that they name: `block_order`: every gate block appears exactly once.
All inputs are finite; a program needn't handle non-finite values.
Results may differ from a plain program's by a relative error of at most 0.013.
Values may be sent and summed in bfloat16 or wider, within the bound.
No kernel may reach another device: no remote copies, remote signals or barrier semaphores. Data moves between devices by JAX's collectives and lax.ppermute only.
A program may use at most 128 MiB of HBM per device.

v0:
```python
import jax
import jax.numpy as jnp
from jax import lax
from jax.experimental import pallas as pl
from jax.experimental.pallas import tpu as pltpu
from jax.sharding import PartitionSpec as P


BF = jnp.bfloat16
F32 = jnp.float32


def fsdp_perm(dx=0, dz=0, dc=0):
    out = []
    for f in range(16):
        x, z, c = f // 4, (f // 2) % 2, f % 2
        out.append((f, (((x + dx) % 4) * 2 + (z ^ dz)) * 2 + (c ^ dc)))
    return out


def tensor_perm(dy=0, dz=0):
    return [(t, ((t // 2 + dy) % 4) * 2 + ((t % 2) ^ dz)) for t in range(8)]


CH = 128


def scan_kernel(bi_ref, g_ref, rate_ref, out_ref):
    rate = rate_ref[...]
    low = lax.broadcasted_iota(jnp.int32, (CH // 8, 8, 256), 1) < 4
    dims = (((1,), (1,)), ((), ()))

    def chunk(n, carry):
        rows = pl.ds(pl.multiple_of(n * CH, CH), CH)
        bi = bi_ref[rows, :]
        pre_r = lax.dot_general(bi, g_ref[0, 0], dims, preferred_element_type=F32)
        pre_i = lax.dot_general(bi, g_ref[1, 0], dims, preferred_element_type=F32)
        log_a = -8.0 * rate * jax.nn.sigmoid(pre_r)
        a = jnp.exp(log_a)
        d = jnp.sqrt(1.0 - jnp.exp(2.0 * log_a)) * (jax.nn.sigmoid(pre_i) * bi.astype(F32))
        a = a.reshape(CH // 8, 8, 256)
        d = d.reshape(CH // 8, 8, 256)
        a_prev = jnp.where(low, 1.0, pltpu.roll(a, 4, 1))
        d_prev = jnp.where(low, 0.0, pltpu.roll(d, 4, 1))
        d = a * d_prev + d
        a = a * a_prev
        a_end = jnp.where(low, pltpu.roll(a, 4, 1), a)
        d_end = jnp.where(low, pltpu.roll(d, 4, 1), d)
        states = []
        for k in range(CH // 8):
            states.append(a[k] * carry + d[k])
            carry = a_end[k] * carry + d_end[k]
        out_ref[rows, :] = jnp.concatenate(states, axis=0)
        return carry

    lax.fori_loop(0, 1024 // CH, chunk, jnp.zeros((8, 256), F32))


def gate_scan(branch_in, gates, rate):
    return pl.pallas_call(
        scan_kernel,
        out_shape=jax.ShapeDtypeStruct((1024, 512), F32),
        grid=(2,),
        in_specs=[
            pl.BlockSpec((1024, 256), lambda j: (0, j)),
            pl.BlockSpec((2, 1, 256, 256), lambda j: (0, j, 0, 0)),
            pl.BlockSpec((1, 256), lambda j: (0, j)),
        ],
        out_specs=pl.BlockSpec((1024, 256), lambda j: (0, j)),
        cost_estimate=pl.CostEstimate(
            flops=8_000_000_000, bytes_accessed=4 << 20, transcendentals=4 << 20
        ),
        name="gate_scan",
    )(branch_in, gates, rate)


def send_x(a, dx):
    return lax.ppermute(a, "fsdp", fsdp_perm(dx=dx))


def send_z(a):
    return lax.ppermute(a, "fsdp", fsdp_perm(dz=1))


def send_core(a):
    return lax.ppermute(a, "fsdp", fsdp_perm(dc=1))


def send_y(a, dy):
    return lax.ppermute(a, "tensor", tensor_perm(dy=dy))


def send_zhi(a):
    return lax.ppermute(a, "tensor", tensor_perm(dz=1))


CHUNKS = (640, 384)


def position():
    f = lax.axis_index("fsdp")
    t = lax.axis_index("tensor")
    return f // 4, (f // 2) % 2, f % 2, t // 2, t % 2


def slot_meta(dx):
    x, z, core, _, _ = position()
    at = (x + jnp.array(dx, jnp.int32) + 4) & 3
    return jnp.concatenate([at, core[None], z[None]]).astype(jnp.int32)


def put(w_ref, core, z, owns, peers):
    for j in range(2):
        at = jnp.bitwise_xor(z, j)
        w_ref[at, core] = owns[j]
        w_ref[at, 1 - core] = peers[j]


def place_kernel(meta, own_ref, peer_ref, w_ref):
    core, z = meta[4], meta[5]
    put(w_ref, core, z, (own_ref[0, 0], own_ref[1, 0]), (peer_ref[0, 0], peer_ref[1, 0]))


def place(meta, own, peer):
    src = pl.BlockSpec((2, 1, 256, 512), lambda s, m: (0, s, 0, 0))
    w = pl.pallas_call(
        place_kernel,
        out_shape=jax.ShapeDtypeStruct((8, 2, 256, 512), BF),
        grid_spec=pltpu.PrefetchScalarGridSpec(
            num_scalar_prefetch=1,
            grid=(4,),
            in_specs=[src, src],
            out_specs=pl.BlockSpec((2, 2, 256, 512), lambda s, m: (m[s], 0, 0, 0)),
        ),
        cost_estimate=pl.CostEstimate(flops=4_000_000, bytes_accessed=8 << 20, transcendentals=0),
        name="place",
    )(meta, own, peer)
    return w.reshape(4096, 512)


def matmul_kernel(steps, extra, tail, meta, *refs):
    refs = list(refs)
    tok_ref, own_ref, peer_ref = refs[:3]
    refs = refs[3:]
    core, z = meta[steps], meta[steps + 1]
    step = pl.program_id(0)
    if tail:
        before_ref = refs.pop(0)
        refs.pop(0)
        if extra:
            refs.pop(0)
        else:
            state_ref = refs.pop(0)
    w_ref = refs.pop(0)
    put(w_ref, core, z, (own_ref[0, :256], own_ref[1, :256]), (peer_ref[0, :256], peer_ref[1, :256]))
    if extra:
        g_ref = refs.pop(0)
        put(g_ref, core, z, (own_ref[0, 256:], own_ref[1, 256:]), (peer_ref[0, 256:], peer_ref[1, 256:]))
    w = w_ref[...].reshape(1024, 512)
    if not tail:
        acc_ref = refs.pop(0)

        @pl.when(step == 0)
        def _():
            acc_ref[...] = jnp.dot(tok_ref[...], w, preferred_element_type=F32)

        @pl.when(step > 0)
        def _():
            acc_ref[...] += jnp.dot(tok_ref[...], w, preferred_element_type=F32)

    elif extra:
        out_ref = refs.pop(0)
        out_ref[...] = (before_ref[...] + jnp.dot(tok_ref[...], w, preferred_element_type=F32)).astype(BF)
    else:
        acc_ref = refs.pop()
        acc_ref[...] = before_ref[...] + jnp.dot(tok_ref[...], w, preferred_element_type=F32)
        base = 0
        for size, out_ref in zip(CHUNKS, refs):

            def rows_step(n, _, base=base, out_ref=out_ref):
                rows = pl.ds(pl.multiple_of(base + n * 32, 32), 32)
                value = state_ref[rows, :] * jax.nn.gelu(acc_ref[rows, :], approximate=True)
                out_ref[pl.ds(pl.multiple_of(n * 32, 32), 32), :] = value.astype(BF)
                return 0

            lax.fori_loop(0, size // 32, rows_step, 0)
            base += size


def whole(shape):
    return pl.BlockSpec(shape, lambda s, m: (0,) * len(shape))


def matmul_part(meta, tokens, own, peer, extra, before=None, w=None, g=None, states=None):
    rows = 256 + extra
    steps = own.shape[0] // 2
    tail = before is not None
    src = pl.BlockSpec((2, rows, 512), lambda s, m: (s, 0, 0))
    operands = [tokens, own, peer]
    in_specs = [pl.BlockSpec((1024, 1024), lambda s, m: (0, m[s])), src, src]
    aliases = {}
    scratch = []
    out_shape = [jax.ShapeDtypeStruct((8, 2, 256, 512), BF)]
    out_specs = [pl.BlockSpec((2, 2, 256, 512), lambda s, m: (m[s], 0, 0, 0))]
    if extra:
        out_shape.append(jax.ShapeDtypeStruct((8, 2, extra, 512), BF))
        out_specs.append(pl.BlockSpec((2, 2, extra, 512), lambda s, m: (m[s], 0, 0, 0)))
    if tail:
        operands += [before, w]
        in_specs += [whole((1024, 512)), pl.BlockSpec(memory_space=pl.ANY)]
        aliases = {5: 0}
        if extra:
            operands.append(g)
            in_specs.append(pl.BlockSpec(memory_space=pl.ANY))
            aliases[6] = 1
            out_shape.append(jax.ShapeDtypeStruct((1024, 512), BF))
            out_specs.append(whole((1024, 512)))
        else:
            operands.append(states)
            in_specs.append(whole((1024, 512)))
            out_shape += [jax.ShapeDtypeStruct((size, 512), BF) for size in CHUNKS]
            out_specs += [whole((size, 512)) for size in CHUNKS]
            scratch = [pltpu.VMEM((1024, 512), F32)]
    else:
        out_shape.append(jax.ShapeDtypeStruct((1024, 512), F32))
        out_specs.append(whole((1024, 512)))
    return pl.pallas_call(
        lambda *refs: matmul_kernel(steps, extra, tail, *refs),
        out_shape=out_shape,
        grid_spec=pltpu.PrefetchScalarGridSpec(
            num_scalar_prefetch=1,
            grid=(steps,),
            in_specs=in_specs,
            out_specs=out_specs,
            scratch_shapes=scratch,
        ),
        input_output_aliases=aliases,
        cost_estimate=pl.CostEstimate(
            flops=1_000_000_000 * steps, bytes_accessed=(4 << 20) * steps, transcendentals=0
        ),
    )(meta, *operands)


def project_kernel(meta, g0, g1, g3, fa, fb, own_ref, peer_ref, give_ref, keep_ref, far_ref):
    core = meta[1]
    half = fa.shape[0]
    dims = (((1,), (1,)), ((), ()))
    step = pl.program_id(0)

    @pl.when(step == 0)
    def _():
        far_ref[:half] = fa[...]
        far_ref[half:] = fb[...]

    def side(out_ref):
        for w_ref, at in ((own_ref, core), (peer_ref, 1 - core)):
            cols = pl.ds(pl.multiple_of(at * 256, 256), 256)
            acc = lax.dot_general(g0[...], w_ref[0, 0], dims, preferred_element_type=F32)
            acc += lax.dot_general(g1[...], w_ref[1, 0], dims, preferred_element_type=F32)
            acc += lax.dot_general(far_ref[...], w_ref[2, 0], dims, preferred_element_type=F32)
            acc += lax.dot_general(g3[...], w_ref[3, 0], dims, preferred_element_type=F32)
            out_ref[:, cols] = acc.astype(out_ref.dtype)

    @pl.when(step == 0)
    def _():
        side(give_ref)

    @pl.when(step == 1)
    def _():
        side(keep_ref)


def project(meta, gs, w_own, w_peer):
    size = gs[0].shape[0]
    wspec = pl.BlockSpec((4, 1, 256, 512), lambda s, m: (0, jnp.bitwise_xor(m[0], s), 0, 0))
    return pl.pallas_call(
        project_kernel,
        out_shape=[
            jax.ShapeDtypeStruct((size, 512), BF),
            jax.ShapeDtypeStruct((size, 512), F32),
        ],
        grid_spec=pltpu.PrefetchScalarGridSpec(
            num_scalar_prefetch=1,
            grid=(2,),
            in_specs=[whole(g.shape) for g in gs] + [wspec, wspec],
            out_specs=[whole((size, 512))] * 2,
            scratch_shapes=[pltpu.VMEM((size, 512), BF)],
        ),
        cost_estimate=pl.CostEstimate(
            flops=size * 2048 * 2048, bytes_accessed=8 << 20, transcendentals=0
        ),
        name="project",
    )(meta, *gs, w_own, w_peer)


def gather_z_first(q):
    other = send_z(q)
    pair = jnp.stack([q, other])
    left = send_x(pair, 1)
    right = send_x(pair, -1)
    far_own = send_x(left[0], 1)
    far_other = send_x(right[1], -1)
    near = jnp.concatenate([pair, left, right])
    far = jnp.stack([far_own, far_other])
    return near, send_core(near), far, send_core(far)


def on_device(
    tokens, input_source, branch_source, output_source, gates_source, decay_param, block_order
):
    x, z, core, y, zh = position()
    own_blocks = lax.dynamic_slice_in_dim(block_order, (y * 2 + zh) * 2, 2)

    def section(w):
        picked = jnp.take(w.astype(BF), block_order, axis=1)
        return jnp.transpose(picked, (1, 0, 2)).reshape(8, 64, 256)

    gates_picked = jnp.take(gates_source.astype(BF), block_order, axis=1)
    gates_flat = jnp.transpose(gates_picked.reshape(2, 8, 2, 16, 32), (1, 0, 2, 3, 4)).reshape(8, 8, 256)
    packed = jnp.concatenate(
        [section(input_source), section(branch_source), section(output_source), gates_flat], axis=1
    )
    swapped = lax.all_to_all(packed, "tensor", 0, 0, tiled=True)

    def piece(n):
        part = swapped[:, n * 64 : (n + 1) * 64].reshape(8, 2, 32, 256)
        return jnp.transpose(part, (3, 1, 0, 2)).reshape(256, 512)

    gate_part = swapped[:, 192:200].reshape(8, 2, 2, 16, 32)
    gate_rows = jnp.transpose(gate_part, (1, 2, 3, 0, 4)).reshape(32, 512)

    near_meta = slot_meta((0, -1, 1))
    far_meta = slot_meta((2,))
    row_meta = slot_meta((0, 1, 2, 3))

    q = piece(2)
    left = send_x(q, 1)
    right = send_x(q, -1)
    far_top = send_x(left[:128], 1)
    far_low = send_x(right[128:], -1)
    row = jnp.stack([q, right, jnp.concatenate([far_top, far_low]), left])
    other_row = send_z(row)

    def along_y(row):
        got = [lax.dynamic_index_in_dim(row, (y - x) & 3, 0, keepdims=False)]
        for r in (1, 2, 3):
            block = lax.dynamic_index_in_dim(row, (y - r - x) & 3, 0, keepdims=False)
            got.append(send_y(block, -r))
        return jnp.stack(got)

    w_own = jnp.stack([along_y(row), along_y(other_row)], axis=1)
    w_peer = send_core(w_own)
    out_own = jnp.stack([row, other_row])
    out_peer = send_core(out_own)

    in_near, in_near_peer, in_far, in_far_peer = gather_z_first(
        jnp.concatenate([piece(0), gate_rows])
    )
    br_near, br_near_peer, br_far, br_far_peer = gather_z_first(piece(1))

    w, g, acc = matmul_part(near_meta, tokens, in_near, in_near_peer, 32)
    w, g, branch_in = matmul_part(far_meta, tokens, in_far, in_far_peer, 32, before=acc, w=w, g=g)
    input_serve = w.reshape(4096, 512)
    gate_all = g.reshape(16, 32, 512)
    gates_serve = jnp.transpose(gate_all.reshape(16, 2, 2, 16, 256), (1, 2, 4, 0, 3)).reshape(2, 2, 256, 256)
    rate = jax.nn.softplus(jnp.take(decay_param, own_blocks, axis=0)).reshape(1, 512)
    states = gate_scan(branch_in, gates_serve, rate)
    w, acc = matmul_part(near_meta, tokens, br_near, br_near_peer, 0)
    w, *gated = matmul_part(
        far_meta, tokens, br_far, br_far_peer, 0, before=acc, w=w, states=states
    )
    branch_serve = w.reshape(4096, 512)
    output_serve = place(row_meta, out_own, out_peer)

    give_meta = jnp.stack([(1 - zh) ^ z, core]).astype(jnp.int32)
    parts = []
    for g in gated:
        half = g.shape[0] // 2
        below = send_y(g, 1)
        above = send_y(g, -1)
        far_a = send_y(below[:half], 1)
        far_b = send_y(above[half:], -1)
        terms = (g, above, below, far_a, far_b)
        give, keep = project(give_meta, terms, w_own, w_peer)
        got = send_zhi(give)
        parts.append((keep + got.astype(F32)).astype(BF))
    mixed = jnp.concatenate(parts)
    return (mixed, input_serve, branch_serve, output_serve, gates_serve)


def solution(mesh):
    return jax.shard_map(
        on_device,
        mesh=mesh,
        in_specs=(
            P("fsdp", None),
            P("tensor", None, "fsdp"),
            P("tensor", None, "fsdp"),
            P("tensor", None, "fsdp"),
            P(None, None, "fsdp", "tensor"),
            P(),
            P(),
        ),
        out_specs=(
            P("fsdp", "tensor"),
            P(None, "tensor"),
            P(None, "tensor"),
            P(None, "tensor"),
            P(None, "tensor", None, None),
        ),
        check_vma=False,
    )
```

profile of v0, /device:TPU:0, one launch (start us, length us, event | category | flops | bytes accessed | tf_op | source)
XLA Modules:
  0.0 223.2 jit_solution(14485403635863033030)
XLA Ops:
  8.7 7.9 %all-to-all-start = ((bf16[8,200,256]{2,1,0:T(8,128)(2,1)}), bf16[8,200,256]{2,1,0:T(8,128)(2,1)S(1)}, u32[]{:S(2)}, u32[]{:S(2)}) async-start(bf16[8,200,256]{2,1,0:T(8,128)(2,1)} %pad_maximum_fusion.6), calls=%async_computation | async-start | bytes 1638400 | tf_op jit(solution)/shard_map/all_to_all | solution.py:323
  18.0 12.2 %all-to-all-done = bf16[8,200,256]{2,1,0:T(8,128)(2,1)S(1)} async-done(((bf16[8,200,256]{2,1,0:T(8,128)(2,1)}), bf16[8,200,256]{2,1,0:T(8,128)(2,1)S(1)}, u32[]{:S(2)}, u32[]{:S(2)}) %all-to-all-start) | async-done | bytes 819232 | tf_op jit(solution)/shard_map/all_to_all | solution.py:323
  38.9 3.2 %collective-permute-start.3 = (bf16[2,256,512]{2,1,0:T(8,128)(2,1)S(1)}, bf16[2,256,512]{2,1,0:T(8,128)(2,1)S(1)}, u32[]{:S(2)}, u32[]{:S(2)}) collective-permute-start(bf16[2,256,512]{2,1,0:T(8,128)(2,1)S(1)} %pad_maximum_fusion.9), channel_id=1, source_target_pairs={{0,96},{8,104},{16,112},{24,120},{32,0},{40,8},{48,16},{56,24},{64... | collective-permute-start | bytes 1572872 | tf_op jit(solution)/shard_map/ppermute | solution.py:78
  43.2 2.4 %collective-permute-start.21 = (bf16[128,512]{1,0:T(8,128)(2,1)}, bf16[128,512]{1,0:T(8,128)(2,1)}, u32[]{:S(2)}, u32[]{:S(2)}) collective-permute-start(bf16[128,512]{1,0:T(8,128)(2,1)} %slice.77), channel_id=1, source_target_pairs={{0,96},{8,104},{16,112},{24,120},{32,0},{40,8},{48,16},{56,24},{64... | collective-permute-start | bytes 393224 | tf_op jit(solution)/shard_map/ppermute | solution.py:78
  48.7 1.8 collective-permute-start.10
  50.4 6.9 %collective-permute-done.21 = bf16[128,512]{1,0:T(8,128)(2,1)} collective-permute-done((bf16[128,512]{1,0:T(8,128)(2,1)}, bf16[128,512]{1,0:T(8,128)(2,1)}, u32[]{:S(2)}, u32[]{:S(2)}) %collective-permute-start.21) | collective-permute-done | bytes 131104 | tf_op jit(solution)/shard_map/ppermute | solution.py:78
  62.2 2.4 %collective-permute-done.1 = bf16[2,256,512]{2,1,0:T(8,128)(2,1)S(1)} collective-permute-done((bf16[2,256,512]{2,1,0:T(8,128)(2,1)S(1)}, bf16[2,256,512]{2,1,0:T(8,128)(2,1)S(1)}, u32[]{:S(2)}, u32[]{:S(2)}) %collective-permute-start.1) | collective-permute-done | bytes 524320 | tf_op jit(solution)/shard_map/ppermute | solution.py:78
  64.6 2.7 %collective-permute-start.23 = (bf16[256,512]{1,0:T(8,128)(2,1)S(1)}, bf16[256,512]{1,0:T(8,128)(2,1)S(1)}, u32[]{:S(2)}, u32[]{:S(2)}) collective-permute-start(bf16[256,512]{1,0:T(8,128)(2,1)S(1)} %get-tuple-element.47), channel_id=1, source_target_pairs={{0,4},{1,5},{2,6},{3,7},{4,0},{5,1},{6,2},{7,3},{8,12},{9,13},{10,... | collective-permute-start | bytes 786440 | tf_op jit(solution)/shard_map/ppermute | solution.py:90
  68.9 5.0 %collective-permute-done.8 = bf16[2,288,512]{2,1,0:T(8,128)(2,1)S(1)} collective-permute-done((bf16[2,288,512]{2,1,0:T(8,128)(2,1)S(1)}, bf16[2,288,512]{2,1,0:T(8,128)(2,1)S(1)}, u32[]{:S(2)}, u32[]{:S(2)}) %collective-permute-start.8) | collective-permute-done | bytes 589856 | tf_op jit(solution)/shard_map/ppermute | solution.py:78
  78.0 6.1 %collective-permute-done.4 = bf16[256,512]{1,0:T(8,128)(2,1)S(1)} collective-permute-done((bf16[256,512]{1,0:T(8,128)(2,1)S(1)}, bf16[256,512]{1,0:T(8,128)(2,1)S(1)}, u32[]{:S(2)}, u32[]{:S(2)}) %collective-permute-start.4) | collective-permute-done | bytes 262176 | tf_op jit(solution)/shard_map/ppermute | solution.py:78
  84.1 2.1 collective-permute-start.11
  86.6 5.6 %collective-permute-done.11 = bf16[288,512]{1,0:T(8,128)(2,1)S(1)} collective-permute-done((bf16[288,512]{1,0:T(8,128)(2,1)S(1)}, bf16[288,512]{1,0:T(8,128)(2,1)S(1)}, u32[]{:S(2)}, u32[]{:S(2)}) %collective-permute-start.11) | collective-permute-done | bytes 294944 | tf_op jit(solution)/shard_map/ppermute | solution.py:78
  92.2 2.8 %collective-permute-start.27 = (bf16[256,512]{1,0:T(8,128)(2,1)S(1)}, bf16[256,512]{1,0:T(8,128)(2,1)S(1)}, u32[]{:S(2)}, u32[]{:S(2)}) collective-permute-start(bf16[256,512]{1,0:T(8,128)(2,1)S(1)} %get-tuple-element.51), channel_id=1, source_target_pairs={{0,4},{1,5},{2,6},{3,7},{4,0},{5,1},{6,2},{7,3},{8,12},{9,13},{10,... | collective-permute-start | bytes 786440 | tf_op jit(solution)/shard_map/ppermute | solution.py:90
  97.5 3.1 %collective-permute-done.28 = bf16[256,512]{1,0:T(8,128)(2,1)S(1)} collective-permute-done((bf16[256,512]{1,0:T(8,128)(2,1)S(1)}, bf16[256,512]{1,0:T(8,128)(2,1)S(1)}, u32[]{:S(2)}, u32[]{:S(2)}) %collective-permute-start.28) | collective-permute-done | bytes 262176 | tf_op jit(solution)/shard_map/ppermute | solution.py:90
  101.1 2.2 collective-permute-done.26
  105.3 9.4 %shard_map.137 = (bf16[8,2,256,512]{3,2,1,0:T(8,128)(2,1)}, f32[1024,512]{1,0:T(8,128)}) custom-call(s32[5]{0:T(128)} %pad_add_fusion.2.refs_0_, bf16[1024,4096]{1,0:T(8,128)(2,1)} %refs_1_.7, bf16[6,256,512]{2,1,0:T(8,128)(2,1)} %copy-done.2, bf16[6,256,512]{2,1,0:T(8,128)(2,1)} %copy-done.5), custom_call_target="tpu_custom_call" | custom-call | flops 3000000000 | bytes 12582912 | tf_op jit(solution)/shard_map/pallas_call | solution.py:227
  114.7 9.6 %shard_map.138 = (bf16[8,2,256,512]{3,2,1,0:T(8,128)(2,1)}, bf16[8,2,32,512]{3,2,1,0:T(8,128)(2,1)}, f32[1024,512]{1,0:T(8,128)}) custom-call(s32[5]{0:T(128)} %pad_add_fusion.2.refs_0_, bf16[1024,4096]{1,0:T(8,128)(2,1)} %refs_1_.7, bf16[6,288,512]{2,1,0:T(8,128)(2,1)} %pad_maximum_fusion.2.refs_2_, bf16[6,288,512]{2,1,0:T(8,128)(2,1)} %collective-permute-done.13.refs_3_), custom_call_target="tpu_custom_call" | custom-call | flops 3000000000 | bytes 12582912 | tf_op jit(solution)/shard_map/pallas_call | solution.py:227
  124.3 5.6 %shard_map.139 = (bf16[8,2,256,512]{3,2,1,0:T(8,128)(2,1)}, bf16[8,2,32,512]{3,2,1,0:T(8,128)(2,1)}, bf16[1024,512]{1,0:T(8,128)(2,1)}) custom-call(s32[3]{0:T(128)} %pad_add_fusion.1.refs_0_, bf16[1024,4096]{1,0:T(8,128)(2,1)} %refs_1_.7, bf16[2,288,512]{2,1,0:T(8,128)(2,1)} %copy-done.3, ...), custom_call_target="tpu_custom_call", output_to_operand_aliasing={{0}: (5, {}), {1}: (6, {})} | custom-call | flops 1000000000 | bytes 4194304 | tf_op jit(solution)/shard_map/pallas_call | solution.py:227
  131.9 2.0 copy.36.g_ref
  134.0 7.9 %gate_scan.1.refs_6_ = f32[1024,512]{1,0:T(8,128)} custom-call(bf16[1024,512]{1,0:T(8,128)(2,1)} %get-tuple-element.26.bi_ref, bf16[2,2,256,256]{3,2,1,0:T(8,128)(2,1)} %copy.36.g_ref, f32[1,512]{1,0:T(1,128)} %compare_select_fusion.rate_ref), custom_call_target="tpu_custom_call" | custom-call | flops 8000000000 | bytes 4194304 | tf_op jit(solution)/shard_map/gate_scan/pallas_call | solution.py:60
  141.8 7.5 %shard_map.140 = (bf16[8,2,256,512]{3,2,1,0:T(8,128)(2,1)}, bf16[640,512]{1,0:T(8,128)(2,1)}, bf16[384,512]{1,0:T(8,128)(2,1)}) custom-call(s32[3]{0:T(128)} %pad_add_fusion.1.refs_0_, bf16[1024,4096]{1,0:T(8,128)(2,1)} %refs_1_.7, bf16[2,256,512]{2,1,0:T(8,128)(2,1)} %copy-done.4, ...), custom_call_target="tpu_custom_call", output_to_operand_aliasing={{0}: (5, {})} | custom-call | flops 1000000000 | bytes 4194304 | tf_op jit(solution)/shard_map/pallas_call | solution.py:227
  151.2 2.7 %collective-permute-start.14 = (bf16[640,512]{1,0:T(8,128)(2,1)}, bf16[640,512]{1,0:T(8,128)(2,1)S(1)}, u32[]{:S(2)}, u32[]{:S(2)}) collective-permute-start(bf16[640,512]{1,0:T(8,128)(2,1)} %get-tuple-element.28.g0), channel_id=1, source_target_pairs={{0,6},{1,7},{2,0},{3,1},{4,2},{5,3},{6,4},{7,5},{8,14},{9,15},{10,... | collective-permute-start | bytes 1966088 | tf_op jit(solution)/shard_map/ppermute | solution.py:90
  153.9 8.8 %collective-permute-done.32.g3 = bf16[384,512]{1,0:T(8,128)(2,1)S(1)} collective-permute-done((bf16[384,512]{1,0:T(8,128)(2,1)}, bf16[384,512]{1,0:T(8,128)(2,1)S(1)}, u32[]{:S(2)}, u32[]{:S(2)}) %collective-permute-start.32) | collective-permute-done | bytes 393248 | tf_op jit(solution)/shard_map/ppermute | solution.py:90
  164.2 12.2 %collective-permute-done.31.g1 = bf16[384,512]{1,0:T(8,128)(2,1)S(1)} collective-permute-done((bf16[384,512]{1,0:T(8,128)(2,1)}, bf16[384,512]{1,0:T(8,128)(2,1)S(1)}, u32[]{:S(2)}, u32[]{:S(2)}) %collective-permute-start.31) | collective-permute-done | bytes 393248 | tf_op jit(solution)/shard_map/ppermute | solution.py:90
  178.2 2.4 %collective-permute-start.34 = (bf16[192,512]{1,0:T(8,128)(2,1)S(1)}, bf16[192,512]{1,0:T(8,128)(2,1)}, u32[]{:S(2)}, u32[]{:S(2)}) collective-permute-start(bf16[192,512]{1,0:T(8,128)(2,1)S(1)} %slice.79), channel_id=1, source_target_pairs={{0,6},{1,7},{2,0},{3,1},{4,2},{5,3},{6,4},{7,5},{8,14},{9,15},{10,... | collective-permute-start | bytes 589832 | tf_op jit(solution)/shard_map/ppermute | solution.py:90
  181.5 2.8 %collective-permute-start.17 = (bf16[320,512]{1,0:T(8,128)(2,1)S(1)}, bf16[320,512]{1,0:T(8,128)(2,1)}, u32[]{:S(2)}, u32[]{:S(2)}) collective-permute-start(bf16[320,512]{1,0:T(8,128)(2,1)S(1)} %slice.74), channel_id=1, source_target_pairs={{0,6},{1,7},{2,0},{3,1},{4,2},{5,3},{6,4},{7,5},{8,14},{9,15},{10,... | collective-permute-start | bytes 983048 | tf_op jit(solution)/shard_map/ppermute | solution.py:90
  186.5 3.1 %copy.43.peer_ref = bf16[4,2,256,512]{3,2,1,0:T(8,128)(2,1)} copy(bf16[4,2,256,512]{3,2,0,1:T(8,128)(2,1)} %collective-permute-done.29) | data formatting | bytes 4194304 | tf_op jit(solution)/shard_map/ppermute | solution.py:86
  189.6 5.8 %project.3 = (bf16[384,512]{1,0:T(8,128)(2,1)}, f32[384,512]{1,0:T(8,128)}) custom-call(s32[2]{0:T(128)} %pad_add_fusion.meta, bf16[384,512]{1,0:T(8,128)(2,1)} %get-tuple-element.31.g0, bf16[384,512]{1,0:T(8,128)(2,1)} %copy-done.13, bf16[384,512]{1,0:T(8,128)(2,1)} %copy-done.12, bf16[192,512]{1,0:T(8,128)(2,1)} %collective-permute-done.33.fa, ...), custom_call_target="tpu_custom_call" | custom-call | flops 1610612736 | bytes 8388608 | tf_op jit(solution)/shard_map/project/pallas_call | solution.py:276
  195.4 3.1 %collective-permute-start.35 = (bf16[384,512]{1,0:T(8,128)(2,1)}, bf16[384,512]{1,0:T(8,128)(2,1)S(1)}, u32[]{:S(2)}, u32[]{:S(2)}) collective-permute-start(bf16[384,512]{1,0:T(8,128)(2,1)} %get-tuple-element.33), channel_id=1, source_target_pairs={{0,1},{1,0},{2,3},{3,2},{4,5},{5,4},{6,7},{7,6},{8,9},{9,8},{10,11... | collective-permute-start | bytes 1179656 | tf_op jit(solution)/shard_map/ppermute | solution.py:94
  198.5 7.5 %project.2 = (bf16[640,512]{1,0:T(8,128)(2,1)}, f32[640,512]{1,0:T(8,128)}) custom-call(s32[2]{0:T(128)} %pad_add_fusion.meta, bf16[640,512]{1,0:T(8,128)(2,1)} %get-tuple-element.28.g0, bf16[640,512]{1,0:T(8,128)(2,1)} %copy-done.11, bf16[640,512]{1,0:T(8,128)(2,1)} %copy-done.10, bf16[320,512]{1,0:T(8,128)(2,1)} %collective-permute-done.16.fa, ...), custom_call_target="tpu_custom_call" | custom-call | flops 2684354560 | bytes 8388608 | tf_op jit(solution)/shard_map/project/pallas_call | solution.py:276
  207.1 5.5 %place.1 = bf16[8,2,256,512]{3,2,1,0:T(8,128)(2,1)} custom-call(s32[6]{0:T(128)} %pad_add_fusion.3.meta, bf16[2,4,256,512]{3,2,1,0:T(8,128)(2,1)} %pad_maximum_fusion.1.own_ref, bf16[2,4,256,512]{3,2,1,0:T(8,128)(2,1)} %collective-permute-done.36.peer_ref), custom_call_target="tpu_custom_call" | custom-call | flops 4000000 | bytes 8388608 | tf_op jit(solution)/shard_map/place/pallas_call | solution.py:126
  212.7 9.2 %collective-permute-done.30 = bf16[640,512]{1,0:T(8,128)(2,1)S(1)} collective-permute-done((bf16[640,512]{1,0:T(8,128)(2,1)}, bf16[640,512]{1,0:T(8,128)(2,1)S(1)}, u32[]{:S(2)}, u32[]{:S(2)}) %collective-permute-start.30) | collective-permute-done | bytes 655392 | tf_op jit(solution)/shard_map/ppermute | solution.py:94
  (158 shorter events, 50.8 us)
Async XLA Ops:
  8.7 21.5 %all-to-all-start = ((bf16[8,200,256]{2,1,0:T(8,128)(2,1)}), bf16[8,200,256]{2,1,0:T(8,128)(2,1)S(1)}, u32[]{:S(2)}, u32[]{:S(2)}) async-start(bf16[8,200,256]{2,1,0:T(8,128)(2,1)} %pad_maximum_fusion.6), calls=%async_computation | async-start | bytes 1638400 | tf_op jit(solution)/shard_map/all_to_all | solution.py:323
  32.4 13.1 %collective-permute-start.19 = (bf16[256,512]{1,0:T(8,128)(2,1)}, bf16[256,512]{1,0:T(8,128)(2,1)S(1)}, u32[]{:S(2)}, u32[]{:S(2)}) collective-permute-start(bf16[256,512]{1,0:T(8,128)(2,1)} %copy.39), channel_id=1, source_target_pairs={{0,32},{8,40},{16,48},{24,56},{32,64},{40,72},{48,80},{56,88},{64,... | collective-permute-start | bytes 786440 | tf_op jit(solution)/shard_map/ppermute | solution.py:78
  37.0 11.6 %collective-permute-start.7 = (bf16[288,512]{1,0:T(8,128)(2,1)}, bf16[288,512]{1,0:T(8,128)(2,1)S(1)}, u32[]{:S(2)}, u32[]{:S(2)}) collective-permute-start(bf16[288,512]{1,0:T(8,128)(2,1)} %get-tuple-element.57), channel_id=1, source_target_pairs={{0,16},{8,24},{16,0},{24,8},{32,48},{40,56},{48,32},{56,40},{64,80... | collective-permute-start | bytes 884744 | tf_op jit(solution)/shard_map/ppermute | solution.py:82
  38.9 22.0 %collective-permute-start.3 = (bf16[2,256,512]{2,1,0:T(8,128)(2,1)S(1)}, bf16[2,256,512]{2,1,0:T(8,128)(2,1)S(1)}, u32[]{:S(2)}, u32[]{:S(2)}) collective-permute-start(bf16[2,256,512]{2,1,0:T(8,128)(2,1)S(1)} %pad_maximum_fusion.9), channel_id=1, source_target_pairs={{0,96},{8,104},{16,112},{24,120},{32,0},{40,8},{48,16},{56,24},{64... | collective-permute-start | bytes 1572872 | tf_op jit(solution)/shard_map/ppermute | solution.py:78
  43.2 14.1 %collective-permute-start.21 = (bf16[128,512]{1,0:T(8,128)(2,1)}, bf16[128,512]{1,0:T(8,128)(2,1)}, u32[]{:S(2)}, u32[]{:S(2)}) collective-permute-start(bf16[128,512]{1,0:T(8,128)(2,1)} %slice.77), channel_id=1, source_target_pairs={{0,96},{8,104},{16,112},{24,120},{32,0},{40,8},{48,16},{56,24},{64... | collective-permute-start | bytes 393224 | tf_op jit(solution)/shard_map/ppermute | solution.py:78
  46.2 12.4 %collective-permute-start.20 = (bf16[128,512]{1,0:T(8,128)(2,1)}, bf16[128,512]{1,0:T(8,128)(2,1)}, u32[]{:S(2)}, u32[]{:S(2)}) collective-permute-start(bf16[128,512]{1,0:T(8,128)(2,1)} %slice.76), channel_id=1, source_target_pairs={{0,32},{8,40},{16,48},{24,56},{32,64},{40,72},{48,80},{56,88},{64,... | collective-permute-start | bytes 393224 | tf_op jit(solution)/shard_map/ppermute | solution.py:78
  46.9 17.7 %collective-permute-start.1 = (bf16[2,256,512]{2,1,0:T(8,128)(2,1)S(1)}, bf16[2,256,512]{2,1,0:T(8,128)(2,1)S(1)}, u32[]{:S(2)}, u32[]{:S(2)}) collective-permute-start(bf16[2,256,512]{2,1,0:T(8,128)(2,1)S(1)} %pad_maximum_fusion.9), channel_id=1, source_target_pairs={{0,32},{8,40},{16,48},{24,56},{32,64},{40,72},{48,80},{56,88},{64,... | collective-permute-start | bytes 1572872 | tf_op jit(solution)/shard_map/ppermute | solution.py:78
  48.7 19.2 %collective-permute-start.10 = (bf16[2,288,512]{2,1,0:T(8,128)(2,1)S(1)}, bf16[2,288,512]{2,1,0:T(8,128)(2,1)S(1)}, u32[]{:S(2)}, u32[]{:S(2)}) collective-permute-start(bf16[2,288,512]{2,1,0:T(8,128)(2,1)S(1)} %pad_maximum_fusion.7), channel_id=1, source_target_pairs={{0,96},{8,104},{16,112},{24,120},{32,0},{40,8},{48,16},{56,24},{64... | collective-permute-start | bytes 1769480 | tf_op jit(solution)/shard_map/ppermute | solution.py:78
  57.3 16.6 %collective-permute-start.8 = (bf16[2,288,512]{2,1,0:T(8,128)(2,1)S(1)}, bf16[2,288,512]{2,1,0:T(8,128)(2,1)S(1)}, u32[]{:S(2)}, u32[]{:S(2)}) collective-permute-start(bf16[2,288,512]{2,1,0:T(8,128)(2,1)S(1)} %pad_maximum_fusion.7), channel_id=1, source_target_pairs={{0,32},{8,40},{16,48},{24,56},{32,64},{40,72},{48,80},{56,88},{64,... | collective-permute-start | bytes 1769480 | tf_op jit(solution)/shard_map/ppermute | solution.py:78
  59.8 26.7 %collective-permute-start.25 = (bf16[4,256,512]{2,1,0:T(8,128)(2,1)S(1)}, bf16[4,256,512]{2,1,0:T(8,128)(2,1)S(1)}, u32[]{:S(2)}, u32[]{:S(2)}) collective-permute-start(bf16[4,256,512]{2,1,0:T(8,128)(2,1)S(1)} %get-tuple-element.44), channel_id=1, source_target_pairs={{0,16},{8,24},{16,0},{24,8},{32,48},{40,56},{48,32},{56,40},{64,80... | collective-permute-start | bytes 3145736 | tf_op jit(solution)/shard_map/ppermute | solution.py:82
  60.9 14.4 %collective-permute-start.24 = (bf16[256,512]{1,0:T(8,128)(2,1)S(1)}, bf16[256,512]{1,0:T(8,128)(2,1)S(1)}, u32[]{:S(2)}, u32[]{:S(2)}) collective-permute-start(bf16[256,512]{1,0:T(8,128)(2,1)S(1)} %get-tuple-element.46), channel_id=1, source_target_pairs={{0,2},{1,3},{2,4},{3,5},{4,6},{5,7},{6,0},{7,1},{8,10},{9,11},{10,... | collective-permute-start | bytes 786440 | tf_op jit(solution)/shard_map/ppermute | solution.py:90
  64.6 11.2 %collective-permute-start.23 = (bf16[256,512]{1,0:T(8,128)(2,1)S(1)}, bf16[256,512]{1,0:T(8,128)(2,1)S(1)}, u32[]{:S(2)}, u32[]{:S(2)}) collective-permute-start(bf16[256,512]{1,0:T(8,128)(2,1)S(1)} %get-tuple-element.47), channel_id=1, source_target_pairs={{0,4},{1,5},{2,6},{3,7},{4,0},{5,1},{6,2},{7,3},{8,12},{9,13},{10,... | collective-permute-start | bytes 786440 | tf_op jit(solution)/shard_map/ppermute | solution.py:90
  67.9 8.9 %collective-permute-start.22 = (bf16[256,512]{1,0:T(8,128)(2,1)S(1)}, bf16[256,512]{1,0:T(8,128)(2,1)S(1)}, u32[]{:S(2)}, u32[]{:S(2)}) collective-permute-start(bf16[256,512]{1,0:T(8,128)(2,1)S(1)} %get-tuple-element.48), channel_id=1, source_target_pairs={{0,6},{1,7},{2,0},{3,1},{4,2},{5,3},{6,4},{7,5},{8,14},{9,15},{10,... | collective-permute-start | bytes 786440 | tf_op jit(solution)/shard_map/ppermute | solution.py:90
  73.9 29.7 %collective-permute-start.6 = (bf16[6,256,512]{2,1,0:T(8,128)(2,1)S(1)}, bf16[6,256,512]{2,1,0:T(8,128)(2,1)S(1)}, u32[]{:S(2)}, u32[]{:S(2)}) collective-permute-start(bf16[6,256,512]{2,1,0:T(8,128)(2,1)S(1)} %pad_maximum_fusion.3.refs_2_), channel_id=1, source_target_pairs={{0,8},{8,0},{16,24},{24,16},{32,40},{40,32},{48,56},{56,48},{64,72... | collective-permute-start | bytes 4718600 | tf_op jit(solution)/shard_map/ppermute | solution.py:86
  75.3 39.4 %collective-permute-start.13 = (bf16[6,288,512]{2,1,0:T(8,128)(2,1)}, bf16[6,288,512]{2,1,0:T(8,128)(2,1)}, u32[]{:S(2)}, u32[]{:S(2)}) collective-permute-start(bf16[6,288,512]{2,1,0:T(8,128)(2,1)} %pad_maximum_fusion.2.refs_2_), channel_id=1, source_target_pairs={{0,8},{8,0},{16,24},{24,16},{32,40},{40,32},{48,56},{56,48},{64,72... | collective-permute-start | bytes 5308424 | tf_op jit(solution)/shard_map/ppermute | solution.py:86
  76.8 9.4 %collective-permute-start.2 = (bf16[256,512]{1,0:T(8,128)(2,1)S(1)}, bf16[256,512]{1,0:T(8,128)(2,1)S(1)}, u32[]{:S(2)}, u32[]{:S(2)}) collective-permute-start(bf16[256,512]{1,0:T(8,128)(2,1)S(1)} %slice_bitcast_fusion.3), channel_id=1, source_target_pairs={{0,32},{8,40},{16,48},{24,56},{32,64},{40,72},{48,80},{56,88},{64,... | collective-permute-start | bytes 786440 | tf_op jit(solution)/shard_map/ppermute | solution.py:78
  86.2 9.0 %collective-permute-start.9 = (bf16[288,512]{1,0:T(8,128)(2,1)S(1)}, bf16[288,512]{1,0:T(8,128)(2,1)S(1)}, u32[]{:S(2)}, u32[]{:S(2)}) collective-permute-start(bf16[288,512]{1,0:T(8,128)(2,1)S(1)} %slice_bitcast_fusion.1), channel_id=1, source_target_pairs={{0,32},{8,40},{16,48},{24,56},{32,64},{40,72},{48,80},{56,88},{64,... | collective-permute-start | bytes 884744 | tf_op jit(solution)/shard_map/ppermute | solution.py:78
  86.5 14.0 %collective-permute-start.28 = (bf16[256,512]{1,0:T(8,128)(2,1)S(1)}, bf16[256,512]{1,0:T(8,128)(2,1)S(1)}, u32[]{:S(2)}, u32[]{:S(2)}) collective-permute-start(bf16[256,512]{1,0:T(8,128)(2,1)S(1)} %get-tuple-element.50), channel_id=1, source_target_pairs={{0,2},{1,3},{2,4},{3,5},{4,6},{5,7},{6,0},{7,1},{8,10},{9,11},{10,... | collective-permute-start | bytes 786440 | tf_op jit(solution)/shard_map/ppermute | solution.py:90
  100.5 41.3 %collective-permute-start.5 = (bf16[2,256,512]{2,1,0:T(8,128)(2,1)S(1)}, bf16[2,256,512]{2,1,0:T(8,128)(2,1)}, u32[]{:S(2)}, u32[]{:S(2)}) collective-permute-start(bf16[2,256,512]{2,1,0:T(8,128)(2,1)S(1)} %pad_maximum_fusion.10.refs_2_), channel_id=1, source_target_pairs={{0,8},{8,0},{16,24},{24,16},{32,40},{40,32},{48,56},{56,48},{64,72... | collective-permute-start | bytes 1572872 | tf_op jit(solution)/shard_map/ppermute | solution.py:86
  100.6 23.7 %collective-permute-start.12 = (bf16[2,288,512]{2,1,0:T(8,128)(2,1)S(1)}, bf16[2,288,512]{2,1,0:T(8,128)(2,1)}, u32[]{:S(2)}, u32[]{:S(2)}) collective-permute-start(bf16[2,288,512]{2,1,0:T(8,128)(2,1)S(1)} %pad_maximum_fusion.8.refs_2_), channel_id=1, source_target_pairs={{0,8},{8,0},{16,24},{24,16},{32,40},{40,32},{48,56},{56,48},{64,72... | collective-permute-start | bytes 1769480 | tf_op jit(solution)/shard_map/ppermute | solution.py:86
  103.2 103.8 %collective-permute-start.36 = (bf16[2,4,256,512]{3,2,1,0:T(8,128)(2,1)}, bf16[2,4,256,512]{3,2,1,0:T(8,128)(2,1)}, u32[]{:S(2)}, u32[]{:S(2)}) collective-permute-start(bf16[2,4,256,512]{3,2,1,0:T(8,128)(2,1)} %pad_maximum_fusion.1.own_ref), channel_id=1, source_target_pairs={{0,8},{8,0},{16,24},{24,16},{32,40},{40,32},{48,56},{56,48},{64,72... | collective-permute-start | bytes 6291464 | tf_op jit(solution)/shard_map/ppermute | solution.py:86
  104.8 75.9 %collective-permute-start.29 = (bf16[4,2,256,512]{3,2,0,1:T(8,128)(2,1)S(1)}, bf16[4,2,256,512]{3,2,0,1:T(8,128)(2,1)}, u32[]{:S(2)}, u32[]{:S(2)}) collective-permute-start(bf16[4,2,256,512]{3,2,0,1:T(8,128)(2,1)S(1)} %pad_maximum_fusion), channel_id=1, source_target_pairs={{0,8},{8,0},{16,24},{24,16},{32,40},{40,32},{48,56},{56,48},{64,72... | collective-permute-start | bytes 6291464 | tf_op jit(solution)/shard_map/ppermute | solution.py:86
  149.3 13.4 %collective-permute-start.32 = (bf16[384,512]{1,0:T(8,128)(2,1)}, bf16[384,512]{1,0:T(8,128)(2,1)S(1)}, u32[]{:S(2)}, u32[]{:S(2)}) collective-permute-start(bf16[384,512]{1,0:T(8,128)(2,1)} %get-tuple-element.31.g0), channel_id=1, source_target_pairs={{0,2},{1,3},{2,4},{3,5},{4,6},{5,7},{6,0},{7,1},{8,10},{9,11},{10,... | collective-permute-start | bytes 1179656 | tf_op jit(solution)/shard_map/ppermute | solution.py:90
  150.7 27.5 %collective-permute-start.15 = (bf16[640,512]{1,0:T(8,128)(2,1)}, bf16[640,512]{1,0:T(8,128)(2,1)S(1)}, u32[]{:S(2)}, u32[]{:S(2)}) collective-permute-start(bf16[640,512]{1,0:T(8,128)(2,1)} %get-tuple-element.28.g0), channel_id=1, source_target_pairs={{0,2},{1,3},{2,4},{3,5},{4,6},{5,7},{6,0},{7,1},{8,10},{9,11},{10,... | collective-permute-start | bytes 1966088 | tf_op jit(solution)/shard_map/ppermute | solution.py:90
  151.2 29.4 %collective-permute-start.14 = (bf16[640,512]{1,0:T(8,128)(2,1)}, bf16[640,512]{1,0:T(8,128)(2,1)S(1)}, u32[]{:S(2)}, u32[]{:S(2)}) collective-permute-start(bf16[640,512]{1,0:T(8,128)(2,1)} %get-tuple-element.28.g0), channel_id=1, source_target_pairs={{0,6},{1,7},{2,0},{3,1},{4,2},{5,3},{6,4},{7,5},{8,14},{9,15},{10,... | collective-permute-start | bytes 1966088 | tf_op jit(solution)/shard_map/ppermute | solution.py:90
  162.7 13.7 %collective-permute-start.31 = (bf16[384,512]{1,0:T(8,128)(2,1)}, bf16[384,512]{1,0:T(8,128)(2,1)S(1)}, u32[]{:S(2)}, u32[]{:S(2)}) collective-permute-start(bf16[384,512]{1,0:T(8,128)(2,1)} %get-tuple-element.31.g0), channel_id=1, source_target_pairs={{0,6},{1,7},{2,0},{3,1},{4,2},{5,3},{6,4},{7,5},{8,14},{9,15},{10,... | collective-permute-start | bytes 1179656 | tf_op jit(solution)/shard_map/ppermute | solution.py:90
  176.4 13.2 %collective-permute-start.33 = (bf16[192,512]{1,0:T(8,128)(2,1)S(1)}, bf16[192,512]{1,0:T(8,128)(2,1)}, u32[]{:S(2)}, u32[]{:S(2)}) collective-permute-start(bf16[192,512]{1,0:T(8,128)(2,1)S(1)} %slice.78), channel_id=1, source_target_pairs={{0,2},{1,3},{2,4},{3,5},{4,6},{5,7},{6,0},{7,1},{8,10},{9,11},{10,... | collective-permute-start | bytes 589832 | tf_op jit(solution)/shard_map/ppermute | solution.py:90
  178.2 11.4 %collective-permute-start.34 = (bf16[192,512]{1,0:T(8,128)(2,1)S(1)}, bf16[192,512]{1,0:T(8,128)(2,1)}, u32[]{:S(2)}, u32[]{:S(2)}) collective-permute-start(bf16[192,512]{1,0:T(8,128)(2,1)S(1)} %slice.79), channel_id=1, source_target_pairs={{0,6},{1,7},{2,0},{3,1},{4,2},{5,3},{6,4},{7,5},{8,14},{9,15},{10,... | collective-permute-start | bytes 589832 | tf_op jit(solution)/shard_map/ppermute | solution.py:90
  180.7 17.9 %collective-permute-start.16 = (bf16[320,512]{1,0:T(8,128)(2,1)S(1)}, bf16[320,512]{1,0:T(8,128)(2,1)}, u32[]{:S(2)}, u32[]{:S(2)}) collective-permute-start(bf16[320,512]{1,0:T(8,128)(2,1)S(1)} %slice.73), channel_id=1, source_target_pairs={{0,2},{1,3},{2,4},{3,5},{4,6},{5,7},{6,0},{7,1},{8,10},{9,11},{10,... | collective-permute-start | bytes 983048 | tf_op jit(solution)/shard_map/ppermute | solution.py:90
  181.5 17.0 %collective-permute-start.17 = (bf16[320,512]{1,0:T(8,128)(2,1)S(1)}, bf16[320,512]{1,0:T(8,128)(2,1)}, u32[]{:S(2)}, u32[]{:S(2)}) collective-permute-start(bf16[320,512]{1,0:T(8,128)(2,1)S(1)} %slice.74), channel_id=1, source_target_pairs={{0,6},{1,7},{2,0},{3,1},{4,2},{5,3},{6,4},{7,5},{8,14},{9,15},{10,... | collective-permute-start | bytes 983048 | tf_op jit(solution)/shard_map/ppermute | solution.py:90
  195.4 17.2 %collective-permute-start.35 = (bf16[384,512]{1,0:T(8,128)(2,1)}, bf16[384,512]{1,0:T(8,128)(2,1)S(1)}, u32[]{:S(2)}, u32[]{:S(2)}) collective-permute-start(bf16[384,512]{1,0:T(8,128)(2,1)} %get-tuple-element.33), channel_id=1, source_target_pairs={{0,1},{1,0},{2,3},{3,2},{4,5},{5,4},{6,7},{7,6},{8,9},{9,8},{10,11... | collective-permute-start | bytes 1179656 | tf_op jit(solution)/shard_map/ppermute | solution.py:94
  206.1 15.8 %collective-permute-start.30 = (bf16[640,512]{1,0:T(8,128)(2,1)}, bf16[640,512]{1,0:T(8,128)(2,1)S(1)}, u32[]{:S(2)}, u32[]{:S(2)}) collective-permute-start(bf16[640,512]{1,0:T(8,128)(2,1)} %get-tuple-element.30), channel_id=1, source_target_pairs={{0,1},{1,0},{2,3},{3,2},{4,5},{5,4},{6,7},{7,6},{8,9},{9,8},{10,11... | collective-permute-start | bytes 1966088 | tf_op jit(solution)/shard_map/ppermute | solution.py:94
  (22 other events, 172.5 us)
where the time goes:
time: 224 us; the launch traced here: 223 us
  waiting for transfers between devices  74.7 us (33%)
  Pallas kernels  58.7 us (26%)
  starting transfers between devices  55.4 us (25%)
  local copies, waits for them, and re-layouts  19.2 us (9%)
  other arithmetic  13.9 us (6%)
    pallas_call x4, Pallas kernels, matmul_part(): pl.pallas_call(lambda *refs: matmul_kernel(steps, extra, tail, *refs), ou...  32 us
    ppermute x12, waiting for transfers between devices, send_x(): return lax.ppermute(a, 'fsdp', fsdp_perm(dx=dx))  27.1 us
    ppermute x14, waiting for transfers between devices, send_y(): return lax.ppermute(a, 'tensor', tensor_perm(dy=dy))  26.3 us
    ppermute x14, starting transfers between devices, send_y(): return lax.ppermute(a, 'tensor', tensor_perm(dy=dy))  21.6 us
    ppermute x12, starting transfers between devices, send_x(): return lax.ppermute(a, 'fsdp', fsdp_perm(dx=dx))  17.7 us
    pallas_call x2, Pallas kernels, project(): pl.pallas_call(project_kernel, out_shape=[jax.ShapeDtypeStruct((size, 512...  13.3 us
    all_to_all x1, waiting for transfers between devices, on_device(): swapped = lax.all_to_all(packed, 'tensor', 0, 0, tiled=True)  12.2 us
    ppermute x2, waiting for transfers between devices, send_zhi(): return lax.ppermute(a, 'tensor', tensor_perm(dz=1))  9.16 us
  transfers between devices with their start and end apart: 38, of which 14 were waited for; matrix products, arithmetic and copies ran while one was open for 10% of the time, Pallas kernels for 26%

commit v1 on v0

v1 whole, which is shorter than its diff:
```python
import jax
import jax.numpy as jnp
from jax import lax
from jax.experimental import pallas as pl
from jax.experimental.pallas import tpu as pltpu
from jax.sharding import PartitionSpec as P


BF = jnp.bfloat16
F32 = jnp.float32


def fsdp_perm(dx=0, dz=0, dc=0):
    out = []
    for f in range(16):
        x, z, c = f // 4, (f // 2) % 2, f % 2
        out.append((f, (((x + dx) % 4) * 2 + (z ^ dz)) * 2 + (c ^ dc)))
    return out


def tensor_perm(dy=0, dz=0):
    return [(t, ((t // 2 + dy) % 4) * 2 + ((t % 2) ^ dz)) for t in range(8)]


CH = 128
BIG = pltpu.CompilerParams(vmem_limit_bytes=60 << 20)


def scan_kernel(bi_ref, g_ref, rate_ref, out_ref, gates_ref):
    rate = rate_ref[...]
    low = lax.broadcasted_iota(jnp.int32, (CH // 8, 8, 256), 1) < 4
    w_r = g_ref[:, :16].reshape(256, 256)
    w_i = g_ref[:, 16:].reshape(256, 256)
    gates_ref[0, 0] = w_r.T
    gates_ref[1, 0] = w_i.T

    def chunk(n, carry):
        rows = pl.ds(pl.multiple_of(n * CH, CH), CH)
        bi = bi_ref[rows, :]
        pre_r = jnp.dot(bi, g_ref[:, :16].reshape(256, 256), preferred_element_type=F32)
        pre_i = jnp.dot(bi, g_ref[:, 16:].reshape(256, 256), preferred_element_type=F32)
        a = jnp.exp(rate * jax.nn.sigmoid(pre_r))
        d = jnp.sqrt(1.0 - a * a) * (jax.nn.sigmoid(pre_i) * bi.astype(F32))
        a = a.reshape(CH // 8, 8, 256)
        d = d.reshape(CH // 8, 8, 256)
        a_prev = jnp.where(low, 1.0, pltpu.roll(a, 4, 1))
        d_prev = jnp.where(low, 0.0, pltpu.roll(d, 4, 1))
        d = a * d_prev + d
        a = a * a_prev
        a_end = jnp.where(low, pltpu.roll(a, 4, 1), a)
        d_end = jnp.where(low, pltpu.roll(d, 4, 1), d)
        states = []
        for k in range(CH // 8):
            states.append(a[k] * carry + d[k])
            carry = a_end[k] * carry + d_end[k]
        out_ref[rows, :] = jnp.concatenate(states, axis=0)
        return carry

    lax.fori_loop(0, 1024 // CH, chunk, jnp.zeros((8, 256), F32))


def gate_scan(branch_in, gates, rate):
    return pl.pallas_call(
        scan_kernel,
        out_shape=[
            jax.ShapeDtypeStruct((1024, 512), F32),
            jax.ShapeDtypeStruct((2, 2, 256, 256), BF),
        ],
        grid=(2,),
        in_specs=[
            pl.BlockSpec((1024, 256), lambda j: (0, j)),
            pl.BlockSpec((16, 32, 256), lambda j: (0, 0, j)),
            pl.BlockSpec((1, 256), lambda j: (0, j)),
        ],
        out_specs=[
            pl.BlockSpec((1024, 256), lambda j: (0, j)),
            pl.BlockSpec((2, 1, 256, 256), lambda j: (0, j, 0, 0)),
        ],
        compiler_params=BIG,
        cost_estimate=pl.CostEstimate(
            flops=8_000_000_000, bytes_accessed=4 << 20, transcendentals=4 << 20
        ),
        name="gate_scan",
    )(branch_in, gates, rate)


def send_x(a, dx):
    return lax.ppermute(a, "fsdp", fsdp_perm(dx=dx))


def send_z(a):
    return lax.ppermute(a, "fsdp", fsdp_perm(dz=1))


def send_core(a):
    return lax.ppermute(a, "fsdp", fsdp_perm(dc=1))


def send_y(a, dy):
    return lax.ppermute(a, "tensor", tensor_perm(dy=dy))


def send_zhi(a):
    return lax.ppermute(a, "tensor", tensor_perm(dz=1))


CHUNKS = (448, 576)


def position():
    f = lax.axis_index("fsdp")
    t = lax.axis_index("tensor")
    return f // 4, (f // 2) % 2, f % 2, t // 2, t % 2


def slot_meta(dx):
    x, z, core, _, _ = position()
    at = (x + jnp.array(dx, jnp.int32) + 4) & 3
    return jnp.concatenate([at, core[None], z[None]]).astype(jnp.int32)


def put(w_ref, core, z, owns, peers):
    for j in range(2):
        at = jnp.bitwise_xor(z, j)
        w_ref[at, core] = owns[j]
        w_ref[at, 1 - core] = peers[j]


def place_kernel(meta, own0, own1, peer0, peer1, w_ref):
    core, z = meta[4], meta[5]
    put(w_ref, core, z, (own0[0], own1[0]), (peer0[0], peer1[0]))


def place(meta, owns, peers):
    src = pl.BlockSpec((1, 256, 512), lambda s, m: (s, 0, 0))
    w = pl.pallas_call(
        place_kernel,
        out_shape=jax.ShapeDtypeStruct((8, 2, 256, 512), BF),
        grid_spec=pltpu.PrefetchScalarGridSpec(
            num_scalar_prefetch=1,
            grid=(4,),
            in_specs=[src] * 4,
            out_specs=pl.BlockSpec((2, 2, 256, 512), lambda s, m: (m[s], 0, 0, 0)),
        ),
        compiler_params=BIG,
        cost_estimate=pl.CostEstimate(flops=4_000_000, bytes_accessed=8 << 20, transcendentals=0),
        name="place",
    )(meta, *owns, *peers)
    return w.reshape(4096, 512)


def matmul_kernel(extra, meta, tok_ref, near_ref, near_peer_ref, far_ref, far_peer_ref, *refs):
    if extra:
        w_ref, g_ref, out_ref, acc_ref = refs
    else:
        state_ref, w_ref, *out_refs, acc_ref = refs
    core, z = meta[4], meta[5]
    step = pl.program_id(0)

    def put_all(own_ref, peer_ref):
        put(w_ref, core, z, (own_ref[0, :256], own_ref[1, :256]), (peer_ref[0, :256], peer_ref[1, :256]))
        if extra:
            put(g_ref, core, z, (own_ref[0, 256:], own_ref[1, 256:]), (peer_ref[0, 256:], peer_ref[1, 256:]))

    @pl.when(step < 3)
    def _():
        put_all(near_ref, near_peer_ref)

    @pl.when(step == 3)
    def _():
        put_all(far_ref, far_peer_ref)

    w = w_ref[...].reshape(1024, 512)

    @pl.when(step == 0)
    def _():
        acc_ref[...] = jnp.dot(tok_ref[...], w, preferred_element_type=F32)

    @pl.when(step > 0)
    def _():
        acc_ref[...] += jnp.dot(tok_ref[...], w, preferred_element_type=F32)

    @pl.when(step == 3)
    def _():
        if extra:
            out_ref[...] = acc_ref[...].astype(BF)
        else:
            base = 0
            for size, part_ref in zip(CHUNKS, out_refs):

                def rows_step(n, _, base=base, part_ref=part_ref):
                    rows = pl.ds(pl.multiple_of(base + n * 32, 32), 32)
                    value = state_ref[rows, :] * jax.nn.gelu(acc_ref[rows, :], approximate=True)
                    part_ref[pl.ds(pl.multiple_of(n * 32, 32), 32), :] = value.astype(BF)
                    return 0

                lax.fori_loop(0, size // 32, rows_step, 0)
                base += size


def whole(shape):
    return pl.BlockSpec(shape, lambda s, m: (0,) * len(shape))


def matmul(meta, tokens, parts, extra, states=None):
    rows = 256 + extra
    near = pl.BlockSpec((2, rows, 512), lambda s, m: (jnp.minimum(s, 2), 0, 0))
    operands = [tokens, *parts]
    in_specs = [pl.BlockSpec((1024, 1024), lambda s, m: (0, m[s])), near, near]
    in_specs += [whole((2, rows, 512))] * 2
    out_shape = [jax.ShapeDtypeStruct((8, 2, 256, 512), BF)]
    out_specs = [pl.BlockSpec((2, 2, 256, 512), lambda s, m: (m[s], 0, 0, 0))]
    if extra:
        out_shape += [jax.ShapeDtypeStruct((8, 2, extra, 512), BF), jax.ShapeDtypeStruct((1024, 512), BF)]
        out_specs += [pl.BlockSpec((2, 2, extra, 512), lambda s, m: (m[s], 0, 0, 0)), whole((1024, 512))]
    else:
        operands.append(states)
        in_specs.append(whole((1024, 512)))
        out_shape += [jax.ShapeDtypeStruct((size, 512), BF) for size in CHUNKS]
        out_specs += [whole((size, 512)) for size in CHUNKS]
    return pl.pallas_call(
        lambda *refs: matmul_kernel(extra, *refs),
        out_shape=out_shape,
        grid_spec=pltpu.PrefetchScalarGridSpec(
            num_scalar_prefetch=1,
            grid=(4,),
            in_specs=in_specs,
            out_specs=out_specs,
            scratch_shapes=[pltpu.VMEM((1024, 512), F32)],
        ),
        compiler_params=BIG,
        cost_estimate=pl.CostEstimate(
            flops=4_300_000_000, bytes_accessed=18 << 20, transcendentals=0
        ),
        name="matmul",
    )(meta, *operands)


def project_kernel(meta, g0, g1, g3, fa, fb, own_ref, peer_ref, give_ref, keep_ref, far_ref):
    core = meta[1]
    half = fa.shape[0]
    dims = (((1,), (1,)), ((), ()))
    step = pl.program_id(0)

    @pl.when(step == 0)
    def _():
        far_ref[:half] = fa[...]
        far_ref[half:] = fb[...]

    def side(out_ref):
        for w_ref, at in ((own_ref, core), (peer_ref, 1 - core)):
            cols = pl.ds(pl.multiple_of(at * 256, 256), 256)
            acc = lax.dot_general(g0[...], w_ref[0, 0], dims, preferred_element_type=F32)
            acc += lax.dot_general(g1[...], w_ref[0, 1], dims, preferred_element_type=F32)
            acc += lax.dot_general(far_ref[...], w_ref[0, 2], dims, preferred_element_type=F32)
            acc += lax.dot_general(g3[...], w_ref[0, 3], dims, preferred_element_type=F32)
            out_ref[:, cols] = acc.astype(out_ref.dtype)

    @pl.when(step == 0)
    def _():
        side(give_ref)

    @pl.when(step == 1)
    def _():
        side(keep_ref)


def project(meta, gs, w_own, w_peer):
    size = gs[0].shape[0]
    wspec = pl.BlockSpec((1, 4, 256, 512), lambda s, m: (jnp.bitwise_xor(m[0], s), 0, 0, 0))
    return pl.pallas_call(
        project_kernel,
        out_shape=[
            jax.ShapeDtypeStruct((size, 512), BF),
            jax.ShapeDtypeStruct((size, 512), F32),
        ],
        grid_spec=pltpu.PrefetchScalarGridSpec(
            num_scalar_prefetch=1,
            grid=(2,),
            in_specs=[whole(g.shape) for g in gs] + [wspec, wspec],
            out_specs=[whole((size, 512))] * 2,
            scratch_shapes=[pltpu.VMEM((size, 512), BF)],
        ),
        compiler_params=BIG,
        cost_estimate=pl.CostEstimate(
            flops=size * 2048 * 2048, bytes_accessed=8 << 20, transcendentals=0
        ),
        name="project",
    )(meta, *gs, w_own, w_peer)


def gather_z_first(q):
    other = send_z(q)
    pair = jnp.stack([q, other])
    left = send_x(pair, 1)
    right = send_x(pair, -1)
    far_own = send_x(left[0], 1)
    far_other = send_x(right[1], -1)
    near = jnp.concatenate([pair, left, right])
    far = jnp.stack([far_own, far_other])
    return near, send_core(near), far, send_core(far)


def on_device(
    tokens, input_source, branch_source, output_source, gates_source, decay_param, block_order
):
    x, z, core, y, zh = position()
    own_blocks = lax.dynamic_slice_in_dim(block_order, (y * 2 + zh) * 2, 2)

    def section(w):
        picked = jnp.take(w.astype(BF), block_order, axis=1)
        return jnp.transpose(picked, (1, 0, 2)).reshape(8, 64, 256)

    gates_picked = jnp.take(gates_source.astype(BF), block_order, axis=1)
    gates_flat = jnp.transpose(gates_picked.reshape(2, 8, 2, 16, 32), (1, 0, 2, 3, 4)).reshape(8, 8, 256)
    packed = jnp.concatenate(
        [section(input_source), section(branch_source), section(output_source), gates_flat], axis=1
    )
    swapped = lax.all_to_all(packed, "tensor", 0, 0, tiled=True)

    def piece(n):
        part = swapped[:, n * 64 : (n + 1) * 64].reshape(8, 2, 32, 256)
        return jnp.transpose(part, (3, 1, 0, 2)).reshape(256, 512)

    gate_part = swapped[:, 192:200].reshape(8, 2, 2, 16, 32)
    gate_rows = jnp.transpose(gate_part, (1, 3, 2, 0, 4)).reshape(32, 512)

    pair_meta = slot_meta((0, -1, 1, 2))
    row_meta = slot_meta((0, 1, 2, 3))

    q = piece(2)
    left = send_x(q, 1)
    right = send_x(q, -1)
    far_top = send_x(left[:128], 1)
    far_low = send_x(right[128:], -1)
    row = jnp.stack([q, right, jnp.concatenate([far_top, far_low]), left])
    other_row = send_z(row)

    def along_y(row):
        got = [lax.dynamic_index_in_dim(row, (y - x) & 3, 0, keepdims=False)]
        for r in (1, 2, 3):
            block = lax.dynamic_index_in_dim(row, (y - r - x) & 3, 0, keepdims=False)
            got.append(send_y(block, -r))
        return jnp.stack(got)

    w_own = jnp.stack([along_y(row), along_y(other_row)])
    w_peer = send_core(w_own)
    out_peers = (send_core(row), send_core(other_row))

    in_parts = gather_z_first(jnp.concatenate([piece(0), gate_rows]))
    br_parts = gather_z_first(piece(1))

    w, g, branch_in = matmul(pair_meta, tokens, in_parts, 32)
    input_serve = w.reshape(4096, 512)
    rate = -8.0 * jax.nn.softplus(jnp.take(decay_param, own_blocks, axis=0)).reshape(1, 512)
    states, gates_serve = gate_scan(branch_in, g.reshape(16, 32, 512), rate)
    w, *gated = matmul(pair_meta, tokens, br_parts, 0, states)
    branch_serve = w.reshape(4096, 512)
    output_serve = place(row_meta, (row, other_row), out_peers)

    give_meta = jnp.stack([(1 - zh) ^ z, core]).astype(jnp.int32)
    parts = []
    for g in gated:
        half = g.shape[0] // 2
        below = send_y(g, 1)
        above = send_y(g, -1)
        far_a = send_y(below[:half], 1)
        far_b = send_y(above[half:], -1)
        terms = (g, above, below, far_a, far_b)
        give, keep = project(give_meta, terms, w_own, w_peer)
        got = send_zhi(give)
        parts.append((keep + got.astype(F32)).astype(BF))
    mixed = jnp.concatenate(parts)
    return (mixed, input_serve, branch_serve, output_serve, gates_serve)


def solution(mesh):
    return jax.shard_map(
        on_device,
        mesh=mesh,
        in_specs=(
            P("fsdp", None),
            P("tensor", None, "fsdp"),
            P("tensor", None, "fsdp"),
            P("tensor", None, "fsdp"),
            P(None, None, "fsdp", "tensor"),
            P(),
            P(),
        ),
        out_specs=(
            P("fsdp", "tensor"),
            P(None, "tensor"),
            P(None, "tensor"),
            P(None, "tensor"),
            P(None, "tensor", None, None),
        ),
        check_vma=False,
    )
```

time: 224 us -> 210 us (0.938)
  Pallas kernels: 58.7 us -> 50 us
  local copies, waits for them, and re-layouts: 19.2 us -> 13.8 us
  starting transfers between devices: 55.4 us -> 51.3 us
  other arithmetic: 13.9 us -> 17.3 us
    ppermute x14, waiting for transfers between devices: 26.3 us -> 37.4 us  [send_y(): return lax.ppermute(a, 'tensor', tensor_perm(dy=dy))]
    ppermute x12, waiting for transfers between devices: 27.1 us -> 18.3 us  [send_x(): return lax.ppermute(a, 'fsdp', fsdp_perm(dx=dx))]
    pallas_call x5 -> x3, Pallas kernels: 39.9 us -> 31.4 us  [the longest x2 23.9 us: matmul(): pl.pallas_call(lambda *refs: matmul_kernel(extra, *refs), out_shape=out_s...]
    another operation x3 -> x0, local copies, waits for them, and re-layouts: 3.59 us -> none  [the longest x2 2.04 us: on_device(): gate_all.reshape(16, 2, 2, 16, 256)]
    ppermute x2, waiting for transfers between devices: 9.16 us -> 5.96 us  [send_zhi(): return lax.ppermute(a, 'tensor', tensor_perm(dz=1))]
    ppermute x1 -> x0, local copies, waits for them, and re-layouts: 3.11 us -> none  [send_core(): return lax.ppermute(a, 'fsdp', fsdp_perm(dc=1))]
    ppermute x14, starting transfers between devices: 21.6 us -> 18.8 us  [send_y(): return lax.ppermute(a, 'tensor', tensor_perm(dy=dy))]
    unnamed x36 -> x54, local copies, waits for them, and re-layouts: 3.91 us -> 5.97 us
  transfers between devices with their start and end apart: 38 -> 39, of which waited for: 14 -> 18; matrix products, arithmetic and copies ran while one was open for 10% -> 8% of each run, Pallas kernels for 26% -> 24%
where the time goes in v1:
time: 210 us; the launch traced here: 209 us
  waiting for transfers between devices  75.8 us (36%)
  starting transfers between devices  51.3 us (24%)
  Pallas kernels  50 us (24%)
  other arithmetic  17.3 us (8%)
  local copies, waits for them, and re-layouts  13.8 us (7%)
    ppermute x14, waiting for transfers between devices, send_y(): return lax.ppermute(a, 'tensor', tensor_perm(dy=dy))  37.4 us
    pallas_call x2, Pallas kernels, matmul(): pl.pallas_call(lambda *refs: matmul_kernel(extra, *refs), out_shape=out_s...  23.9 us
    ppermute x14, starting transfers between devices, send_y(): return lax.ppermute(a, 'tensor', tensor_perm(dy=dy))  18.8 us
    ppermute x12, waiting for transfers between devices, send_x(): return lax.ppermute(a, 'fsdp', fsdp_perm(dx=dx))  18.3 us
    ppermute x12, starting transfers between devices, send_x(): return lax.ppermute(a, 'fsdp', fsdp_perm(dx=dx))  16.9 us
    pallas_call x2, Pallas kernels, project(): pl.pallas_call(project_kernel, out_shape=[jax.ShapeDtypeStruct((size, 512...  13.3 us
    all_to_all x1, waiting for transfers between devices, on_device(): swapped = lax.all_to_all(packed, 'tensor', 0, 0, tiled=True)  12.8 us
    all_to_all x1, starting transfers between devices, on_device(): swapped = lax.all_to_all(packed, 'tensor', 0, 0, tiled=True)  7.89 us
  transfers between devices with their start and end apart: 39, of which 18 were waited for; matrix products, arithmetic and copies ran while one was open for 8% of the time, Pallas kernels for 24%

profile of v1, /device:TPU:0, one launch (start us, length us, event | category | flops | bytes accessed | tf_op | source)
XLA Modules:
  0.0 209.5 jit_solution(13304202783043375181)
XLA Ops:
  8.7 7.9 %all-to-all-start = ((bf16[8,200,256]{2,1,0:T(8,128)(2,1)}), bf16[8,200,256]{2,1,0:T(8,128)(2,1)S(1)}, u32[]{:S(2)}, u32[]{:S(2)}) async-start(bf16[8,200,256]{2,1,0:T(8,128)(2,1)} %pad_maximum_fusion.5), calls=%async_computation | async-start | bytes 1638400 | tf_op jit(solution)/shard_map/all_to_all | solution.py:319
  17.4 12.8 %all-to-all-done = bf16[8,200,256]{2,1,0:T(8,128)(2,1)S(1)} async-done(((bf16[8,200,256]{2,1,0:T(8,128)(2,1)}), bf16[8,200,256]{2,1,0:T(8,128)(2,1)S(1)}, u32[]{:S(2)}, u32[]{:S(2)}) %all-to-all-start) | async-done | bytes 819232 | tf_op jit(solution)/shard_map/all_to_all | solution.py:319
  30.5 1.6 collective-permute-start.19
  32.0 1.7 collective-permute-start.18
  39.4 3.0 %collective-permute-start.21 = (bf16[128,512]{1,0:T(8,128)(2,1)S(1)}, bf16[128,512]{1,0:T(8,128)(2,1)}, u32[]{:S(2)}, u32[]{:S(2)}) collective-permute-start(bf16[128,512]{1,0:T(8,128)(2,1)S(1)} %slice.77), channel_id=1, source_target_pairs={{0,96},{8,104},{16,112},{24,120},{32,0},{40,8},{48,16},{56,24},{64... | collective-permute-start | bytes 393224 | tf_op jit(solution)/shard_map/ppermute | solution.py:88
  45.2 2.0 collective-permute-start.9
  48.2 3.2 %collective-permute-start.2 = (bf16[2,256,512]{2,1,0:T(8,128)(2,1)S(1)}, bf16[2,256,512]{2,1,0:T(8,128)(2,1)S(1)}, u32[]{:S(2)}, u32[]{:S(2)}) collective-permute-start(bf16[2,256,512]{2,1,0:T(8,128)(2,1)S(1)} %pad_maximum_fusion.8), channel_id=1, source_target_pairs={{0,96},{8,104},{16,112},{24,120},{32,0},{40,8},{48,16},{56,24},{64... | collective-permute-start | bytes 1572872 | tf_op jit(solution)/shard_map/ppermute | solution.py:88
  54.7 7.0 %collective-permute-done.9 = bf16[2,288,512]{2,1,0:T(8,128)(2,1)} collective-permute-done((bf16[2,288,512]{2,1,0:T(8,128)(2,1)}, bf16[2,288,512]{2,1,0:T(8,128)(2,1)}, u32[]{:S(2)}, u32[]{:S(2)}) %collective-permute-start.9) | collective-permute-done | bytes 589856 | tf_op jit(solution)/shard_map/ppermute | solution.py:88
  61.8 3.0 %collective-permute-done.8 = bf16[2,288,512]{2,1,0:T(8,128)(2,1)S(1)} collective-permute-done((bf16[2,288,512]{2,1,0:T(8,128)(2,1)}, bf16[2,288,512]{2,1,0:T(8,128)(2,1)S(1)}, u32[]{:S(2)}, u32[]{:S(2)}) %collective-permute-start.8) | collective-permute-done | bytes 589856 | tf_op jit(solution)/shard_map/ppermute | solution.py:88
  67.4 2.0 collective-permute-done.24
  69.3 3.2 %collective-permute-start.12 = (bf16[288,512]{1,0:T(8,128)(2,1)S(1)}, bf16[288,512]{1,0:T(8,128)(2,1)S(1)}, u32[]{:S(2)}, u32[]{:S(2)}) collective-permute-start(bf16[288,512]{1,0:T(8,128)(2,1)S(1)} %slice_bitcast_fusion), channel_id=1, source_target_pairs={{0,96},{8,104},{16,112},{24,120},{32,0},{40,8},{48,16},{56,24},{64... | collective-permute-start | bytes 884744 | tf_op jit(solution)/shard_map/ppermute | solution.py:88
  72.6 2.4 %collective-permute-done.1 = bf16[2,256,512]{2,1,0:T(8,128)(2,1)S(1)} collective-permute-done((bf16[2,256,512]{2,1,0:T(8,128)(2,1)S(1)}, bf16[2,256,512]{2,1,0:T(8,128)(2,1)S(1)}, u32[]{:S(2)}, u32[]{:S(2)}) %collective-permute-start.1) | collective-permute-done | bytes 524320 | tf_op jit(solution)/shard_map/ppermute | solution.py:88
  75.0 2.4 %collective-permute-start.23 = (bf16[256,512]{1,0:T(8,128)(2,1)S(1)}, bf16[256,512]{1,0:T(8,128)(2,1)S(1)}, u32[]{:S(2)}, u32[]{:S(2)}) collective-permute-start(bf16[256,512]{1,0:T(8,128)(2,1)S(1)} %get-tuple-element.34), channel_id=1, source_target_pairs={{0,4},{1,5},{2,6},{3,7},{4,0},{5,1},{6,2},{7,3},{8,12},{9,13},{10,... | collective-permute-start | bytes 786440 | tf_op jit(solution)/shard_map/ppermute | solution.py:100
  77.7 2.8 %collective-permute-done.11 = bf16[288,512]{1,0:T(8,128)(2,1)S(1)} collective-permute-done((bf16[288,512]{1,0:T(8,128)(2,1)S(1)}, bf16[288,512]{1,0:T(8,128)(2,1)S(1)}, u32[]{:S(2)}, u32[]{:S(2)}) %collective-permute-start.11) | collective-permute-done | bytes 294944 | tf_op jit(solution)/shard_map/ppermute | solution.py:88
  83.8 1.7 collective-permute-start.28
  86.9 1.7 collective-permute-start.27
  91.6 2.7 %collective-permute-done.28 = bf16[256,512]{1,0:T(8,128)(2,1)S(1)} collective-permute-done((bf16[256,512]{1,0:T(8,128)(2,1)S(1)}, bf16[256,512]{1,0:T(8,128)(2,1)S(1)}, u32[]{:S(2)}, u32[]{:S(2)}) %collective-permute-start.28) | collective-permute-done | bytes 262176 | tf_op jit(solution)/shard_map/ppermute | solution.py:100
  94.3 4.8 %collective-permute-done.27 = bf16[256,512]{1,0:T(8,128)(2,1)S(1)} collective-permute-done((bf16[256,512]{1,0:T(8,128)(2,1)S(1)}, bf16[256,512]{1,0:T(8,128)(2,1)S(1)}, u32[]{:S(2)}, u32[]{:S(2)}) %collective-permute-start.27) | collective-permute-done | bytes 262176 | tf_op jit(solution)/shard_map/ppermute | solution.py:100
  102.1 11.2 %matmul.2 = (bf16[8,2,256,512]{3,2,1,0:T(8,128)(2,1)}, bf16[8,2,32,512]{3,2,1,0:T(8,128)(2,1)}, bf16[1024,512]{1,0:T(8,128)(2,1)}) custom-call(s32[6]{0:T(128)} %add_add_fusion.refs_0_, bf16[1024,4096]{1,0:T(8,128)(2,1)} %refs_1_.3, bf16[6,288,512]{2,1,0:T(8,128)(2,1)} %copy-done.4, bf16[6,288,512]{2,1,0:T(8,128)(2,1)} %collective-permute-done.10.refs_3_, ...), custom_call_target="tpu_custom_call" | custom-call | flops 4300000256 | bytes 18874368 | tf_op jit(solution)/shard_map/matmul/pallas_call | solution.py:221
  113.3 7.5 %gate_scan.1 = (f32[1024,512]{1,0:T(8,128)}, bf16[2,2,256,256]{3,2,1,0:T(8,128)(2,1)}) custom-call(bf16[1024,512]{1,0:T(8,128)(2,1)} %get-tuple-element.18.bi_ref, bf16[16,32,512]{2,1,0:T(8,128)(2,1)} %bitcast.122, f32[1,512]{1,0:T(1,128)} %fusion.1.rate_ref), custom_call_target="tpu_custom_call" | custom-call | flops 8000000000 | bytes 4194304 | tf_op jit(solution)/shard_map/gate_scan/pallas_call | solution.py:63
  121.6 12.6 %matmul.3 = (bf16[8,2,256,512]{3,2,1,0:T(8,128)(2,1)}, bf16[448,512]{1,0:T(8,128)(2,1)}, bf16[576,512]{1,0:T(8,128)(2,1)}) custom-call(s32[6]{0:T(128)} %add_add_fusion.refs_0_, bf16[1024,4096]{1,0:T(8,128)(2,1)} %refs_1_.3, bf16[6,256,512]{2,1,0:T(8,128)(2,1)} %pad_maximum_fusion.2.refs_2_, bf16[6,256,512]{2,1,0:T(8,128)(2,1)} %collective-permute-done.3.refs_3_, ...), custom_call_target="tpu_custom_call" | custom-call | flops 4300000256 | bytes 18874368 | tf_op jit(solution)/shard_map/matmul/pallas_call | solution.py:221
  134.2 2.3 %collective-permute-start.31 = (bf16[576,512]{1,0:T(8,128)(2,1)}, bf16[576,512]{1,0:T(8,128)(2,1)S(1)}, u32[]{:S(2)}, u32[]{:S(2)}) collective-permute-start(bf16[576,512]{1,0:T(8,128)(2,1)} %get-tuple-element.24.g0), channel_id=1, source_target_pairs={{0,6},{1,7},{2,0},{3,1},{4,2},{5,3},{6,4},{7,5},{8,14},{9,15},{10,... | collective-permute-start | bytes 1769480 | tf_op jit(solution)/shard_map/ppermute | solution.py:100
  137.7 2.2 %collective-permute-start.14 = (bf16[448,512]{1,0:T(8,128)(2,1)}, bf16[448,512]{1,0:T(8,128)(2,1)S(1)}, u32[]{:S(2)}, u32[]{:S(2)}) collective-permute-start(bf16[448,512]{1,0:T(8,128)(2,1)} %get-tuple-element.21.g0), channel_id=1, source_target_pairs={{0,6},{1,7},{2,0},{3,1},{4,2},{5,3},{6,4},{7,5},{8,14},{9,15},{10,... | collective-permute-start | bytes 1376264 | tf_op jit(solution)/shard_map/ppermute | solution.py:100
  139.9 23.5 %collective-permute-done.15.g3 = bf16[448,512]{1,0:T(8,128)(2,1)S(1)} collective-permute-done((bf16[448,512]{1,0:T(8,128)(2,1)}, bf16[448,512]{1,0:T(8,128)(2,1)S(1)}, u32[]{:S(2)}, u32[]{:S(2)}) %collective-permute-start.15) | collective-permute-done | bytes 458784 | tf_op jit(solution)/shard_map/ppermute | solution.py:100
  163.5 3.3 %collective-permute-start.17 = (bf16[224,512]{1,0:T(8,128)(2,1)S(1)}, bf16[224,512]{1,0:T(8,128)(2,1)S(1)}, u32[]{:S(2)}, u32[]{:S(2)}) collective-permute-start(bf16[224,512]{1,0:T(8,128)(2,1)S(1)} %slice.74), channel_id=1, source_target_pairs={{0,6},{1,7},{2,0},{3,1},{4,2},{5,3},{6,4},{7,5},{8,14},{9,15},{10,... | collective-permute-start | bytes 688136 | tf_op jit(solution)/shard_map/ppermute | solution.py:100
  168.2 3.3 %collective-permute-done.16.fa = bf16[224,512]{1,0:T(8,128)(2,1)S(1)} collective-permute-done((bf16[224,512]{1,0:T(8,128)(2,1)S(1)}, bf16[224,512]{1,0:T(8,128)(2,1)S(1)}, u32[]{:S(2)}, u32[]{:S(2)}) %collective-permute-start.16) | collective-permute-done | bytes 229408 | tf_op jit(solution)/shard_map/ppermute | solution.py:100
  172.9 2.6 %collective-permute-start.34 = (bf16[288,512]{1,0:T(8,128)(2,1)S(1)}, bf16[288,512]{1,0:T(8,128)(2,1)}, u32[]{:S(2)}, u32[]{:S(2)}) collective-permute-start(bf16[288,512]{1,0:T(8,128)(2,1)S(1)} %slice.79), channel_id=1, source_target_pairs={{0,6},{1,7},{2,0},{3,1},{4,2},{5,3},{6,4},{7,5},{8,14},{9,15},{10,... | collective-permute-start | bytes 884744 | tf_op jit(solution)/shard_map/ppermute | solution.py:100
  176.1 6.2 %project.2 = (bf16[448,512]{1,0:T(8,128)(2,1)}, f32[448,512]{1,0:T(8,128)}) custom-call(s32[2]{0:T(128)} %pad_add_fusion.meta, bf16[448,512]{1,0:T(8,128)(2,1)} %get-tuple-element.21.g0, bf16[448,512]{1,0:T(8,128)(2,1)} %copy-done.18, bf16[448,512]{1,0:T(8,128)(2,1)} %copy-done.17, bf16[224,512]{1,0:T(8,128)(2,1)} %copy-done.22, ...), custom_call_target="tpu_custom_call" | custom-call | flops 1879048192 | bytes 8388608 | tf_op jit(solution)/shard_map/project/pallas_call | solution.py:271
  182.3 2.1 %collective-permute-start.30 = (bf16[448,512]{1,0:T(8,128)(2,1)}, bf16[448,512]{1,0:T(8,128)(2,1)}, u32[]{:S(2)}, u32[]{:S(2)}) collective-permute-start(bf16[448,512]{1,0:T(8,128)(2,1)} %get-tuple-element.23), channel_id=1, source_target_pairs={{0,1},{1,0},{2,3},{3,2},{4,5},{5,4},{6,7},{7,6},{8,9},{9,8},{10,11... | collective-permute-start | bytes 1376264 | tf_op jit(solution)/shard_map/ppermute | solution.py:104
  184.5 7.1 %project.3 = (bf16[576,512]{1,0:T(8,128)(2,1)}, f32[576,512]{1,0:T(8,128)}) custom-call(s32[2]{0:T(128)} %pad_add_fusion.meta, bf16[576,512]{1,0:T(8,128)(2,1)} %get-tuple-element.24.g0, bf16[576,512]{1,0:T(8,128)(2,1)} %copy-done.15, bf16[576,512]{1,0:T(8,128)(2,1)} %copy-done.16, bf16[288,512]{1,0:T(8,128)(2,1)} %collective-permute-done.33.fa, ...), custom_call_target="tpu_custom_call" | custom-call | flops 2415919104 | bytes 8388608 | tf_op jit(solution)/shard_map/project/pallas_call | solution.py:271
  194.6 5.3 %place.1 = bf16[8,2,256,512]{3,2,1,0:T(8,128)(2,1)} custom-call(s32[6]{0:T(128)} %add_add_fusion.1.meta, bf16[4,256,512]{2,1,0:T(8,128)(2,1)} %copy-done.2, bf16[4,256,512]{2,1,0:T(8,128)(2,1)} %copy-done.3, bf16[4,256,512]{2,1,0:T(8,128)(2,1)} %copy-done.6, bf16[4,256,512]{2,1,0:T(8,128)(2,1)} %collective-permute-done.37.peer1), custom_call_target="tpu_custom_call" | custom-call | flops 4000000 | bytes 8388608 | tf_op jit(solution)/shard_map/place/pallas_call | solution.py:136
  201.2 6.0 %collective-permute-done.35 = bf16[576,512]{1,0:T(8,128)(2,1)} collective-permute-done((bf16[576,512]{1,0:T(8,128)(2,1)}, bf16[576,512]{1,0:T(8,128)(2,1)}, u32[]{:S(2)}, u32[]{:S(2)}) %collective-permute-start.35) | collective-permute-done | bytes 589856 | tf_op jit(solution)/shard_map/ppermute | solution.py:104
  (169 shorter events, 47.2 us)
Async XLA Ops:
  8.7 21.5 %all-to-all-start = ((bf16[8,200,256]{2,1,0:T(8,128)(2,1)}), bf16[8,200,256]{2,1,0:T(8,128)(2,1)S(1)}, u32[]{:S(2)}, u32[]{:S(2)}) async-start(bf16[8,200,256]{2,1,0:T(8,128)(2,1)} %pad_maximum_fusion.5), calls=%async_computation | async-start | bytes 1638400 | tf_op jit(solution)/shard_map/all_to_all | solution.py:319
  30.5 11.9 %collective-permute-start.19 = (bf16[256,512]{1,0:T(8,128)(2,1)S(1)}, bf16[256,512]{1,0:T(8,128)(2,1)S(1)}, u32[]{:S(2)}, u32[]{:S(2)}) collective-permute-start(bf16[256,512]{1,0:T(8,128)(2,1)S(1)} %copy.28), channel_id=1, source_target_pairs={{0,32},{8,40},{16,48},{24,56},{32,64},{40,72},{48,80},{56,88},{64,... | collective-permute-start | bytes 786440 | tf_op jit(solution)/shard_map/ppermute | solution.py:88
  34.4 10.0 %collective-permute-start.7 = (bf16[288,512]{1,0:T(8,128)(2,1)S(1)}, bf16[288,512]{1,0:T(8,128)(2,1)S(1)}, u32[]{:S(2)}, u32[]{:S(2)}) collective-permute-start(bf16[288,512]{1,0:T(8,128)(2,1)S(1)} %get-tuple-element.44), channel_id=1, source_target_pairs={{0,16},{8,24},{16,0},{24,8},{32,48},{40,56},{48,32},{56,40},{64,80... | collective-permute-start | bytes 884744 | tf_op jit(solution)/shard_map/ppermute | solution.py:92
  37.0 11.1 %collective-permute-start = (bf16[256,512]{1,0:T(8,128)(2,1)}, bf16[256,512]{1,0:T(8,128)(2,1)S(1)}, u32[]{:S(2)}, u32[]{:S(2)}) collective-permute-start(bf16[256,512]{1,0:T(8,128)(2,1)} %copy.20), channel_id=1, source_target_pairs={{0,16},{8,24},{16,0},{24,8},{32,48},{40,56},{48,32},{56,40},{64,80... | collective-permute-start | bytes 786440 | tf_op jit(solution)/shard_map/ppermute | solution.py:92
  39.4 12.0 %collective-permute-start.21 = (bf16[128,512]{1,0:T(8,128)(2,1)S(1)}, bf16[128,512]{1,0:T(8,128)(2,1)}, u32[]{:S(2)}, u32[]{:S(2)}) collective-permute-start(bf16[128,512]{1,0:T(8,128)(2,1)S(1)} %slice.77), channel_id=1, source_target_pairs={{0,96},{8,104},{16,112},{24,120},{32,0},{40,8},{48,16},{56,24},{64... | collective-permute-start | bytes 393224 | tf_op jit(solution)/shard_map/ppermute | solution.py:88
  43.1 8.4 %collective-permute-start.20 = (bf16[128,512]{1,0:T(8,128)(2,1)}, bf16[128,512]{1,0:T(8,128)(2,1)}, u32[]{:S(2)}, u32[]{:S(2)}) collective-permute-start(bf16[128,512]{1,0:T(8,128)(2,1)} %slice.76), channel_id=1, source_target_pairs={{0,32},{8,40},{16,48},{24,56},{32,64},{40,72},{48,80},{56,88},{64,... | collective-permute-start | bytes 393224 | tf_op jit(solution)/shard_map/ppermute | solution.py:88
  45.2 16.5 %collective-permute-start.9 = (bf16[2,288,512]{2,1,0:T(8,128)(2,1)}, bf16[2,288,512]{2,1,0:T(8,128)(2,1)}, u32[]{:S(2)}, u32[]{:S(2)}) collective-permute-start(bf16[2,288,512]{2,1,0:T(8,128)(2,1)} %pad_maximum_fusion.6), channel_id=1, source_target_pairs={{0,96},{8,104},{16,112},{24,120},{32,0},{40,8},{48,16},{56,24},{64... | collective-permute-start | bytes 1769480 | tf_op jit(solution)/shard_map/ppermute | solution.py:88
  47.2 17.6 %collective-permute-start.8 = (bf16[2,288,512]{2,1,0:T(8,128)(2,1)}, bf16[2,288,512]{2,1,0:T(8,128)(2,1)S(1)}, u32[]{:S(2)}, u32[]{:S(2)}) collective-permute-start(bf16[2,288,512]{2,1,0:T(8,128)(2,1)} %pad_maximum_fusion.6), channel_id=1, source_target_pairs={{0,32},{8,40},{16,48},{24,56},{32,64},{40,72},{48,80},{56,88},{64,... | collective-permute-start | bytes 1769480 | tf_op jit(solution)/shard_map/ppermute | solution.py:88
  48.2 24.3 %collective-permute-start.2 = (bf16[2,256,512]{2,1,0:T(8,128)(2,1)S(1)}, bf16[2,256,512]{2,1,0:T(8,128)(2,1)S(1)}, u32[]{:S(2)}, u32[]{:S(2)}) collective-permute-start(bf16[2,256,512]{2,1,0:T(8,128)(2,1)S(1)} %pad_maximum_fusion.8), channel_id=1, source_target_pairs={{0,96},{8,104},{16,112},{24,120},{32,0},{40,8},{48,16},{56,24},{64... | collective-permute-start | bytes 1572872 | tf_op jit(solution)/shard_map/ppermute | solution.py:88
  51.4 23.6 %collective-permute-start.1 = (bf16[2,256,512]{2,1,0:T(8,128)(2,1)S(1)}, bf16[2,256,512]{2,1,0:T(8,128)(2,1)S(1)}, u32[]{:S(2)}, u32[]{:S(2)}) collective-permute-start(bf16[2,256,512]{2,1,0:T(8,128)(2,1)S(1)} %pad_maximum_fusion.8), channel_id=1, source_target_pairs={{0,32},{8,40},{16,48},{24,56},{32,64},{40,72},{48,80},{56,88},{64,... | collective-permute-start | bytes 1572872 | tf_op jit(solution)/shard_map/ppermute | solution.py:88
  53.5 27.8 %collective-permute-start.25 = (bf16[4,256,512]{2,1,0:T(8,128)(2,1)S(1)}, bf16[4,256,512]{2,1,0:T(8,128)(2,1)S(1)}, u32[]{:S(2)}, u32[]{:S(2)}) collective-permute-start(bf16[4,256,512]{2,1,0:T(8,128)(2,1)S(1)} %pad_maximum_fusion.3.own0), channel_id=1, source_target_pairs={{0,16},{8,24},{16,0},{24,8},{32,48},{40,56},{48,32},{56,40},{64,80... | collective-permute-start | bytes 3145736 | tf_op jit(solution)/shard_map/ppermute | solution.py:92
  66.1 36.0 %collective-permute-start.10 = (bf16[6,288,512]{2,1,0:T(8,128)(2,1)S(1)}, bf16[6,288,512]{2,1,0:T(8,128)(2,1)}, u32[]{:S(2)}, u32[]{:S(2)}) collective-permute-start(bf16[6,288,512]{2,1,0:T(8,128)(2,1)S(1)} %pad_maximum_fusion.1.refs_2_), channel_id=1, source_target_pairs={{0,8},{8,0},{16,24},{24,16},{32,40},{40,32},{48,56},{56,48},{64,72... | collective-permute-start | bytes 5308424 | tf_op jit(solution)/shard_map/ppermute | solution.py:96
  69.3 8.1 %collective-permute-start.12 = (bf16[288,512]{1,0:T(8,128)(2,1)S(1)}, bf16[288,512]{1,0:T(8,128)(2,1)S(1)}, u32[]{:S(2)}, u32[]{:S(2)}) collective-permute-start(bf16[288,512]{1,0:T(8,128)(2,1)S(1)} %slice_bitcast_fusion), channel_id=1, source_target_pairs={{0,96},{8,104},{16,112},{24,120},{32,0},{40,8},{48,16},{56,24},{64... | collective-permute-start | bytes 884744 | tf_op jit(solution)/shard_map/ppermute | solution.py:88
  82.9 18.3 %collective-permute-start.13 = (bf16[2,288,512]{2,1,0:T(8,128)(2,1)S(1)}, bf16[2,288,512]{2,1,0:T(8,128)(2,1)S(1)}, u32[]{:S(2)}, u32[]{:S(2)}) collective-permute-start(bf16[2,288,512]{2,1,0:T(8,128)(2,1)S(1)} %pad_maximum_fusion.7.refs_4_), channel_id=1, source_target_pairs={{0,8},{8,0},{16,24},{24,16},{32,40},{40,32},{48,56},{56,48},{64,72... | collective-permute-start | bytes 1769480 | tf_op jit(solution)/shard_map/ppermute | solution.py:96
  83.8 10.4 %collective-permute-start.28 = (bf16[256,512]{1,0:T(8,128)(2,1)S(1)}, bf16[256,512]{1,0:T(8,128)(2,1)S(1)}, u32[]{:S(2)}, u32[]{:S(2)}) collective-permute-start(bf16[256,512]{1,0:T(8,128)(2,1)S(1)} %get-tuple-element.37), channel_id=1, source_target_pairs={{0,2},{1,3},{2,4},{3,5},{4,6},{5,7},{6,0},{7,1},{8,10},{9,11},{10,... | collective-permute-start | bytes 786440 | tf_op jit(solution)/shard_map/ppermute | solution.py:100
  86.9 12.2 %collective-permute-start.27 = (bf16[256,512]{1,0:T(8,128)(2,1)S(1)}, bf16[256,512]{1,0:T(8,128)(2,1)S(1)}, u32[]{:S(2)}, u32[]{:S(2)}) collective-permute-start(bf16[256,512]{1,0:T(8,128)(2,1)S(1)} %get-tuple-element.38), channel_id=1, source_target_pairs={{0,4},{1,5},{2,6},{3,7},{4,0},{5,1},{6,2},{7,3},{8,12},{9,13},{10,... | collective-permute-start | bytes 786440 | tf_op jit(solution)/shard_map/ppermute | solution.py:100
  88.9 10.4 %collective-permute-start.26 = (bf16[256,512]{1,0:T(8,128)(2,1)S(1)}, bf16[256,512]{1,0:T(8,128)(2,1)S(1)}, u32[]{:S(2)}, u32[]{:S(2)}) collective-permute-start(bf16[256,512]{1,0:T(8,128)(2,1)S(1)} %get-tuple-element.39), channel_id=1, source_target_pairs={{0,6},{1,7},{2,0},{3,1},{4,2},{5,3},{6,4},{7,5},{8,14},{9,15},{10,... | collective-permute-start | bytes 786440 | tf_op jit(solution)/shard_map/ppermute | solution.py:100
  94.2 26.6 %collective-permute-start.3 = (bf16[6,256,512]{2,1,0:T(8,128)(2,1)}, bf16[6,256,512]{2,1,0:T(8,128)(2,1)}, u32[]{:S(2)}, u32[]{:S(2)}) collective-permute-start(bf16[6,256,512]{2,1,0:T(8,128)(2,1)} %pad_maximum_fusion.2.refs_2_), channel_id=1, source_target_pairs={{0,8},{8,0},{16,24},{24,16},{32,40},{40,32},{48,56},{56,48},{64,72... | collective-permute-start | bytes 4718600 | tf_op jit(solution)/shard_map/ppermute | solution.py:96
  99.1 21.7 %collective-permute-start.6 = (bf16[2,256,512]{2,1,0:T(8,128)(2,1)S(1)}, bf16[2,256,512]{2,1,0:T(8,128)(2,1)S(1)}, u32[]{:S(2)}, u32[]{:S(2)}) collective-permute-start(bf16[2,256,512]{2,1,0:T(8,128)(2,1)S(1)} %pad_maximum_fusion.9.refs_4_), channel_id=1, source_target_pairs={{0,8},{8,0},{16,24},{24,16},{32,40},{40,32},{48,56},{56,48},{64,72... | collective-permute-start | bytes 1572872 | tf_op jit(solution)/shard_map/ppermute | solution.py:96
  100.9 75.2 %collective-permute-start.29 = (bf16[2,4,256,512]{3,2,1,0:T(8,128)(2,1)}, bf16[2,4,256,512]{3,2,1,0:T(8,128)(2,1)}, u32[]{:S(2)}, u32[]{:S(2)}) collective-permute-start(bf16[2,4,256,512]{3,2,1,0:T(8,128)(2,1)} %pad_maximum_fusion.own_ref), channel_id=1, source_target_pairs={{0,8},{8,0},{16,24},{24,16},{32,40},{40,32},{48,56},{56,48},{64,72... | collective-permute-start | bytes 6291464 | tf_op jit(solution)/shard_map/ppermute | solution.py:96
  134.2 32.5 %collective-permute-start.31 = (bf16[576,512]{1,0:T(8,128)(2,1)}, bf16[576,512]{1,0:T(8,128)(2,1)S(1)}, u32[]{:S(2)}, u32[]{:S(2)}) collective-permute-start(bf16[576,512]{1,0:T(8,128)(2,1)} %get-tuple-element.24.g0), channel_id=1, source_target_pairs={{0,6},{1,7},{2,0},{3,1},{4,2},{5,3},{6,4},{7,5},{8,14},{9,15},{10,... | collective-permute-start | bytes 1769480 | tf_op jit(solution)/shard_map/ppermute | solution.py:100
  136.6 30.2 %collective-permute-start.32 = (bf16[576,512]{1,0:T(8,128)(2,1)}, bf16[576,512]{1,0:T(8,128)(2,1)S(1)}, u32[]{:S(2)}, u32[]{:S(2)}) collective-permute-start(bf16[576,512]{1,0:T(8,128)(2,1)} %get-tuple-element.24.g0), channel_id=1, source_target_pairs={{0,2},{1,3},{2,4},{3,5},{4,6},{5,7},{6,0},{7,1},{8,10},{9,11},{10,... | collective-permute-start | bytes 1769480 | tf_op jit(solution)/shard_map/ppermute | solution.py:100
  136.6 26.7 %collective-permute-start.15 = (bf16[448,512]{1,0:T(8,128)(2,1)}, bf16[448,512]{1,0:T(8,128)(2,1)S(1)}, u32[]{:S(2)}, u32[]{:S(2)}) collective-permute-start(bf16[448,512]{1,0:T(8,128)(2,1)} %get-tuple-element.21.g0), channel_id=1, source_target_pairs={{0,2},{1,3},{2,4},{3,5},{4,6},{5,7},{6,0},{7,1},{8,10},{9,11},{10,... | collective-permute-start | bytes 1376264 | tf_op jit(solution)/shard_map/ppermute | solution.py:100
  137.7 25.7 %collective-permute-start.14 = (bf16[448,512]{1,0:T(8,128)(2,1)}, bf16[448,512]{1,0:T(8,128)(2,1)S(1)}, u32[]{:S(2)}, u32[]{:S(2)}) collective-permute-start(bf16[448,512]{1,0:T(8,128)(2,1)} %get-tuple-element.21.g0), channel_id=1, source_target_pairs={{0,6},{1,7},{2,0},{3,1},{4,2},{5,3},{6,4},{7,5},{8,14},{9,15},{10,... | collective-permute-start | bytes 1376264 | tf_op jit(solution)/shard_map/ppermute | solution.py:100
  163.3 8.2 %collective-permute-start.16 = (bf16[224,512]{1,0:T(8,128)(2,1)S(1)}, bf16[224,512]{1,0:T(8,128)(2,1)S(1)}, u32[]{:S(2)}, u32[]{:S(2)}) collective-permute-start(bf16[224,512]{1,0:T(8,128)(2,1)S(1)} %slice.73), channel_id=1, source_target_pairs={{0,2},{1,3},{2,4},{3,5},{4,6},{5,7},{6,0},{7,1},{8,10},{9,11},{10,... | collective-permute-start | bytes 688136 | tf_op jit(solution)/shard_map/ppermute | solution.py:100
  163.5 8.0 %collective-permute-start.17 = (bf16[224,512]{1,0:T(8,128)(2,1)S(1)}, bf16[224,512]{1,0:T(8,128)(2,1)S(1)}, u32[]{:S(2)}, u32[]{:S(2)}) collective-permute-start(bf16[224,512]{1,0:T(8,128)(2,1)S(1)} %slice.74), channel_id=1, source_target_pairs={{0,6},{1,7},{2,0},{3,1},{4,2},{5,3},{6,4},{7,5},{8,14},{9,15},{10,... | collective-permute-start | bytes 688136 | tf_op jit(solution)/shard_map/ppermute | solution.py:100
  166.7 26.9 %collective-permute-start.36 = (bf16[4,256,512]{2,1,0:T(8,128)(2,1)S(1)}, bf16[4,256,512]{2,1,0:T(8,128)(2,1)S(1)}, u32[]{:S(2)}, u32[]{:S(2)}) collective-permute-start(bf16[4,256,512]{2,1,0:T(8,128)(2,1)S(1)} %pad_maximum_fusion.3.own0), channel_id=1, source_target_pairs={{0,8},{8,0},{16,24},{24,16},{32,40},{40,32},{48,56},{56,48},{64,72... | collective-permute-start | bytes 3145736 | tf_op jit(solution)/shard_map/ppermute | solution.py:96
  166.9 26.8 %collective-permute-start.37 = (bf16[4,256,512]{2,1,0:T(8,128)(2,1)S(1)}, bf16[4,256,512]{2,1,0:T(8,128)(2,1)}, u32[]{:S(2)}, u32[]{:S(2)}) collective-permute-start(bf16[4,256,512]{2,1,0:T(8,128)(2,1)S(1)} %collective-permute-done.25.own1), channel_id=1, source_target_pairs={{0,8},{8,0},{16,24},{24,16},{32,40},{40,32},{48,56},{56,48},{64,72... | collective-permute-start | bytes 3145736 | tf_op jit(solution)/shard_map/ppermute | solution.py:96
  171.5 13.0 %collective-permute-start.33 = (bf16[288,512]{1,0:T(8,128)(2,1)}, bf16[288,512]{1,0:T(8,128)(2,1)}, u32[]{:S(2)}, u32[]{:S(2)}) collective-permute-start(bf16[288,512]{1,0:T(8,128)(2,1)} %slice.78), channel_id=1, source_target_pairs={{0,2},{1,3},{2,4},{3,5},{4,6},{5,7},{6,0},{7,1},{8,10},{9,11},{10,... | collective-permute-start | bytes 884744 | tf_op jit(solution)/shard_map/ppermute | solution.py:100
  172.9 11.6 %collective-permute-start.34 = (bf16[288,512]{1,0:T(8,128)(2,1)S(1)}, bf16[288,512]{1,0:T(8,128)(2,1)}, u32[]{:S(2)}, u32[]{:S(2)}) collective-permute-start(bf16[288,512]{1,0:T(8,128)(2,1)S(1)} %slice.79), channel_id=1, source_target_pairs={{0,6},{1,7},{2,0},{3,1},{4,2},{5,3},{6,4},{7,5},{8,14},{9,15},{10,... | collective-permute-start | bytes 884744 | tf_op jit(solution)/shard_map/ppermute | solution.py:100
  182.3 17.6 %collective-permute-start.30 = (bf16[448,512]{1,0:T(8,128)(2,1)}, bf16[448,512]{1,0:T(8,128)(2,1)}, u32[]{:S(2)}, u32[]{:S(2)}) collective-permute-start(bf16[448,512]{1,0:T(8,128)(2,1)} %get-tuple-element.23), channel_id=1, source_target_pairs={{0,1},{1,0},{2,3},{3,2},{4,5},{5,4},{6,7},{7,6},{8,9},{9,8},{10,11... | collective-permute-start | bytes 1376264 | tf_op jit(solution)/shard_map/ppermute | solution.py:104
  191.5 15.6 %collective-permute-start.35 = (bf16[576,512]{1,0:T(8,128)(2,1)}, bf16[576,512]{1,0:T(8,128)(2,1)}, u32[]{:S(2)}, u32[]{:S(2)}) collective-permute-start(bf16[576,512]{1,0:T(8,128)(2,1)} %get-tuple-element.26), channel_id=1, source_target_pairs={{0,1},{1,0},{2,3},{3,2},{4,5},{5,4},{6,7},{7,6},{8,9},{9,8},{10,11... | collective-permute-start | bytes 1769480 | tf_op jit(solution)/shard_map/ppermute | solution.py:104
  (32 other events, 375.4 us)

commit v2 on v1

--- a/solution.py
+++ b/solution.py
@@ -22,7 +22,7 @@
     return [(t, ((t // 2 + dy) % 4) * 2 + ((t % 2) ^ dz)) for t in range(8)]
 
 
-CH = 128
+CH = 512
 BIG = pltpu.CompilerParams(vmem_limit_bytes=60 << 20)
 
 
@@ -104,7 +104,7 @@
     return lax.ppermute(a, "tensor", tensor_perm(dz=1))
 
 
-CHUNKS = (448, 576)
+CHUNKS = (384, 384, 256)
 
 
 def position():
@@ -236,23 +236,17 @@
     )(meta, *operands)
 
 
-def project_kernel(meta, g0, g1, g3, fa, fb, own_ref, peer_ref, give_ref, keep_ref, far_ref):
+def project_kernel(meta, g0, g1, g2, g3, own_ref, peer_ref, give_ref, keep_ref):
     core = meta[1]
-    half = fa.shape[0]
     dims = (((1,), (1,)), ((), ()))
     step = pl.program_id(0)
-
-    @pl.when(step == 0)
-    def _():
-        far_ref[:half] = fa[...]
-        far_ref[half:] = fb[...]
 
     def side(out_ref):
         for w_ref, at in ((own_ref, core), (peer_ref, 1 - core)):
             cols = pl.ds(pl.multiple_of(at * 256, 256), 256)
             acc = lax.dot_general(g0[...], w_ref[0, 0], dims, preferred_element_type=F32)
             acc += lax.dot_general(g1[...], w_ref[0, 1], dims, preferred_element_type=F32)
-            acc += lax.dot_general(far_ref[...], w_ref[0, 2], dims, preferred_element_type=F32)
+            acc += lax.dot_general(g2[...], w_ref[0, 2], dims, preferred_element_type=F32)
             acc += lax.dot_general(g3[...], w_ref[0, 3], dims, preferred_element_type=F32)
             out_ref[:, cols] = acc.astype(out_ref.dtype)
 
@@ -279,7 +273,6 @@
             grid=(2,),
             in_specs=[whole(g.shape) for g in gs] + [wspec, wspec],
             out_specs=[whole((size, 512))] * 2,
-            scratch_shapes=[pltpu.VMEM((size, 512), BF)],
         ),
         compiler_params=BIG,
         cost_estimate=pl.CostEstimate(
@@ -289,15 +282,16 @@
     )(meta, *gs, w_own, w_peer)
 
 
-def gather_z_first(q):
+def gather_z_first(name, q):
     other = send_z(q)
     pair = jnp.stack([q, other])
     left = send_x(pair, 1)
     right = send_x(pair, -1)
-    far_own = send_x(left[0], 1)
-    far_other = send_x(right[1], -1)
+    if name == "in":
+        far = jnp.stack([send_x(left[0], 1), send_x(right[1], -1)])
+    else:
+        far = send_x(pair, 2)
     near = jnp.concatenate([pair, left, right])
-    far = jnp.stack([far_own, far_other])
     return near, send_core(near), far, send_core(far)
 
 
@@ -308,10 +302,10 @@
     own_blocks = lax.dynamic_slice_in_dim(block_order, (y * 2 + zh) * 2, 2)
 
     def section(w):
-        picked = jnp.take(w.astype(BF), block_order, axis=1)
+        picked = jnp.take(w.astype(BF), block_order, axis=1, mode="clip")
         return jnp.transpose(picked, (1, 0, 2)).reshape(8, 64, 256)
 
-    gates_picked = jnp.take(gates_source.astype(BF), block_order, axis=1)
+    gates_picked = jnp.take(gates_source.astype(BF), block_order, axis=1, mode="clip")
     gates_flat = jnp.transpose(gates_picked.reshape(2, 8, 2, 16, 32), (1, 0, 2, 3, 4)).reshape(8, 8, 256)
     packed = jnp.concatenate(
         [section(input_source), section(branch_source), section(output_source), gates_flat], axis=1
@@ -347,12 +341,12 @@
     w_peer = send_core(w_own)
     out_peers = (send_core(row), send_core(other_row))
 
-    in_parts = gather_z_first(jnp.concatenate([piece(0), gate_rows]))
-    br_parts = gather_z_first(piece(1))
+    in_parts = gather_z_first("in", jnp.concatenate([piece(0), gate_rows]))
+    br_parts = gather_z_first("br", piece(1))
 
     w, g, branch_in = matmul(pair_meta, tokens, in_parts, 32)
     input_serve = w.reshape(4096, 512)
-    rate = -8.0 * jax.nn.softplus(jnp.take(decay_param, own_blocks, axis=0)).reshape(1, 512)
+    rate = -8.0 * jax.nn.softplus(jnp.take(decay_param, own_blocks, axis=0, mode="clip")).reshape(1, 512)
     states, gates_serve = gate_scan(branch_in, g.reshape(16, 32, 512), rate)
     w, *gated = matmul(pair_meta, tokens, br_parts, 0, states)
     branch_serve = w.reshape(4096, 512)
@@ -360,13 +354,16 @@
 
     give_meta = jnp.stack([(1 - zh) ^ z, core]).astype(jnp.int32)
     parts = []
-    for g in gated:
-        half = g.shape[0] // 2
+    for n, g in enumerate(gated):
         below = send_y(g, 1)
         above = send_y(g, -1)
-        far_a = send_y(below[:half], 1)
-        far_b = send_y(above[half:], -1)
-        terms = (g, above, below, far_a, far_b)
+        if n == 0:
+            far = send_y(below, 1)
+        elif n == 1:
+            far = send_y(above, -1)
+        else:
+            far = send_y(g, 2)
+        terms = (g, above, far, below)
         give, keep = project(give_meta, terms, w_own, w_peer)
         got = send_zhi(give)
         parts.append((keep + got.astype(F32)).astype(BF))

time: 210 us -> 221 us (1.052)
  blocking collectives: 0 us -> 22.6 us
  waiting for transfers between devices: 75.8 us -> 71 us
  other arithmetic: 17.3 us -> 13.1 us
    all_to_all x0 -> x1, blocking collectives: none -> 22.6 us  [on_device(): swapped = lax.all_to_all(packed, 'tensor', 0, 0, tiled=True)]
    ppermute x12 -> x11, waiting for transfers between devices: 18.3 us -> 33.6 us  [send_x(): return lax.ppermute(a, 'fsdp', fsdp_perm(dx=dx))]
    all_to_all x1 -> x0, waiting for transfers between devices: 12.8 us -> none  [on_device(): swapped = lax.all_to_all(packed, 'tensor', 0, 0, tiled=True)]
    ppermute x14 -> x15, waiting for transfers between devices: 37.4 us -> 28.1 us  [send_y(): return lax.ppermute(a, 'tensor', tensor_perm(dy=dy))]
    all_to_all x1 -> x0, starting transfers between devices: 7.89 us -> none  [on_device(): swapped = lax.all_to_all(packed, 'tensor', 0, 0, tiled=True)]
    ppermute x2 -> x3, waiting for transfers between devices: 5.96 us -> 9.34 us  [send_zhi(): return lax.ppermute(a, 'tensor', tensor_perm(dz=1))]
    pallas_call x2 -> x3, Pallas kernels: 13.3 us -> 16.5 us  [project(): pl.pallas_call(project_kernel, out_shape=[jax.ShapeDtypeStruct((size, 512...]
    ppermute x12 -> x11, starting transfers between devices: 16.9 us -> 19.9 us  [send_x(): return lax.ppermute(a, 'fsdp', fsdp_perm(dx=dx))]
  transfers between devices with their start and end apart: 39 -> 39, of which waited for: 18 -> 15; matrix products, arithmetic and copies ran while one was open for 8% -> 7% of each run, Pallas kernels for 24% -> 23%
where the time goes in v2:
time: 221 us
  waiting for transfers between devices  71 us (32%)
  Pallas kernels  51.2 us (23%)
  starting transfers between devices  50.1 us (23%)
  blocking collectives  22.6 us (10%)
  other arithmetic  13.1 us (6%)
  local copies, waits for them, and re-layouts  11.6 us (5%)
    ppermute x11, waiting for transfers between devices, send_x(): return lax.ppermute(a, 'fsdp', fsdp_perm(dx=dx))  33.6 us
    ppermute x15, waiting for transfers between devices, send_y(): return lax.ppermute(a, 'tensor', tensor_perm(dy=dy))  28.1 us
    pallas_call x2, Pallas kernels, matmul(): pl.pallas_call(lambda *refs: matmul_kernel(extra, *refs), out_shape=out_s...  23.9 us
    all_to_all x1, blocking collectives, on_device(): swapped = lax.all_to_all(packed, 'tensor', 0, 0, tiled=True)  22.6 us
    ppermute x15, starting transfers between devices, send_y(): return lax.ppermute(a, 'tensor', tensor_perm(dy=dy))  20.6 us
    ppermute x11, starting transfers between devices, send_x(): return lax.ppermute(a, 'fsdp', fsdp_perm(dx=dx))  19.9 us
    pallas_call x3, Pallas kernels, project(): pl.pallas_call(project_kernel, out_shape=[jax.ShapeDtypeStruct((size, 512...  16.5 us
    ppermute x3, waiting for transfers between devices, send_zhi(): return lax.ppermute(a, 'tensor', tensor_perm(dz=1))  9.34 us
  transfers between devices with their start and end apart: 39, of which 15 were waited for; matrix products, arithmetic and copies ran while one was open for 7% of the time, Pallas kernels for 23%

profile of v2, /device:TPU:0, one launch (start us, length us, event | category | flops | bytes accessed | tf_op | source)
XLA Modules:
  0.0 220.9 jit_solution(2592122699235647006)
XLA Ops:
  6.8 22.6 %all_to_all.5 = bf16[8,200,256]{2,1,0:T(8,128)(2,1)S(1)} all-to-all(bf16[8,200,256]{2,1,0:T(8,128)(2,1)S(1)} %pad_maximum_fusion.5), channel_id=1, replica_groups=mesh['fsdp'=16,'tensor'=8] {'tensor'}, dimensions={0} | all-to-all | bytes 1638400 | tf_op jit(solution)/shard_map/all_to_all | solution.py:313
  31.5 2.8 %collective-permute-start.16 = (bf16[256,512]{1,0:T(8,128)(2,1)S(1)}, bf16[256,512]{1,0:T(8,128)(2,1)S(1)}, u32[]{:S(2)}, u32[]{:S(2)}) collective-permute-start(bf16[256,512]{1,0:T(8,128)(2,1)S(1)} %copy.28), channel_id=1, source_target_pairs={{0,96},{8,104},{16,112},{24,120},{32,0},{40,8},{48,16},{56,24},{64... | collective-permute-start | bytes 786440 | tf_op jit(solution)/shard_map/ppermute | solution.py:88
  34.4 3.9 %collective-permute-done.16 = bf16[256,512]{1,0:T(8,128)(2,1)S(1)} collective-permute-done((bf16[256,512]{1,0:T(8,128)(2,1)S(1)}, bf16[256,512]{1,0:T(8,128)(2,1)S(1)}, u32[]{:S(2)}, u32[]{:S(2)}) %collective-permute-start.16) | collective-permute-done | bytes 262176 | tf_op jit(solution)/shard_map/ppermute | solution.py:88
  38.3 3.8 %collective-permute-start.19 = (bf16[128,512]{1,0:T(8,128)(2,1)S(1)}, bf16[128,512]{1,0:T(8,128)(2,1)}, u32[]{:S(2)}, u32[]{:S(2)}) collective-permute-start(bf16[128,512]{1,0:T(8,128)(2,1)S(1)} %slice.49), channel_id=1, source_target_pairs={{0,96},{8,104},{16,112},{24,120},{32,0},{40,8},{48,16},{56,24},{64... | collective-permute-start | bytes 393224 | tf_op jit(solution)/shard_map/ppermute | solution.py:88
  43.7 3.2 %collective-permute-start.8 = (bf16[2,288,512]{2,1,0:T(8,128)(2,1)}, bf16[2,288,512]{2,1,0:T(8,128)(2,1)S(1)}, u32[]{:S(2)}, u32[]{:S(2)}) collective-permute-start(bf16[2,288,512]{2,1,0:T(8,128)(2,1)} %pad_maximum_fusion.6), channel_id=1, source_target_pairs={{0,96},{8,104},{16,112},{24,120},{32,0},{40,8},{48,16},{56,24},{64... | collective-permute-start | bytes 1769480 | tf_op jit(solution)/shard_map/ppermute | solution.py:88
  58.7 2.8 %collective-permute-done.7 = bf16[2,288,512]{2,1,0:T(8,128)(2,1)S(1)} collective-permute-done((bf16[2,288,512]{2,1,0:T(8,128)(2,1)}, bf16[2,288,512]{2,1,0:T(8,128)(2,1)S(1)}, u32[]{:S(2)}, u32[]{:S(2)}) %collective-permute-start.7) | collective-permute-done | bytes 589856 | tf_op jit(solution)/shard_map/ppermute | solution.py:88
  64.2 2.6 %collective-permute-done.22 = bf16[256,512]{1,0:T(8,128)(2,1)S(1)} collective-permute-done((bf16[256,512]{1,0:T(8,128)(2,1)S(1)}, bf16[256,512]{1,0:T(8,128)(2,1)S(1)}, u32[]{:S(2)}, u32[]{:S(2)}) %collective-permute-start.22) | collective-permute-done | bytes 262176 | tf_op jit(solution)/shard_map/ppermute | solution.py:100
  66.9 3.4 %collective-permute-start.11 = (bf16[288,512]{1,0:T(8,128)(2,1)S(1)}, bf16[288,512]{1,0:T(8,128)(2,1)S(1)}, u32[]{:S(2)}, u32[]{:S(2)}) collective-permute-start(bf16[288,512]{1,0:T(8,128)(2,1)S(1)} %slice_bitcast_fusion), channel_id=1, source_target_pairs={{0,96},{8,104},{16,112},{24,120},{32,0},{40,8},{48,16},{56,24},{64... | collective-permute-start | bytes 884744 | tf_op jit(solution)/shard_map/ppermute | solution.py:88
  73.8 3.8 %collective-permute-done.11 = bf16[288,512]{1,0:T(8,128)(2,1)S(1)} collective-permute-done((bf16[288,512]{1,0:T(8,128)(2,1)S(1)}, bf16[288,512]{1,0:T(8,128)(2,1)S(1)}, u32[]{:S(2)}, u32[]{:S(2)}) %collective-permute-start.11) | collective-permute-done | bytes 294944 | tf_op jit(solution)/shard_map/ppermute | solution.py:88
  77.6 1.9 collective-permute-start.4
  79.6 2.7 %collective-permute-start.10 = (bf16[288,512]{1,0:T(8,128)(2,1)S(1)}, bf16[288,512]{1,0:T(8,128)(2,1)S(1)}, u32[]{:S(2)}, u32[]{:S(2)}) collective-permute-start(bf16[288,512]{1,0:T(8,128)(2,1)S(1)} %slice_bitcast_fusion.1), channel_id=1, source_target_pairs={{0,32},{8,40},{16,48},{24,56},{32,64},{40,72},{48,80},{56,88},{64,... | collective-permute-start | bytes 884744 | tf_op jit(solution)/shard_map/ppermute | solution.py:88
  84.2 20.1 %collective-permute-done.10 = bf16[288,512]{1,0:T(8,128)(2,1)S(1)} collective-permute-done((bf16[288,512]{1,0:T(8,128)(2,1)S(1)}, bf16[288,512]{1,0:T(8,128)(2,1)S(1)}, u32[]{:S(2)}, u32[]{:S(2)}) %collective-permute-start.10) | collective-permute-done | bytes 294944 | tf_op jit(solution)/shard_map/ppermute | solution.py:88
  105.2 3.1 %collective-permute-start.25 = (bf16[256,512]{1,0:T(8,128)(2,1)S(1)}, bf16[256,512]{1,0:T(8,128)(2,1)S(1)}, u32[]{:S(2)}, u32[]{:S(2)}) collective-permute-start(bf16[256,512]{1,0:T(8,128)(2,1)S(1)} %get-tuple-element.41), channel_id=1, source_target_pairs={{0,4},{1,5},{2,6},{3,7},{4,0},{5,1},{6,2},{7,3},{8,12},{9,13},{10,... | collective-permute-start | bytes 786440 | tf_op jit(solution)/shard_map/ppermute | solution.py:100
  110.1 3.3 %collective-permute-done.26 = bf16[256,512]{1,0:T(8,128)(2,1)S(1)} collective-permute-done((bf16[256,512]{1,0:T(8,128)(2,1)S(1)}, bf16[256,512]{1,0:T(8,128)(2,1)S(1)}, u32[]{:S(2)}, u32[]{:S(2)}) %collective-permute-start.26) | collective-permute-done | bytes 262176 | tf_op jit(solution)/shard_map/ppermute | solution.py:100
  114.6 4.1 %collective-permute-done.25 = bf16[256,512]{1,0:T(8,128)(2,1)S(1)} collective-permute-done((bf16[256,512]{1,0:T(8,128)(2,1)S(1)}, bf16[256,512]{1,0:T(8,128)(2,1)S(1)}, u32[]{:S(2)}, u32[]{:S(2)}) %collective-permute-start.25) | collective-permute-done | bytes 262176 | tf_op jit(solution)/shard_map/ppermute | solution.py:100
  118.7 2.3 %collective-permute-done.24 = bf16[256,512]{1,0:T(8,128)(2,1)S(1)} collective-permute-done((bf16[256,512]{1,0:T(8,128)(2,1)S(1)}, bf16[256,512]{1,0:T(8,128)(2,1)S(1)}, u32[]{:S(2)}, u32[]{:S(2)}) %collective-permute-start.24) | collective-permute-done | bytes 262176 | tf_op jit(solution)/shard_map/ppermute | solution.py:100
  122.7 11.2 %matmul.2 = (bf16[8,2,256,512]{3,2,1,0:T(8,128)(2,1)}, bf16[8,2,32,512]{3,2,1,0:T(8,128)(2,1)}, bf16[1024,512]{1,0:T(8,128)(2,1)}) custom-call(s32[6]{0:T(128)} %add_add_fusion.refs_0_, bf16[1024,4096]{1,0:T(8,128)(2,1)} %refs_1_.3, bf16[6,288,512]{2,1,0:T(8,128)(2,1)} %pad_maximum_fusion.1.refs_2_, bf16[6,288,512]{2,1,0:T(8,128)(2,1)} %collective-permute-done.9.refs_3_, ...), custom_call_target="tpu_custom_call" | custom-call | flops 4300000256 | bytes 18874368 | tf_op jit(solution)/shard_map/matmul/pallas_call | solution.py:221
  133.9 5.5 %gate_scan.1 = (f32[1024,512]{1,0:T(8,128)}, bf16[2,2,256,256]{3,2,1,0:T(8,128)(2,1)}) custom-call(bf16[1024,512]{1,0:T(8,128)(2,1)} %get-tuple-element.20.bi_ref, bf16[16,32,512]{2,1,0:T(8,128)(2,1)} %bitcast.106, f32[1,512]{1,0:T(1,128)} %fusion.rate_ref), custom_call_target="tpu_custom_call" | custom-call | flops 8000000000 | bytes 4194304 | tf_op jit(solution)/shard_map/gate_scan/pallas_call | solution.py:63
  139.4 12.6 %matmul.3 = (bf16[8,2,256,512]{3,2,1,0:T(8,128)(2,1)}, bf16[384,512]{1,0:T(8,128)(2,1)}, bf16[384,512]{1,0:T(8,128)(2,1)}, bf16[256,512]{1,0:T(8,128)(2,1)}) custom-call(s32[6]{0:T(128)} %add_add_fusion.refs_0_, bf16[1024,4096]{1,0:T(8,128)(2,1)} %refs_1_.3, bf16[6,256,512]{2,1,0:T(8,128)(2,1)} %pad_maximum_fusion.2.refs_2_, ...), custom_call_target="tpu_custom_call" | custom-call | flops 4300000256 | bytes 18874368 | tf_op jit(solution)/shard_map/matmul/pallas_call | solution.py:221
  152.1 2.6 %collective-permute-start.33 = (bf16[256,512]{1,0:T(8,128)(2,1)}, bf16[256,512]{1,0:T(8,128)(2,1)S(1)}, u32[]{:S(2)}, u32[]{:S(2)}) collective-permute-start(bf16[256,512]{1,0:T(8,128)(2,1)} %get-tuple-element.29.g0), channel_id=1, source_target_pairs={{0,6},{1,7},{2,0},{3,1},{4,2},{5,3},{6,4},{7,5},{8,14},{9,15},{10,... | collective-permute-start | bytes 786440 | tf_op jit(solution)/shard_map/ppermute | solution.py:100
  154.8 2.0 collective-permute-start.14
  157.0 4.7 %collective-permute-done.33.g1 = bf16[256,512]{1,0:T(8,128)(2,1)S(1)} collective-permute-done((bf16[256,512]{1,0:T(8,128)(2,1)}, bf16[256,512]{1,0:T(8,128)(2,1)S(1)}, u32[]{:S(2)}, u32[]{:S(2)}) %collective-permute-start.33) | collective-permute-done | bytes 262176 | tf_op jit(solution)/shard_map/ppermute | solution.py:100
  162.3 10.5 %collective-permute-done.34.g2 = bf16[256,512]{1,0:T(8,128)(2,1)S(1)} collective-permute-done((bf16[256,512]{1,0:T(8,128)(2,1)}, bf16[256,512]{1,0:T(8,128)(2,1)S(1)}, u32[]{:S(2)}, u32[]{:S(2)}) %collective-permute-start.34) | collective-permute-done | bytes 262176 | tf_op jit(solution)/shard_map/ppermute | solution.py:100
  172.8 3.5 %collective-permute-start.31 = (bf16[384,512]{1,0:T(8,128)(2,1)}, bf16[384,512]{1,0:T(8,128)(2,1)S(1)}, u32[]{:S(2)}, u32[]{:S(2)}) collective-permute-start(bf16[384,512]{1,0:T(8,128)(2,1)} %get-tuple-element.26.g0), channel_id=1, source_target_pairs={{0,2},{1,3},{2,4},{3,5},{4,6},{5,7},{6,0},{7,1},{8,10},{9,11},{10,... | collective-permute-start | bytes 1179656 | tf_op jit(solution)/shard_map/ppermute | solution.py:100
  176.3 2.2 collective-permute-start.30
  182.3 5.3 %place.1 = bf16[8,2,256,512]{3,2,1,0:T(8,128)(2,1)} custom-call(s32[6]{0:T(128)} %add_add_fusion.1.meta, bf16[4,256,512]{2,1,0:T(8,128)(2,1)} %copy-done.2, bf16[4,256,512]{2,1,0:T(8,128)(2,1)} %collective-permute-done.23.own1, bf16[4,256,512]{2,1,0:T(8,128)(2,1)} %collective-permute-done.37.peer0, bf16[4,256,512]{2,1,0:T(8,128)(2,1)} %collective-permute-done.38.peer1), custom_call_target="tpu_custom_call" | custom-call | flops 4000000 | bytes 8388608 | tf_op jit(solution)/shard_map/place/pallas_call | solution.py:136
  187.7 5.0 %project.5 = (bf16[256,512]{1,0:T(8,128)(2,1)}, f32[256,512]{1,0:T(8,128)}) custom-call(s32[2]{0:T(128)} %pad_add_fusion.meta, bf16[256,512]{1,0:T(8,128)(2,1)} %get-tuple-element.29.g0, bf16[256,512]{1,0:T(8,128)(2,1)} %copy-done.15, bf16[256,512]{1,0:T(8,128)(2,1)} %copy-done.16, bf16[256,512]{1,0:T(8,128)(2,1)} %copy-done.17, ...), custom_call_target="tpu_custom_call" | custom-call | flops 1073741824 | bytes 8388608 | tf_op jit(solution)/shard_map/project/pallas_call | solution.py:265
  195.0 5.8 %project.4 = (bf16[384,512]{1,0:T(8,128)(2,1)}, f32[384,512]{1,0:T(8,128)}) custom-call(s32[2]{0:T(128)} %pad_add_fusion.meta, bf16[384,512]{1,0:T(8,128)(2,1)} %get-tuple-element.26.g0, bf16[384,512]{1,0:T(8,128)(2,1)} %collective-permute-done.29.g1, bf16[384,512]{1,0:T(8,128)(2,1)} %collective-permute-done.30.g2, bf16[384,512]{1,0:T(8,128)(2,1)} %copy-done.21, ...), custom_call_target="tpu_custom_call" | custom-call | flops 1610612736 | bytes 8388608 | tf_op jit(solution)/shard_map/project/pallas_call | solution.py:265
  200.8 2.0 collective-permute-start.32
  202.8 5.8 %project.3 = (bf16[384,512]{1,0:T(8,128)(2,1)}, f32[384,512]{1,0:T(8,128)}) custom-call(s32[2]{0:T(128)} %pad_add_fusion.meta, bf16[384,512]{1,0:T(8,128)(2,1)} %get-tuple-element.23.g0, bf16[384,512]{1,0:T(8,128)(2,1)} %collective-permute-done.13.g1, bf16[384,512]{1,0:T(8,128)(2,1)} %collective-permute-done.15.g2, ...), custom_call_target="tpu_custom_call" | custom-call | flops 1610612736 | bytes 8388608 | tf_op jit(solution)/shard_map/project/pallas_call | solution.py:265
  210.3 2.0 collective-permute-done.32
  212.4 7.3 %collective-permute-done.28 = bf16[384,512]{1,0:T(8,128)(2,1)S(1)} collective-permute-done((bf16[384,512]{1,0:T(8,128)(2,1)}, bf16[384,512]{1,0:T(8,128)(2,1)S(1)}, u32[]{:S(2)}, u32[]{:S(2)}) %collective-permute-start.28) | collective-permute-done | bytes 393248 | tf_op jit(solution)/shard_map/ppermute | solution.py:104
  (156 shorter events, 45.0 us)
Async XLA Ops:
  30.2 12.6 %collective-permute-start.6 = (bf16[288,512]{1,0:T(8,128)(2,1)S(1)}, bf16[288,512]{1,0:T(8,128)(2,1)S(1)}, u32[]{:S(2)}, u32[]{:S(2)}) collective-permute-start(bf16[288,512]{1,0:T(8,128)(2,1)S(1)} %get-tuple-element.47), channel_id=1, source_target_pairs={{0,16},{8,24},{16,0},{24,8},{32,48},{40,56},{48,32},{56,40},{64,80... | collective-permute-start | bytes 884744 | tf_op jit(solution)/shard_map/ppermute | solution.py:92
  38.3 11.3 %collective-permute-start.19 = (bf16[128,512]{1,0:T(8,128)(2,1)S(1)}, bf16[128,512]{1,0:T(8,128)(2,1)}, u32[]{:S(2)}, u32[]{:S(2)}) collective-permute-start(bf16[128,512]{1,0:T(8,128)(2,1)S(1)} %slice.49), channel_id=1, source_target_pairs={{0,96},{8,104},{16,112},{24,120},{32,0},{40,8},{48,16},{56,24},{64... | collective-permute-start | bytes 393224 | tf_op jit(solution)/shard_map/ppermute | solution.py:88
  43.7 13.7 %collective-permute-start.8 = (bf16[2,288,512]{2,1,0:T(8,128)(2,1)}, bf16[2,288,512]{2,1,0:T(8,128)(2,1)S(1)}, u32[]{:S(2)}, u32[]{:S(2)}) collective-permute-start(bf16[2,288,512]{2,1,0:T(8,128)(2,1)} %pad_maximum_fusion.6), channel_id=1, source_target_pairs={{0,96},{8,104},{16,112},{24,120},{32,0},{40,8},{48,16},{56,24},{64... | collective-permute-start | bytes 1769480 | tf_op jit(solution)/shard_map/ppermute | solution.py:88
  46.9 14.7 %collective-permute-start.7 = (bf16[2,288,512]{2,1,0:T(8,128)(2,1)}, bf16[2,288,512]{2,1,0:T(8,128)(2,1)S(1)}, u32[]{:S(2)}, u32[]{:S(2)}) collective-permute-start(bf16[2,288,512]{2,1,0:T(8,128)(2,1)} %pad_maximum_fusion.6), channel_id=1, source_target_pairs={{0,32},{8,40},{16,48},{24,56},{32,64},{40,72},{48,80},{56,88},{64,... | collective-permute-start | bytes 1769480 | tf_op jit(solution)/shard_map/ppermute | solution.py:88
  47.8 15.2 %collective-permute-start = (bf16[256,512]{1,0:T(8,128)(2,1)}, bf16[256,512]{1,0:T(8,128)(2,1)S(1)}, u32[]{:S(2)}, u32[]{:S(2)}) collective-permute-start(bf16[256,512]{1,0:T(8,128)(2,1)} %copy.20), channel_id=1, source_target_pairs={{0,16},{8,24},{16,0},{24,8},{32,48},{40,56},{48,32},{56,40},{64,80... | collective-permute-start | bytes 786440 | tf_op jit(solution)/shard_map/ppermute | solution.py:92
  52.9 26.6 %collective-permute-start.23 = (bf16[4,256,512]{2,1,0:T(8,128)(2,1)S(1)}, bf16[4,256,512]{2,1,0:T(8,128)(2,1)}, u32[]{:S(2)}, u32[]{:S(2)}) collective-permute-start(bf16[4,256,512]{2,1,0:T(8,128)(2,1)S(1)} %pad_maximum_fusion.3.own0), channel_id=1, source_target_pairs={{0,16},{8,24},{16,0},{24,8},{32,48},{40,56},{48,32},{56,40},{64,80... | collective-permute-start | bytes 3145736 | tf_op jit(solution)/shard_map/ppermute | solution.py:92
  54.9 11.9 %collective-permute-start.22 = (bf16[256,512]{1,0:T(8,128)(2,1)S(1)}, bf16[256,512]{1,0:T(8,128)(2,1)S(1)}, u32[]{:S(2)}, u32[]{:S(2)}) collective-permute-start(bf16[256,512]{1,0:T(8,128)(2,1)S(1)} %get-tuple-element.36), channel_id=1, source_target_pairs={{0,2},{1,3},{2,4},{3,5},{4,6},{5,7},{6,0},{7,1},{8,10},{9,11},{10,... | collective-permute-start | bytes 786440 | tf_op jit(solution)/shard_map/ppermute | solution.py:100
  57.3 14.4 %collective-permute-start.21 = (bf16[256,512]{1,0:T(8,128)(2,1)}, bf16[256,512]{1,0:T(8,128)(2,1)}, u32[]{:S(2)}, u32[]{:S(2)}) collective-permute-start(bf16[256,512]{1,0:T(8,128)(2,1)} %get-tuple-element.37), channel_id=1, source_target_pairs={{0,4},{1,5},{2,6},{3,7},{4,0},{5,1},{6,2},{7,3},{8,12},{9,13},{10,... | collective-permute-start | bytes 786440 | tf_op jit(solution)/shard_map/ppermute | solution.py:100
  62.9 59.3 %collective-permute-start.9 = (bf16[6,288,512]{2,1,0:T(8,128)(2,1)}, bf16[6,288,512]{2,1,0:T(8,128)(2,1)}, u32[]{:S(2)}, u32[]{:S(2)}) collective-permute-start(bf16[6,288,512]{2,1,0:T(8,128)(2,1)} %pad_maximum_fusion.1.refs_2_), channel_id=1, source_target_pairs={{0,8},{8,0},{16,24},{24,16},{32,40},{40,32},{48,56},{56,48},{64,72... | collective-permute-start | bytes 5308424 | tf_op jit(solution)/shard_map/ppermute | solution.py:96
  71.7 33.4 %collective-permute-start.2 = (bf16[2,256,512]{2,1,0:T(8,128)(2,1)S(1)}, bf16[2,256,512]{2,1,0:T(8,128)(2,1)S(1)}, u32[]{:S(2)}, u32[]{:S(2)}) collective-permute-start(bf16[2,256,512]{2,1,0:T(8,128)(2,1)S(1)} %pad_maximum_fusion.8), channel_id=1, source_target_pairs={{0,96},{8,104},{16,112},{24,120},{32,0},{40,8},{48,16},{56,24},{64... | collective-permute-start | bytes 1572872 | tf_op jit(solution)/shard_map/ppermute | solution.py:88
  72.5 32.8 %collective-permute-start.1 = (bf16[2,256,512]{2,1,0:T(8,128)(2,1)S(1)}, bf16[2,256,512]{2,1,0:T(8,128)(2,1)S(1)}, u32[]{:S(2)}, u32[]{:S(2)}) collective-permute-start(bf16[2,256,512]{2,1,0:T(8,128)(2,1)S(1)} %pad_maximum_fusion.8), channel_id=1, source_target_pairs={{0,32},{8,40},{16,48},{24,56},{32,64},{40,72},{48,80},{56,88},{64,... | collective-permute-start | bytes 1572872 | tf_op jit(solution)/shard_map/ppermute | solution.py:88
  77.6 30.7 %collective-permute-start.4 = (bf16[2,256,512]{2,1,0:T(8,128)(2,1)S(1)}, bf16[2,256,512]{2,1,0:T(8,128)(2,1)S(1)}, u32[]{:S(2)}, u32[]{:S(2)}) collective-permute-start(bf16[2,256,512]{2,1,0:T(8,128)(2,1)S(1)} %pad_maximum_fusion.8), channel_id=1, source_target_pairs={{0,64},{8,72},{16,80},{24,88},{32,96},{40,104},{48,112},{56,120},{... | collective-permute-start | bytes 1572872 | tf_op jit(solution)/shard_map/ppermute | solution.py:88
  79.6 24.7 %collective-permute-start.10 = (bf16[288,512]{1,0:T(8,128)(2,1)S(1)}, bf16[288,512]{1,0:T(8,128)(2,1)S(1)}, u32[]{:S(2)}, u32[]{:S(2)}) collective-permute-start(bf16[288,512]{1,0:T(8,128)(2,1)S(1)} %slice_bitcast_fusion.1), channel_id=1, source_target_pairs={{0,32},{8,40},{16,48},{24,56},{32,64},{40,72},{48,80},{56,88},{64,... | collective-permute-start | bytes 884744 | tf_op jit(solution)/shard_map/ppermute | solution.py:88
  105.1 16.2 %collective-permute-start.12 = (bf16[2,288,512]{2,1,0:T(8,128)(2,1)S(1)}, bf16[2,288,512]{2,1,0:T(8,128)(2,1)S(1)}, u32[]{:S(2)}, u32[]{:S(2)}) collective-permute-start(bf16[2,288,512]{2,1,0:T(8,128)(2,1)S(1)} %pad_maximum_fusion.7.refs_4_), channel_id=1, source_target_pairs={{0,8},{8,0},{16,24},{24,16},{32,40},{40,32},{48,56},{56,48},{64,72... | collective-permute-start | bytes 1769480 | tf_op jit(solution)/shard_map/ppermute | solution.py:96
  105.2 13.4 %collective-permute-start.25 = (bf16[256,512]{1,0:T(8,128)(2,1)S(1)}, bf16[256,512]{1,0:T(8,128)(2,1)S(1)}, u32[]{:S(2)}, u32[]{:S(2)}) collective-permute-start(bf16[256,512]{1,0:T(8,128)(2,1)S(1)} %get-tuple-element.41), channel_id=1, source_target_pairs={{0,4},{1,5},{2,6},{3,7},{4,0},{5,1},{6,2},{7,3},{8,12},{9,13},{10,... | collective-permute-start | bytes 786440 | tf_op jit(solution)/shard_map/ppermute | solution.py:100
  108.4 12.6 %collective-permute-start.24 = (bf16[256,512]{1,0:T(8,128)(2,1)S(1)}, bf16[256,512]{1,0:T(8,128)(2,1)S(1)}, u32[]{:S(2)}, u32[]{:S(2)}) collective-permute-start(bf16[256,512]{1,0:T(8,128)(2,1)S(1)} %get-tuple-element.42), channel_id=1, source_target_pairs={{0,6},{1,7},{2,0},{3,1},{4,2},{5,3},{6,4},{7,5},{8,14},{9,15},{10,... | collective-permute-start | bytes 786440 | tf_op jit(solution)/shard_map/ppermute | solution.py:100
  113.5 26.0 %collective-permute-start.3 = (bf16[6,256,512]{2,1,0:T(8,128)(2,1)}, bf16[6,256,512]{2,1,0:T(8,128)(2,1)}, u32[]{:S(2)}, u32[]{:S(2)}) collective-permute-start(bf16[6,256,512]{2,1,0:T(8,128)(2,1)} %pad_maximum_fusion.2.refs_2_), channel_id=1, source_target_pairs={{0,8},{8,0},{16,24},{24,16},{32,40},{40,32},{48,56},{56,48},{64,72... | collective-permute-start | bytes 4718600 | tf_op jit(solution)/shard_map/ppermute | solution.py:96
  118.7 36.1 %collective-permute-start.37 = (bf16[4,256,512]{2,1,0:T(8,128)(2,1)S(1)}, bf16[4,256,512]{2,1,0:T(8,128)(2,1)}, u32[]{:S(2)}, u32[]{:S(2)}) collective-permute-start(bf16[4,256,512]{2,1,0:T(8,128)(2,1)S(1)} %pad_maximum_fusion.3.own0), channel_id=1, source_target_pairs={{0,8},{8,0},{16,24},{24,16},{32,40},{40,32},{48,56},{56,48},{64,72... | collective-permute-start | bytes 3145736 | tf_op jit(solution)/shard_map/ppermute | solution.py:96
  121.0 18.4 %collective-permute-start.5 = (bf16[2,256,512]{2,1,0:T(8,128)(2,1)S(1)}, bf16[2,256,512]{2,1,0:T(8,128)(2,1)}, u32[]{:S(2)}, u32[]{:S(2)}) collective-permute-start(bf16[2,256,512]{2,1,0:T(8,128)(2,1)S(1)} %collective-permute-done.4.refs_4_), channel_id=1, source_target_pairs={{0,8},{8,0},{16,24},{24,16},{32,40},{40,32},{48,56},{56,48},{64,72... | collective-permute-start | bytes 1572872 | tf_op jit(solution)/shard_map/ppermute | solution.py:96
  121.3 35.4 %collective-permute-start.38 = (bf16[4,256,512]{2,1,0:T(8,128)(2,1)}, bf16[4,256,512]{2,1,0:T(8,128)(2,1)}, u32[]{:S(2)}, u32[]{:S(2)}) collective-permute-start(bf16[4,256,512]{2,1,0:T(8,128)(2,1)} %collective-permute-done.23.own1), channel_id=1, source_target_pairs={{0,8},{8,0},{16,24},{24,16},{32,40},{40,32},{48,56},{56,48},{64,72... | collective-permute-start | bytes 3145736 | tf_op jit(solution)/shard_map/ppermute | solution.py:96
  122.2 65.4 %collective-permute-start.27 = (bf16[2,4,256,512]{3,2,1,0:T(8,128)(2,1)S(1)}, bf16[2,4,256,512]{3,2,1,0:T(8,128)(2,1)}, u32[]{:S(2)}, u32[]{:S(2)}) collective-permute-start(bf16[2,4,256,512]{3,2,1,0:T(8,128)(2,1)S(1)} %pad_maximum_fusion.own_ref), channel_id=1, source_target_pairs={{0,8},{8,0},{16,24},{24,16},{32,40},{40,32},{48,56},{56,48},{64,72... | collective-permute-start | bytes 6291464 | tf_op jit(solution)/shard_map/ppermute | solution.py:96
  154.7 21.6 %collective-permute-start.29 = (bf16[384,512]{1,0:T(8,128)(2,1)}, bf16[384,512]{1,0:T(8,128)(2,1)}, u32[]{:S(2)}, u32[]{:S(2)}) collective-permute-start(bf16[384,512]{1,0:T(8,128)(2,1)} %get-tuple-element.26.g0), channel_id=1, source_target_pairs={{0,6},{1,7},{2,0},{3,1},{4,2},{5,3},{6,4},{7,5},{8,14},{9,15},{10,... | collective-permute-start | bytes 1179656 | tf_op jit(solution)/shard_map/ppermute | solution.py:100
  154.8 24.7 %collective-permute-start.14 = (bf16[384,512]{1,0:T(8,128)(2,1)}, bf16[384,512]{1,0:T(8,128)(2,1)}, u32[]{:S(2)}, u32[]{:S(2)}) collective-permute-start(bf16[384,512]{1,0:T(8,128)(2,1)} %get-tuple-element.23.g0), channel_id=1, source_target_pairs={{0,2},{1,3},{2,4},{3,5},{4,6},{5,7},{6,0},{7,1},{8,10},{9,11},{10,... | collective-permute-start | bytes 1179656 | tf_op jit(solution)/shard_map/ppermute | solution.py:100
  156.7 16.1 %collective-permute-start.34 = (bf16[256,512]{1,0:T(8,128)(2,1)}, bf16[256,512]{1,0:T(8,128)(2,1)S(1)}, u32[]{:S(2)}, u32[]{:S(2)}) collective-permute-start(bf16[256,512]{1,0:T(8,128)(2,1)} %get-tuple-element.29.g0), channel_id=1, source_target_pairs={{0,4},{1,5},{2,6},{3,7},{4,0},{5,1},{6,2},{7,3},{8,12},{9,13},{10,... | collective-permute-start | bytes 786440 | tf_op jit(solution)/shard_map/ppermute | solution.py:100
  161.7 17.2 %collective-permute-start.35 = (bf16[256,512]{1,0:T(8,128)(2,1)}, bf16[256,512]{1,0:T(8,128)(2,1)S(1)}, u32[]{:S(2)}, u32[]{:S(2)}) collective-permute-start(bf16[256,512]{1,0:T(8,128)(2,1)} %get-tuple-element.29.g0), channel_id=1, source_target_pairs={{0,2},{1,3},{2,4},{3,5},{4,6},{5,7},{6,0},{7,1},{8,10},{9,11},{10,... | collective-permute-start | bytes 786440 | tf_op jit(solution)/shard_map/ppermute | solution.py:100
  172.8 21.4 %collective-permute-start.31 = (bf16[384,512]{1,0:T(8,128)(2,1)}, bf16[384,512]{1,0:T(8,128)(2,1)S(1)}, u32[]{:S(2)}, u32[]{:S(2)}) collective-permute-start(bf16[384,512]{1,0:T(8,128)(2,1)} %get-tuple-element.26.g0), channel_id=1, source_target_pairs={{0,2},{1,3},{2,4},{3,5},{4,6},{5,7},{6,0},{7,1},{8,10},{9,11},{10,... | collective-permute-start | bytes 1179656 | tf_op jit(solution)/shard_map/ppermute | solution.py:100
  176.3 17.9 %collective-permute-start.30 = (bf16[384,512]{1,0:T(8,128)(2,1)}, bf16[384,512]{1,0:T(8,128)(2,1)}, u32[]{:S(2)}, u32[]{:S(2)}) collective-permute-start(bf16[384,512]{1,0:T(8,128)(2,1)} %collective-permute-done.29.g1), channel_id=1, source_target_pairs={{0,6},{1,7},{2,0},{3,1},{4,2},{5,3},{6,4},{7,5},{8,14},{9,15},{10,... | collective-permute-start | bytes 1179656 | tf_op jit(solution)/shard_map/ppermute | solution.py:100
  178.9 23.8 %collective-permute-start.13 = (bf16[384,512]{1,0:T(8,128)(2,1)}, bf16[384,512]{1,0:T(8,128)(2,1)}, u32[]{:S(2)}, u32[]{:S(2)}) collective-permute-start(bf16[384,512]{1,0:T(8,128)(2,1)} %get-tuple-element.23.g0), channel_id=1, source_target_pairs={{0,6},{1,7},{2,0},{3,1},{4,2},{5,3},{6,4},{7,5},{8,14},{9,15},{10,... | collective-permute-start | bytes 1179656 | tf_op jit(solution)/shard_map/ppermute | solution.py:100
  179.4 23.3 %collective-permute-start.15 = (bf16[384,512]{1,0:T(8,128)(2,1)}, bf16[384,512]{1,0:T(8,128)(2,1)}, u32[]{:S(2)}, u32[]{:S(2)}) collective-permute-start(bf16[384,512]{1,0:T(8,128)(2,1)} %collective-permute-done.14.g3), channel_id=1, source_target_pairs={{0,2},{1,3},{2,4},{3,5},{4,6},{5,7},{6,0},{7,1},{8,10},{9,11},{10,... | collective-permute-start | bytes 1179656 | tf_op jit(solution)/shard_map/ppermute | solution.py:100
  192.6 17.6 %collective-permute-start.36 = (bf16[256,512]{1,0:T(8,128)(2,1)}, bf16[256,512]{1,0:T(8,128)(2,1)S(1)}, u32[]{:S(2)}, u32[]{:S(2)}) collective-permute-start(bf16[256,512]{1,0:T(8,128)(2,1)} %get-tuple-element.31), channel_id=1, source_target_pairs={{0,1},{1,0},{2,3},{3,2},{4,5},{5,4},{6,7},{7,6},{8,9},{9,8},{10,11... | collective-permute-start | bytes 786440 | tf_op jit(solution)/shard_map/ppermute | solution.py:104
  200.8 11.5 %collective-permute-start.32 = (bf16[384,512]{1,0:T(8,128)(2,1)}, bf16[384,512]{1,0:T(8,128)(2,1)S(1)}, u32[]{:S(2)}, u32[]{:S(2)}) collective-permute-start(bf16[384,512]{1,0:T(8,128)(2,1)} %get-tuple-element.28), channel_id=1, source_target_pairs={{0,1},{1,0},{2,3},{3,2},{4,5},{5,4},{6,7},{7,6},{8,9},{9,8},{10,11... | collective-permute-start | bytes 1179656 | tf_op jit(solution)/shard_map/ppermute | solution.py:104
  208.6 11.2 %collective-permute-start.28 = (bf16[384,512]{1,0:T(8,128)(2,1)}, bf16[384,512]{1,0:T(8,128)(2,1)S(1)}, u32[]{:S(2)}, u32[]{:S(2)}) collective-permute-start(bf16[384,512]{1,0:T(8,128)(2,1)} %get-tuple-element.25), channel_id=1, source_target_pairs={{0,1},{1,0},{2,3},{3,2},{4,5},{5,4},{6,7},{7,6},{8,9},{9,8},{10,11... | collective-permute-start | bytes 1179656 | tf_op jit(solution)/shard_map/ppermute | solution.py:104
  (30 other events, 389.7 us)

commit v3 on v2

--- a/solution.py
+++ b/solution.py
@@ -23,7 +23,7 @@
 
 
 CH = 512
-BIG = pltpu.CompilerParams(vmem_limit_bytes=60 << 20)
+BIG = pltpu.CompilerParams(vmem_limit_bytes=28 << 20)
 
 
 def scan_kernel(bi_ref, g_ref, rate_ref, out_ref, gates_ref):
@@ -171,14 +171,18 @@
         put_all(far_ref, far_peer_ref)
 
     w = w_ref[...].reshape(1024, 512)
+    if extra:
+        tok = tok_ref[...]
+    else:
+        tok = tok_ref[:, pl.ds(pl.multiple_of(meta[step] * 1024, 1024), 1024)]
 
     @pl.when(step == 0)
     def _():
-        acc_ref[...] = jnp.dot(tok_ref[...], w, preferred_element_type=F32)
+        acc_ref[...] = jnp.dot(tok, w, preferred_element_type=F32)
 
     @pl.when(step > 0)
     def _():
-        acc_ref[...] += jnp.dot(tok_ref[...], w, preferred_element_type=F32)
+        acc_ref[...] += jnp.dot(tok, w, preferred_element_type=F32)
 
     @pl.when(step == 3)
     def _():
@@ -206,7 +210,8 @@
     rows = 256 + extra
     near = pl.BlockSpec((2, rows, 512), lambda s, m: (jnp.minimum(s, 2), 0, 0))
     operands = [tokens, *parts]
-    in_specs = [pl.BlockSpec((1024, 1024), lambda s, m: (0, m[s])), near, near]
+    blocked = pl.BlockSpec((1024, 1024), lambda s, m: (0, m[s]))
+    in_specs = [blocked if extra else pl.BlockSpec(memory_space=pltpu.VMEM), near, near]
     in_specs += [whole((2, rows, 512))] * 2
     out_shape = [jax.ShapeDtypeStruct((8, 2, 256, 512), BF)]
     out_specs = [pl.BlockSpec((2, 2, 256, 512), lambda s, m: (m[s], 0, 0, 0))]
@@ -228,7 +233,7 @@
             out_specs=out_specs,
             scratch_shapes=[pltpu.VMEM((1024, 512), F32)],
         ),
-        compiler_params=BIG,
+        compiler_params=pltpu.CompilerParams(vmem_limit_bytes=(58 if extra else 28) << 20),
         cost_estimate=pl.CostEstimate(
             flops=4_300_000_000, bytes_accessed=18 << 20, transcendentals=0
         ),
@@ -259,7 +264,7 @@
         side(keep_ref)
 
 
-def project(meta, gs, w_own, w_peer):
+def project(meta, gs, w_own, w_peer, limit):
     size = gs[0].shape[0]
     wspec = pl.BlockSpec((1, 4, 256, 512), lambda s, m: (jnp.bitwise_xor(m[0], s), 0, 0, 0))
     return pl.pallas_call(
@@ -274,12 +279,77 @@
             in_specs=[whole(g.shape) for g in gs] + [wspec, wspec],
             out_specs=[whole((size, 512))] * 2,
         ),
-        compiler_params=BIG,
+        compiler_params=pltpu.CompilerParams(vmem_limit_bytes=limit << 20),
         cost_estimate=pl.CostEstimate(
             flops=size * 2048 * 2048, bytes_accessed=8 << 20, transcendentals=0
         ),
         name="project",
     )(meta, *gs, w_own, w_peer)
+
+
+def pack_kernel(meta, in_ref, br_ref, out_ref, g_ref, *refs):
+    sends, turned = refs[:8], refs[8]
+    for n, w_ref in enumerate((in_ref, br_ref, out_ref)):
+        turned[n] = jnp.swapaxes(w_ref[...], 0, 1).astype(BF)
+    for r in range(8):
+        peer = jnp.bitwise_xor(meta[16], r)
+        blocks = [meta[2 * peer + j] for j in range(2)]
+        for n in range(3):
+            for j in range(2):
+                sends[r][n * 64 + j * 32 : n * 64 + j * 32 + 32, :] = turned[n, blocks[j]]
+        parts = [g_ref[g, blocks[j]] for g in range(2) for j in range(2)]
+        gates = jnp.concatenate(parts, axis=1)
+        sends[r][192:208, :] = jnp.concatenate([gates, gates], axis=1).astype(BF)
+
+
+def pack(meta, sources, gates):
+    return pl.pallas_call(
+        pack_kernel,
+        out_shape=[jax.ShapeDtypeStruct((208, 256), BF)] * 8,
+        grid_spec=pltpu.PrefetchScalarGridSpec(
+            num_scalar_prefetch=1,
+            grid=(1,),
+            in_specs=[whole((32, 16, 256))] * 3 + [whole((2, 16, 16, 32))],
+            out_specs=[whole((208, 256))] * 8,
+            scratch_shapes=[pltpu.VMEM((3, 16, 32, 256), BF)],
+        ),
+        cost_estimate=pl.CostEstimate(flops=4_000_000, bytes_accessed=3 << 20, transcendentals=0),
+        name="pack",
+    )(meta, *sources, gates)
+
+
+def unpack_kernel(meta, *refs):
+    got, (in_ref, br_ref, out_ref), rows, gates = refs[:8], refs[8:11], refs[11], refs[12]
+    for r in range(8):
+        peer = jnp.bitwise_xor(meta[16], r)
+        for n in range(3):
+            for j in range(2):
+                rows[n, j, peer] = got[r][n * 64 + j * 32 : n * 64 + j * 32 + 32, :]
+        gates[peer] = got[r][192:208, :128].astype(F32)
+    for n, ref in enumerate((in_ref, br_ref, out_ref)):
+        for j in range(2):
+            ref[:256, j * 256 : j * 256 + 256] = rows[n, j].reshape(256, 256).T
+    for g in range(2):
+        for j in range(2):
+            at = (g * 2 + j) * 32
+            line = jnp.concatenate([gates[p][:, at : at + 32] for p in range(8)], axis=1)
+            in_ref[256 + g * 16 : 272 + g * 16, j * 256 : j * 256 + 256] = line.astype(BF)
+
+
+def unpack(meta, got):
+    return pl.pallas_call(
+        unpack_kernel,
+        out_shape=[jax.ShapeDtypeStruct((rows, 512), BF) for rows in (288, 256, 256)],
+        grid_spec=pltpu.PrefetchScalarGridSpec(
+            num_scalar_prefetch=1,
+            grid=(1,),
+            in_specs=[whole((208, 256))] * 8,
+            out_specs=[whole((rows, 512)) for rows in (288, 256, 256)],
+            scratch_shapes=[pltpu.VMEM((3, 2, 8, 32, 256), BF), pltpu.VMEM((8, 16, 128), F32)],
+        ),
+        cost_estimate=pl.CostEstimate(flops=4_000_000, bytes_accessed=3 << 20, transcendentals=0),
+        name="unpack",
+    )(meta, *got)
 
 
 def gather_z_first(name, q):
@@ -301,28 +371,17 @@
     x, z, core, y, zh = position()
     own_blocks = lax.dynamic_slice_in_dim(block_order, (y * 2 + zh) * 2, 2)
 
-    def section(w):
-        picked = jnp.take(w.astype(BF), block_order, axis=1, mode="clip")
-        return jnp.transpose(picked, (1, 0, 2)).reshape(8, 64, 256)
-
-    gates_picked = jnp.take(gates_source.astype(BF), block_order, axis=1, mode="clip")
-    gates_flat = jnp.transpose(gates_picked.reshape(2, 8, 2, 16, 32), (1, 0, 2, 3, 4)).reshape(8, 8, 256)
-    packed = jnp.concatenate(
-        [section(input_source), section(branch_source), section(output_source), gates_flat], axis=1
-    )
-    swapped = lax.all_to_all(packed, "tensor", 0, 0, tiled=True)
-
-    def piece(n):
-        part = swapped[:, n * 64 : (n + 1) * 64].reshape(8, 2, 32, 256)
-        return jnp.transpose(part, (3, 1, 0, 2)).reshape(256, 512)
-
-    gate_part = swapped[:, 192:200].reshape(8, 2, 2, 16, 32)
-    gate_rows = jnp.transpose(gate_part, (1, 3, 2, 0, 4)).reshape(32, 512)
+    pack_meta = jnp.concatenate([block_order, lax.axis_index("tensor")[None]]).astype(jnp.int32)
+    sends = pack(pack_meta, (input_source, branch_source, output_source), gates_source)
+    got = [sends[0]]
+    for r in range(1, 8):
+        got.append(lax.ppermute(sends[r], "tensor", [(t, t ^ r) for t in range(8)]))
+    in_piece, br_piece, out_piece = unpack(pack_meta, got)
 
     pair_meta = slot_meta((0, -1, 1, 2))
     row_meta = slot_meta((0, 1, 2, 3))
 
-    q = piece(2)
+    q = out_piece
     left = send_x(q, 1)
     right = send_x(q, -1)
     far_top = send_x(left[:128], 1)
@@ -341,14 +400,15 @@
     w_peer = send_core(w_own)
     out_peers = (send_core(row), send_core(other_row))
 
-    in_parts = gather_z_first("in", jnp.concatenate([piece(0), gate_rows]))
-    br_parts = gather_z_first("br", piece(1))
+    in_parts = gather_z_first("in", in_piece)
+    br_parts = gather_z_first("br", br_piece)
 
     w, g, branch_in = matmul(pair_meta, tokens, in_parts, 32)
     input_serve = w.reshape(4096, 512)
     rate = -8.0 * jax.nn.softplus(jnp.take(decay_param, own_blocks, axis=0, mode="clip")).reshape(1, 512)
     states, gates_serve = gate_scan(branch_in, g.reshape(16, 32, 512), rate)
-    w, *gated = matmul(pair_meta, tokens, br_parts, 0, states)
+    held = pltpu.with_memory_space_constraint(tokens, pltpu.VMEM)
+    w, *gated = matmul(pair_meta, held, br_parts, 0, states)
     branch_serve = w.reshape(4096, 512)
     output_serve = place(row_meta, (row, other_row), out_peers)
 
@@ -364,7 +424,7 @@
         else:
             far = send_y(g, 2)
         terms = (g, above, far, below)
-        give, keep = project(give_meta, terms, w_own, w_peer)
+        give, keep = project(give_meta, terms, w_own, w_peer, (28, 58, 28)[n])
         got = send_zhi(give)
         parts.append((keep + got.astype(F32)).astype(BF))
     mixed = jnp.concatenate(parts)

time: 221 us -> 227 us (1.027)
  blocking collectives: 22.6 us -> 0 us
  waiting for transfers between devices: 71 us -> 88 us
  starting transfers between devices: 50.1 us -> 65.6 us
  other arithmetic: 13.1 us -> 8.83 us
    all_to_all x1 -> x0, blocking collectives: 22.6 us -> none  [on_device(): swapped = lax.all_to_all(packed, 'tensor', 0, 0, tiled=True)]
    ppermute x0 -> x7, starting transfers between devices: none -> 15 us  [on_device(): got.append(lax.ppermute(sends[r], 'tensor', [(t, t ^ r) for t in range(8)]))]
    ppermute x0 -> x7, waiting for transfers between devices: none -> 8.5 us  [on_device(): got.append(lax.ppermute(sends[r], 'tensor', [(t, t ^ r) for t in range(8)]))]
    unnamed x50 -> x67, local copies, waits for them, and re-layouts: 3.04 us -> 10.3 us
    ppermute x11, waiting for transfers between devices: 33.6 us -> 40.5 us  [send_x(): return lax.ppermute(a, 'fsdp', fsdp_perm(dx=dx))]
    ppermute x11, starting transfers between devices: 19.9 us -> 13.3 us  [send_x(): return lax.ppermute(a, 'fsdp', fsdp_perm(dx=dx))]
    pallas_call x0 -> x2, Pallas kernels: none -> 6.41 us  [the longest x1 3.39 us: pack(): pl.pallas_call(pack_kernel, out_shape=[jax.ShapeDtypeStruct((208, 256), B...]
    ppermute x15, starting transfers between devices: 20.6 us -> 26.2 us  [send_y(): return lax.ppermute(a, 'tensor', tensor_perm(dy=dy))]
  transfers between devices with their start and end apart: 39 -> 46, of which waited for: 15 -> 18; matrix products, arithmetic and copies ran while one was open for 7% -> 4% of each run, Pallas kernels for 23% -> 20%
where the time goes in v3:
time: 227 us
  waiting for transfers between devices  88 us (39%)
  starting transfers between devices  65.6 us (29%)
  Pallas kernels  51 us (22%)
  local copies, waits for them, and re-layouts  12 us (5%)
  other arithmetic  8.83 us (4%)
    ppermute x11, waiting for transfers between devices, send_x(): return lax.ppermute(a, 'fsdp', fsdp_perm(dx=dx))  40.5 us
    ppermute x15, waiting for transfers between devices, send_y(): return lax.ppermute(a, 'tensor', tensor_perm(dy=dy))  28.6 us
    ppermute x15, starting transfers between devices, send_y(): return lax.ppermute(a, 'tensor', tensor_perm(dy=dy))  26.2 us
    pallas_call x2, Pallas kernels, matmul(): pl.pallas_call(lambda *refs: matmul_kernel(extra, *refs), out_shape=out_s...  22 us
    ppermute x7, starting transfers between devices, on_device(): got.append(lax.ppermute(sends[r], 'tensor', [(t, t ^ r) for t in range(8)]))  15 us
    pallas_call x3, Pallas kernels, project(): pl.pallas_call(project_kernel, out_shape=[jax.ShapeDtypeStruct((size, 512...  13.6 us
    ppermute x11, starting transfers between devices, send_x(): return lax.ppermute(a, 'fsdp', fsdp_perm(dx=dx))  13.3 us
    ppermute x3, waiting for transfers between devices, send_zhi(): return lax.ppermute(a, 'tensor', tensor_perm(dz=1))  10.5 us
  transfers between devices with their start and end apart: 46, of which 18 were waited for; matrix products, arithmetic and copies ran while one was open for 4% of the time, Pallas kernels for 20%

profile of v3, /device:TPU:0, one launch (start us, length us, event | category | flops | bytes accessed | tf_op | source)
XLA Modules:
  0.0 226.6 jit_solution(15747534338368714509)
XLA Ops:
  2.0 3.4 %pack.1 = (bf16[208,256]{1,0:T(8,128)(2,1)}, bf16[208,256]{1,0:T(8,128)(2,1)}, bf16[208,256]{1,0:T(8,128)(2,1)}, bf16[208,256]{1,0:T(8,128)(2,1)}, bf16[208,256]...) custom-call(s32[17]{0:T(128)} %pad_add_fusion.1.meta, ...), custom_call_target="tpu_custom_call" | custom-call | flops 4000000 | bytes 3145728 | tf_op jit(solution)/shard_map/pack/pallas_call | solution.py:306
  5.4 4.0 %collective-permute-start = (bf16[208,256]{1,0:T(8,128)(2,1)}, bf16[208,256]{1,0:T(8,128)(2,1)S(1)}, u32[]{:S(2)}, u32[]{:S(2)}) collective-permute-start(bf16[208,256]{1,0:T(8,128)(2,1)} %get-tuple-element.32), channel_id=1, source_target_pairs={{0,1},{1,0},{2,3},{3,2},{4,5},{5,4},{6,7},{7,6},{8,9},{9,8},{10,11... | collective-permute-start | bytes 319496 | tf_op jit(solution)/shard_map/ppermute | solution.py:378
  11.0 3.2 %collective-permute-start.3 = (bf16[208,256]{1,0:T(8,128)(2,1)}, bf16[208,256]{1,0:T(8,128)(2,1)S(1)}, u32[]{:S(2)}, u32[]{:S(2)}) collective-permute-start(bf16[208,256]{1,0:T(8,128)(2,1)} %get-tuple-element.35), channel_id=1, source_target_pairs={{0,4},{1,5},{2,6},{3,7},{4,0},{5,1},{6,2},{7,3},{8,12},{9,13},{10,... | collective-permute-start | bytes 319496 | tf_op jit(solution)/shard_map/ppermute | solution.py:378
  14.2 3.2 %collective-permute-start.4 = (bf16[208,256]{1,0:T(8,128)(2,1)}, bf16[208,256]{1,0:T(8,128)(2,1)S(1)}, u32[]{:S(2)}, u32[]{:S(2)}) collective-permute-start(bf16[208,256]{1,0:T(8,128)(2,1)} %get-tuple-element.36), channel_id=1, source_target_pairs={{0,5},{1,4},{2,7},{3,6},{4,1},{5,0},{6,3},{7,2},{8,13},{9,12},{10,... | collective-permute-start | bytes 319496 | tf_op jit(solution)/shard_map/ppermute | solution.py:378
  17.4 3.0 %collective-permute-start.5 = (bf16[208,256]{1,0:T(8,128)(2,1)}, bf16[208,256]{1,0:T(8,128)(2,1)S(1)}, u32[]{:S(2)}, u32[]{:S(2)}) collective-permute-start(bf16[208,256]{1,0:T(8,128)(2,1)} %get-tuple-element.37), channel_id=1, source_target_pairs={{0,6},{1,7},{2,4},{3,5},{4,2},{5,3},{6,0},{7,1},{8,14},{9,15},{10,... | collective-permute-start | bytes 319496 | tf_op jit(solution)/shard_map/ppermute | solution.py:378
  25.7 3.2 %collective-permute-done.6.refs_7_ = bf16[208,256]{1,0:T(8,128)(2,1)S(1)} collective-permute-done((bf16[208,256]{1,0:T(8,128)(2,1)}, bf16[208,256]{1,0:T(8,128)(2,1)S(1)}, u32[]{:S(2)}, u32[]{:S(2)}) %collective-permute-start.6) | collective-permute-done | bytes 106528 | tf_op jit(solution)/shard_map/ppermute | solution.py:378
  29.6 3.0 %unpack.1 = (bf16[288,512]{1,0:T(8,128)(2,1)}, bf16[256,512]{1,0:T(8,128)(2,1)}, bf16[256,512]{1,0:T(8,128)(2,1)}) custom-call(s32[17]{0:T(128)} %pad_add_fusion.1.meta, bf16[208,256]{1,0:T(8,128)(2,1)} %get-tuple-element.31.refs_0_, bf16[208,256]{1,0:T(8,128)(2,1)} %copy-done.23, bf16[208,256]{1,0:T(8,128)(2,1)} %copy-done.24, bf16[208,256]{1,0:T(8,128)(2,1)} %copy-done.25, ...), custom_call_target="tpu_custom_call" | custom-call | flops 4000000 | bytes 3145728 | tf_op jit(solution)/shard_map/unpack/pallas_call | solution.py:340
  36.5 4.2 %collective-permute-done.23 = bf16[256,512]{1,0:T(8,128)(2,1)S(1)} collective-permute-done((bf16[256,512]{1,0:T(8,128)(2,1)}, bf16[256,512]{1,0:T(8,128)(2,1)S(1)}, u32[]{:S(2)}, u32[]{:S(2)}) %collective-permute-start.23) | collective-permute-done | bytes 262176 | tf_op jit(solution)/shard_map/ppermute | solution.py:88
  40.7 3.6 %collective-permute-start.26 = (bf16[128,512]{1,0:T(8,128)(2,1)S(1)}, bf16[128,512]{1,0:T(8,128)(2,1)S(1)}, u32[]{:S(2)}, u32[]{:S(2)}) collective-permute-start(bf16[128,512]{1,0:T(8,128)(2,1)S(1)} %slice.21), channel_id=1, source_target_pairs={{0,96},{8,104},{16,112},{24,120},{32,0},{40,8},{48,16},{56,24},{64... | collective-permute-start | bytes 393224 | tf_op jit(solution)/shard_map/ppermute | solution.py:88
  45.5 3.3 %collective-permute-start.15 = (bf16[2,288,512]{2,1,0:T(8,128)(2,1)S(1)}, bf16[2,288,512]{2,1,0:T(8,128)(2,1)S(1)}, u32[]{:S(2)}, u32[]{:S(2)}) collective-permute-start(bf16[2,288,512]{2,1,0:T(8,128)(2,1)S(1)} %pad_maximum_fusion.5), channel_id=1, source_target_pairs={{0,96},{8,104},{16,112},{24,120},{32,0},{40,8},{48,16},{56,24},{64... | collective-permute-start | bytes 1769480 | tf_op jit(solution)/shard_map/ppermute | solution.py:88
  54.2 4.4 %collective-permute-done.15 = bf16[2,288,512]{2,1,0:T(8,128)(2,1)S(1)} collective-permute-done((bf16[2,288,512]{2,1,0:T(8,128)(2,1)S(1)}, bf16[2,288,512]{2,1,0:T(8,128)(2,1)S(1)}, u32[]{:S(2)}, u32[]{:S(2)}) %collective-permute-start.15) | collective-permute-done | bytes 589856 | tf_op jit(solution)/shard_map/ppermute | solution.py:88
  58.6 3.4 %collective-permute-start.28 = (bf16[256,512]{1,0:T(8,128)(2,1)}, bf16[256,512]{1,0:T(8,128)(2,1)}, u32[]{:S(2)}, u32[]{:S(2)}) collective-permute-start(bf16[256,512]{1,0:T(8,128)(2,1)} %get-tuple-element.59), channel_id=1, source_target_pairs={{0,4},{1,5},{2,6},{3,7},{4,0},{5,1},{6,2},{7,3},{8,12},{9,13},{10,... | collective-permute-start | bytes 786440 | tf_op jit(solution)/shard_map/ppermute | solution.py:100
  63.4 4.0 %collective-permute-start.27 = (bf16[256,512]{1,0:T(8,128)(2,1)}, bf16[256,512]{1,0:T(8,128)(2,1)}, u32[]{:S(2)}, u32[]{:S(2)}) collective-permute-start(bf16[256,512]{1,0:T(8,128)(2,1)} %get-tuple-element.60), channel_id=1, source_target_pairs={{0,6},{1,7},{2,0},{3,1},{4,2},{5,3},{6,4},{7,5},{8,14},{9,15},{10,... | collective-permute-start | bytes 786440 | tf_op jit(solution)/shard_map/ppermute | solution.py:100
  70.5 3.5 %collective-permute-done.27 = bf16[256,512]{1,0:T(8,128)(2,1)} collective-permute-done((bf16[256,512]{1,0:T(8,128)(2,1)}, bf16[256,512]{1,0:T(8,128)(2,1)}, u32[]{:S(2)}, u32[]{:S(2)}) %collective-permute-start.27) | collective-permute-done | bytes 262176 | tf_op jit(solution)/shard_map/ppermute | solution.py:100
  74.0 3.4 %collective-permute-done.18 = bf16[288,512]{1,0:T(8,128)(2,1)} collective-permute-done((bf16[288,512]{1,0:T(8,128)(2,1)S(1)}, bf16[288,512]{1,0:T(8,128)(2,1)}, u32[]{:S(2)}, u32[]{:S(2)}) %collective-permute-start.18) | collective-permute-done | bytes 294944 | tf_op jit(solution)/shard_map/ppermute | solution.py:88
  79.9 26.3 %collective-permute-done.17 = bf16[288,512]{1,0:T(8,128)(2,1)S(1)} collective-permute-done((bf16[288,512]{1,0:T(8,128)(2,1)S(1)}, bf16[288,512]{1,0:T(8,128)(2,1)S(1)}, u32[]{:S(2)}, u32[]{:S(2)}) %collective-permute-start.17) | collective-permute-done | bytes 294944 | tf_op jit(solution)/shard_map/ppermute | solution.py:88
  108.8 3.8 %collective-permute-start.32 = (bf16[256,512]{1,0:T(8,128)(2,1)S(1)}, bf16[256,512]{1,0:T(8,128)(2,1)S(1)}, u32[]{:S(2)}, u32[]{:S(2)}) collective-permute-start(bf16[256,512]{1,0:T(8,128)(2,1)S(1)} %get-tuple-element.63), channel_id=1, source_target_pairs={{0,4},{1,5},{2,6},{3,7},{4,0},{5,1},{6,2},{7,3},{8,12},{9,13},{10,... | collective-permute-start | bytes 786440 | tf_op jit(solution)/shard_map/ppermute | solution.py:100
  112.8 3.3 %collective-permute-done.33 = bf16[256,512]{1,0:T(8,128)(2,1)S(1)} collective-permute-done((bf16[256,512]{1,0:T(8,128)(2,1)S(1)}, bf16[256,512]{1,0:T(8,128)(2,1)S(1)}, u32[]{:S(2)}, u32[]{:S(2)}) %collective-permute-start.33) | collective-permute-done | bytes 262176 | tf_op jit(solution)/shard_map/ppermute | solution.py:100
  117.3 4.6 %collective-permute-done.32 = bf16[256,512]{1,0:T(8,128)(2,1)S(1)} collective-permute-done((bf16[256,512]{1,0:T(8,128)(2,1)S(1)}, bf16[256,512]{1,0:T(8,128)(2,1)S(1)}, u32[]{:S(2)}, u32[]{:S(2)}) %collective-permute-start.32) | collective-permute-done | bytes 262176 | tf_op jit(solution)/shard_map/ppermute | solution.py:100
  127.2 11.6 %matmul.2 = (bf16[8,2,256,512]{3,2,1,0:T(8,128)(2,1)}, bf16[8,2,32,512]{3,2,1,0:T(8,128)(2,1)}, bf16[1024,512]{1,0:T(8,128)(2,1)}) custom-call(s32[6]{0:T(128)} %add_add_fusion.refs_0_, bf16[1024,4096]{1,0:T(8,128)(2,1)} %refs_1_.3, bf16[6,288,512]{2,1,0:T(8,128)(2,1)} %pad_maximum_fusion.1.refs_2_, bf16[6,288,512]{2,1,0:T(8,128)(2,1)} %collective-permute-done.16.refs_3_, ...), custom_call_target="tpu_custom_call" | custom-call | flops 4300000256 | bytes 18874368 | tf_op jit(solution)/shard_map/matmul/pallas_call | solution.py:226
  141.1 4.3 %gate_scan.1 = (f32[1024,512]{1,0:T(8,128)S(1)}, bf16[2,2,256,256]{3,2,1,0:T(8,128)(2,1)}) custom-call(bf16[1024,512]{1,0:T(8,128)(2,1)S(1)} %copy-done.14, bf16[16,32,512]{2,1,0:T(8,128)(2,1)S(1)} %bitcast.48, f32[1,512]{1,0:T(1,128)S(1)} %fusion.rate_ref), custom_call_target="tpu_custom_call" | custom-call | flops 8000000000 | bytes 4194304 | tf_op jit(solution)/shard_map/gate_scan/pallas_call | solution.py:63
  145.4 3.4 %copy-done.12 = bf16[1024,4096]{1,0:T(8,128)(2,1)S(1)} copy-done((bf16[1024,4096]{1,0:T(8,128)(2,1)S(1)}, bf16[1024,4096]{1,0:T(8,128)(2,1)}, u32[]{:S(2)}) %copy-start.12) | copy-done | bytes 8388632
  148.7 10.4 %matmul.3 = (bf16[8,2,256,512]{3,2,1,0:T(8,128)(2,1)}, bf16[384,512]{1,0:T(8,128)(2,1)}, bf16[384,512]{1,0:T(8,128)(2,1)}, bf16[256,512]{1,0:T(8,128)(2,1)S(1)}) custom-call(s32[6]{0:T(128)S(1)} %copy-done.9, bf16[1024,4096]{1,0:T(8,128)(2,1)S(1)} %copy-done.12, bf16[6,256,512]{2,1,0:T(8,128)(2,1)S(1)} %pad_maximum_fusion.2.refs_2_, ...), custom_call_target="tpu_custom_call" | custom-call | flops 4300000256 | bytes 18874368 | tf_op jit(solution)/shard_map/matmul/pallas_call | solution.py:226
  164.6 3.8 %collective-permute-done.40.g1 = bf16[256,512]{1,0:T(8,128)(2,1)S(1)} collective-permute-done((bf16[256,512]{1,0:T(8,128)(2,1)S(1)}, bf16[256,512]{1,0:T(8,128)(2,1)S(1)}, u32[]{:S(2)}, u32[]{:S(2)}) %collective-permute-start.40) | collective-permute-done | bytes 262176 | tf_op jit(solution)/shard_map/ppermute | solution.py:100
  170.4 10.2 %collective-permute-done.41.g2 = bf16[256,512]{1,0:T(8,128)(2,1)} collective-permute-done((bf16[256,512]{1,0:T(8,128)(2,1)S(1)}, bf16[256,512]{1,0:T(8,128)(2,1)}, u32[]{:S(2)}, u32[]{:S(2)}) %collective-permute-start.41) | collective-permute-done | bytes 262176 | tf_op jit(solution)/shard_map/ppermute | solution.py:100
  189.6 4.7 %place.1 = bf16[8,2,256,512]{3,2,1,0:T(8,128)(2,1)} custom-call(s32[6]{0:T(128)S(1)} %add_add_fusion.1.meta, bf16[4,256,512]{2,1,0:T(8,128)(2,1)S(1)} %pad_maximum_fusion.3.own0, bf16[4,256,512]{2,1,0:T(8,128)(2,1)S(1)} %copy-done.6, bf16[4,256,512]{2,1,0:T(8,128)(2,1)} %collective-permute-done.44.peer0, bf16[4,256,512]{2,1,0:T(8,128)(2,1)} %collective-permute-done.45.peer1), custom_call_target="tpu_custom_call" | custom-call | flops 4000000 | bytes 8388608 | tf_op jit(solution)/shard_map/place/pallas_call | solution.py:136
  194.3 3.5 %project.5 = (bf16[256,512]{1,0:T(8,128)(2,1)S(1)}, f32[256,512]{1,0:T(8,128)S(1)}) custom-call(s32[2]{0:T(128)S(1)} %pad_add_fusion.meta, bf16[256,512]{1,0:T(8,128)(2,1)S(1)} %get-tuple-element.51.g0, bf16[256,512]{1,0:T(8,128)(2,1)S(1)} %copy-done.8, bf16[256,512]{1,0:T(8,128)(2,1)} %collective-permute-done.41.g2, ...), custom_call_target="tpu_custom_call" | custom-call | flops 1073741824 | bytes 8388608 | tf_op jit(solution)/shard_map/project/pallas_call | solution.py:270
  197.8 3.1 %collective-permute-start.43 = (bf16[256,512]{1,0:T(8,128)(2,1)S(1)}, bf16[256,512]{1,0:T(8,128)(2,1)S(1)}, u32[]{:S(2)}, u32[]{:S(2)}) collective-permute-start(bf16[256,512]{1,0:T(8,128)(2,1)S(1)} %get-tuple-element.53), channel_id=1, source_target_pairs={{0,1},{1,0},{2,3},{3,2},{4,5},{5,4},{6,7},{7,6},{8,9},{9,8},{10,11... | collective-permute-start | bytes 786440 | tf_op jit(solution)/shard_map/ppermute | solution.py:104
  201.0 5.8 %project.4 = (bf16[384,512]{1,0:T(8,128)(2,1)}, f32[384,512]{1,0:T(8,128)}) custom-call(s32[2]{0:T(128)} %copy-done.10, bf16[384,512]{1,0:T(8,128)(2,1)} %get-tuple-element.48.g0, bf16[384,512]{1,0:T(8,128)(2,1)} %collective-permute-done.36.g1, bf16[384,512]{1,0:T(8,128)(2,1)} %collective-permute-done.37.g2, bf16[384,512]{1,0:T(8,128)(2,1)} %collective-permute-done.38.g3, ...), custom_call_target="tpu_custom_call" | custom-call | flops 1610612736 | bytes 8388608 | tf_op jit(solution)/shard_map/project/pallas_call | solution.py:270
  207.5 4.3 %project.3 = (bf16[384,512]{1,0:T(8,128)(2,1)S(1)}, f32[384,512]{1,0:T(8,128)S(1)}) custom-call(s32[2]{0:T(128)S(1)} %copy-done.11, bf16[384,512]{1,0:T(8,128)(2,1)} %get-tuple-element.44.g0, bf16[384,512]{1,0:T(8,128)(2,1)} %collective-permute-done.20.g1, bf16[384,512]{1,0:T(8,128)(2,1)} %collective-permute-done.22.g2, ...), custom_call_target="tpu_custom_call" | custom-call | flops 1610612736 | bytes 8388608 | tf_op jit(solution)/shard_map/project/pallas_call | solution.py:270
  214.8 5.6 %collective-permute-done.39 = bf16[384,512]{1,0:T(8,128)(2,1)S(1)} collective-permute-done((bf16[384,512]{1,0:T(8,128)(2,1)}, bf16[384,512]{1,0:T(8,128)(2,1)S(1)}, u32[]{:S(2)}, u32[]{:S(2)}) %collective-permute-start.39) | collective-permute-done | bytes 393248 | tf_op jit(solution)/shard_map/ppermute | solution.py:104
  220.6 4.8 %collective-permute-done.35 = bf16[384,512]{1,0:T(8,128)(2,1)S(1)} collective-permute-done((bf16[384,512]{1,0:T(8,128)(2,1)S(1)}, bf16[384,512]{1,0:T(8,128)(2,1)S(1)}, u32[]{:S(2)}, u32[]{:S(2)}) %collective-permute-start.35) | collective-permute-done | bytes 393248 | tf_op jit(solution)/shard_map/ppermute | solution.py:104
  (166 shorter events, 59.1 us)
Async XLA Ops:
  5.4 12.0 %collective-permute-start = (bf16[208,256]{1,0:T(8,128)(2,1)}, bf16[208,256]{1,0:T(8,128)(2,1)S(1)}, u32[]{:S(2)}, u32[]{:S(2)}) collective-permute-start(bf16[208,256]{1,0:T(8,128)(2,1)} %get-tuple-element.32), channel_id=1, source_target_pairs={{0,1},{1,0},{2,3},{3,2},{4,5},{5,4},{6,7},{7,6},{8,9},{9,8},{10,11... | collective-permute-start | bytes 319496 | tf_op jit(solution)/shard_map/ppermute | solution.py:378
  11.0 11.2 %collective-permute-start.3 = (bf16[208,256]{1,0:T(8,128)(2,1)}, bf16[208,256]{1,0:T(8,128)(2,1)S(1)}, u32[]{:S(2)}, u32[]{:S(2)}) collective-permute-start(bf16[208,256]{1,0:T(8,128)(2,1)} %get-tuple-element.35), channel_id=1, source_target_pairs={{0,4},{1,5},{2,6},{3,7},{4,0},{5,1},{6,2},{7,3},{8,12},{9,13},{10,... | collective-permute-start | bytes 319496 | tf_op jit(solution)/shard_map/ppermute | solution.py:378
  32.6 11.8 %collective-permute-start.13 = (bf16[288,512]{1,0:T(8,128)(2,1)}, bf16[288,512]{1,0:T(8,128)(2,1)S(1)}, u32[]{:S(2)}, u32[]{:S(2)}) collective-permute-start(bf16[288,512]{1,0:T(8,128)(2,1)} %get-tuple-element.40), channel_id=1, source_target_pairs={{0,16},{8,24},{16,0},{24,8},{32,48},{40,56},{48,32},{56,40},{64,80... | collective-permute-start | bytes 884744 | tf_op jit(solution)/shard_map/ppermute | solution.py:92
  45.5 13.1 %collective-permute-start.15 = (bf16[2,288,512]{2,1,0:T(8,128)(2,1)S(1)}, bf16[2,288,512]{2,1,0:T(8,128)(2,1)S(1)}, u32[]{:S(2)}, u32[]{:S(2)}) collective-permute-start(bf16[2,288,512]{2,1,0:T(8,128)(2,1)S(1)} %pad_maximum_fusion.5), channel_id=1, source_target_pairs={{0,96},{8,104},{16,112},{24,120},{32,0},{40,8},{48,16},{56,24},{64... | collective-permute-start | bytes 1769480 | tf_op jit(solution)/shard_map/ppermute | solution.py:88
  48.7 13.2 %collective-permute-start.14 = (bf16[2,288,512]{2,1,0:T(8,128)(2,1)S(1)}, bf16[2,288,512]{2,1,0:T(8,128)(2,1)S(1)}, u32[]{:S(2)}, u32[]{:S(2)}) collective-permute-start(bf16[2,288,512]{2,1,0:T(8,128)(2,1)S(1)} %pad_maximum_fusion.5), channel_id=1, source_target_pairs={{0,32},{8,40},{16,48},{24,56},{32,64},{40,72},{48,80},{56,88},{64,... | collective-permute-start | bytes 1769480 | tf_op jit(solution)/shard_map/ppermute | solution.py:88
  48.8 14.6 %collective-permute-start.7 = (bf16[256,512]{1,0:T(8,128)(2,1)S(1)}, bf16[256,512]{1,0:T(8,128)(2,1)S(1)}, u32[]{:S(2)}, u32[]{:S(2)}) collective-permute-start(bf16[256,512]{1,0:T(8,128)(2,1)S(1)} %copy-done.16), channel_id=1, source_target_pairs={{0,16},{8,24},{16,0},{24,8},{32,48},{40,56},{48,32},{56,40},{64,80... | collective-permute-start | bytes 786440 | tf_op jit(solution)/shard_map/ppermute | solution.py:92
  52.2 26.5 %collective-permute-start.30 = (bf16[4,256,512]{2,1,0:T(8,128)(2,1)S(1)}, bf16[4,256,512]{2,1,0:T(8,128)(2,1)S(1)}, u32[]{:S(2)}, u32[]{:S(2)}) collective-permute-start(bf16[4,256,512]{2,1,0:T(8,128)(2,1)S(1)} %pad_maximum_fusion.3.own0), channel_id=1, source_target_pairs={{0,16},{8,24},{16,0},{24,8},{32,48},{40,56},{48,32},{56,40},{64,80... | collective-permute-start | bytes 3145736 | tf_op jit(solution)/shard_map/ppermute | solution.py:92
  54.2 13.2 %collective-permute-start.29 = (bf16[256,512]{1,0:T(8,128)(2,1)S(1)}, bf16[256,512]{1,0:T(8,128)(2,1)S(1)}, u32[]{:S(2)}, u32[]{:S(2)}) collective-permute-start(bf16[256,512]{1,0:T(8,128)(2,1)S(1)} %get-tuple-element.58), channel_id=1, source_target_pairs={{0,2},{1,3},{2,4},{3,5},{4,6},{5,7},{6,0},{7,1},{8,10},{9,11},{10,... | collective-permute-start | bytes 786440 | tf_op jit(solution)/shard_map/ppermute | solution.py:100
  63.4 63.3 %collective-permute-start.16 = (bf16[6,288,512]{2,1,0:T(8,128)(2,1)}, bf16[6,288,512]{2,1,0:T(8,128)(2,1)}, u32[]{:S(2)}, u32[]{:S(2)}) collective-permute-start(bf16[6,288,512]{2,1,0:T(8,128)(2,1)} %pad_maximum_fusion.1.refs_2_), channel_id=1, source_target_pairs={{0,8},{8,0},{16,24},{24,16},{32,40},{40,32},{48,56},{56,48},{64,72... | collective-permute-start | bytes 5308424 | tf_op jit(solution)/shard_map/ppermute | solution.py:96
  69.4 39.3 %collective-permute-start.9 = (bf16[2,256,512]{2,1,0:T(8,128)(2,1)S(1)}, bf16[2,256,512]{2,1,0:T(8,128)(2,1)S(1)}, u32[]{:S(2)}, u32[]{:S(2)}) collective-permute-start(bf16[2,256,512]{2,1,0:T(8,128)(2,1)S(1)} %pad_maximum_fusion.7), channel_id=1, source_target_pairs={{0,96},{8,104},{16,112},{24,120},{32,0},{40,8},{48,16},{56,24},{64... | collective-permute-start | bytes 1572872 | tf_op jit(solution)/shard_map/ppermute | solution.py:88
  74.0 34.8 %collective-permute-start.8 = (bf16[2,256,512]{2,1,0:T(8,128)(2,1)S(1)}, bf16[2,256,512]{2,1,0:T(8,128)(2,1)S(1)}, u32[]{:S(2)}, u32[]{:S(2)}) collective-permute-start(bf16[2,256,512]{2,1,0:T(8,128)(2,1)S(1)} %pad_maximum_fusion.7), channel_id=1, source_target_pairs={{0,32},{8,40},{16,48},{24,56},{32,64},{40,72},{48,80},{56,88},{64,... | collective-permute-start | bytes 1572872 | tf_op jit(solution)/shard_map/ppermute | solution.py:88
  77.4 35.2 %collective-permute-start.11 = (bf16[2,256,512]{2,1,0:T(8,128)(2,1)S(1)}, bf16[2,256,512]{2,1,0:T(8,128)(2,1)}, u32[]{:S(2)}, u32[]{:S(2)}) collective-permute-start(bf16[2,256,512]{2,1,0:T(8,128)(2,1)S(1)} %pad_maximum_fusion.7), channel_id=1, source_target_pairs={{0,64},{8,72},{16,80},{24,88},{32,96},{40,104},{48,112},{56,120},{... | collective-permute-start | bytes 1572872 | tf_op jit(solution)/shard_map/ppermute | solution.py:88
  78.7 27.5 %collective-permute-start.17 = (bf16[288,512]{1,0:T(8,128)(2,1)S(1)}, bf16[288,512]{1,0:T(8,128)(2,1)S(1)}, u32[]{:S(2)}, u32[]{:S(2)}) collective-permute-start(bf16[288,512]{1,0:T(8,128)(2,1)S(1)} %slice_bitcast_fusion.1), channel_id=1, source_target_pairs={{0,32},{8,40},{16,48},{24,56},{32,64},{40,72},{48,80},{56,88},{64,... | collective-permute-start | bytes 884744 | tf_op jit(solution)/shard_map/ppermute | solution.py:88
  108.7 15.9 %collective-permute-start.19 = (bf16[2,288,512]{2,1,0:T(8,128)(2,1)S(1)}, bf16[2,288,512]{2,1,0:T(8,128)(2,1)S(1)}, u32[]{:S(2)}, u32[]{:S(2)}) collective-permute-start(bf16[2,288,512]{2,1,0:T(8,128)(2,1)S(1)} %pad_maximum_fusion.6.refs_4_), channel_id=1, source_target_pairs={{0,8},{8,0},{16,24},{24,16},{32,40},{40,32},{48,56},{56,48},{64,72... | collective-permute-start | bytes 1769480 | tf_op jit(solution)/shard_map/ppermute | solution.py:96
  108.8 13.2 %collective-permute-start.32 = (bf16[256,512]{1,0:T(8,128)(2,1)S(1)}, bf16[256,512]{1,0:T(8,128)(2,1)S(1)}, u32[]{:S(2)}, u32[]{:S(2)}) collective-permute-start(bf16[256,512]{1,0:T(8,128)(2,1)S(1)} %get-tuple-element.63), channel_id=1, source_target_pairs={{0,4},{1,5},{2,6},{3,7},{4,0},{5,1},{6,2},{7,3},{8,12},{9,13},{10,... | collective-permute-start | bytes 786440 | tf_op jit(solution)/shard_map/ppermute | solution.py:100
  112.6 11.7 %collective-permute-start.31 = (bf16[256,512]{1,0:T(8,128)(2,1)S(1)}, bf16[256,512]{1,0:T(8,128)(2,1)S(1)}, u32[]{:S(2)}, u32[]{:S(2)}) collective-permute-start(bf16[256,512]{1,0:T(8,128)(2,1)S(1)} %get-tuple-element.64), channel_id=1, source_target_pairs={{0,6},{1,7},{2,0},{3,1},{4,2},{5,3},{6,4},{7,5},{8,14},{9,15},{10,... | collective-permute-start | bytes 786440 | tf_op jit(solution)/shard_map/ppermute | solution.py:100
  116.2 29.2 %collective-permute-start.10 = (bf16[6,256,512]{2,1,0:T(8,128)(2,1)S(1)}, bf16[6,256,512]{2,1,0:T(8,128)(2,1)}, u32[]{:S(2)}, u32[]{:S(2)}) collective-permute-start(bf16[6,256,512]{2,1,0:T(8,128)(2,1)S(1)} %pad_maximum_fusion.2.refs_2_), channel_id=1, source_target_pairs={{0,8},{8,0},{16,24},{24,16},{32,40},{40,32},{48,56},{56,48},{64,72... | collective-permute-start | bytes 4718600 | tf_op jit(solution)/shard_map/ppermute | solution.py:96
  122.0 39.8 %collective-permute-start.44 = (bf16[4,256,512]{2,1,0:T(8,128)(2,1)S(1)}, bf16[4,256,512]{2,1,0:T(8,128)(2,1)}, u32[]{:S(2)}, u32[]{:S(2)}) collective-permute-start(bf16[4,256,512]{2,1,0:T(8,128)(2,1)S(1)} %pad_maximum_fusion.3.own0), channel_id=1, source_target_pairs={{0,8},{8,0},{16,24},{24,16},{32,40},{40,32},{48,56},{56,48},{64,72... | collective-permute-start | bytes 3145736 | tf_op jit(solution)/shard_map/ppermute | solution.py:96
  124.3 21.1 %collective-permute-start.12 = (bf16[2,256,512]{2,1,0:T(8,128)(2,1)}, bf16[2,256,512]{2,1,0:T(8,128)(2,1)}, u32[]{:S(2)}, u32[]{:S(2)}) collective-permute-start(bf16[2,256,512]{2,1,0:T(8,128)(2,1)} %collective-permute-done.11.refs_4_), channel_id=1, source_target_pairs={{0,8},{8,0},{16,24},{24,16},{32,40},{40,32},{48,56},{56,48},{64,72... | collective-permute-start | bytes 1572872 | tf_op jit(solution)/shard_map/ppermute | solution.py:96
  125.9 37.9 %collective-permute-start.45 = (bf16[4,256,512]{2,1,0:T(8,128)(2,1)S(1)}, bf16[4,256,512]{2,1,0:T(8,128)(2,1)}, u32[]{:S(2)}, u32[]{:S(2)}) collective-permute-start(bf16[4,256,512]{2,1,0:T(8,128)(2,1)S(1)} %copy-done.5), channel_id=1, source_target_pairs={{0,8},{8,0},{16,24},{24,16},{32,40},{40,32},{48,56},{56,48},{64,72... | collective-permute-start | bytes 3145736 | tf_op jit(solution)/shard_map/ppermute | solution.py:96
  126.7 67.6 %collective-permute-start.34 = (bf16[2,4,256,512]{3,2,1,0:T(8,128)(2,1)S(1)}, bf16[2,4,256,512]{3,2,1,0:T(8,128)(2,1)}, u32[]{:S(2)}, u32[]{:S(2)}) collective-permute-start(bf16[2,4,256,512]{3,2,1,0:T(8,128)(2,1)S(1)} %pad_maximum_fusion.own_ref), channel_id=1, source_target_pairs={{0,8},{8,0},{16,24},{24,16},{32,40},{40,32},{48,56},{56,48},{64,72... | collective-permute-start | bytes 6291464 | tf_op jit(solution)/shard_map/ppermute | solution.py:96
  161.8 21.5 %collective-permute-start.36 = (bf16[384,512]{1,0:T(8,128)(2,1)}, bf16[384,512]{1,0:T(8,128)(2,1)}, u32[]{:S(2)}, u32[]{:S(2)}) collective-permute-start(bf16[384,512]{1,0:T(8,128)(2,1)} %get-tuple-element.48.g0), channel_id=1, source_target_pairs={{0,6},{1,7},{2,0},{3,1},{4,2},{5,3},{6,4},{7,5},{8,14},{9,15},{10,... | collective-permute-start | bytes 1179656 | tf_op jit(solution)/shard_map/ppermute | solution.py:100
  161.8 24.5 %collective-permute-start.21 = (bf16[384,512]{1,0:T(8,128)(2,1)}, bf16[384,512]{1,0:T(8,128)(2,1)}, u32[]{:S(2)}, u32[]{:S(2)}) collective-permute-start(bf16[384,512]{1,0:T(8,128)(2,1)} %get-tuple-element.44.g0), channel_id=1, source_target_pairs={{0,2},{1,3},{2,4},{3,5},{4,6},{5,7},{6,0},{7,1},{8,10},{9,11},{10,... | collective-permute-start | bytes 1179656 | tf_op jit(solution)/shard_map/ppermute | solution.py:100
  163.8 16.8 %collective-permute-start.41 = (bf16[256,512]{1,0:T(8,128)(2,1)S(1)}, bf16[256,512]{1,0:T(8,128)(2,1)}, u32[]{:S(2)}, u32[]{:S(2)}) collective-permute-start(bf16[256,512]{1,0:T(8,128)(2,1)S(1)} %get-tuple-element.51.g0), channel_id=1, source_target_pairs={{0,4},{1,5},{2,6},{3,7},{4,0},{5,1},{6,2},{7,3},{8,12},{9,13},{10,... | collective-permute-start | bytes 786440 | tf_op jit(solution)/shard_map/ppermute | solution.py:100
  169.2 17.0 %collective-permute-start.42 = (bf16[256,512]{1,0:T(8,128)(2,1)S(1)}, bf16[256,512]{1,0:T(8,128)(2,1)}, u32[]{:S(2)}, u32[]{:S(2)}) collective-permute-start(bf16[256,512]{1,0:T(8,128)(2,1)S(1)} %get-tuple-element.51.g0), channel_id=1, source_target_pairs={{0,2},{1,3},{2,4},{3,5},{4,6},{5,7},{6,0},{7,1},{8,10},{9,11},{10,... | collective-permute-start | bytes 786440 | tf_op jit(solution)/shard_map/ppermute | solution.py:100
  180.5 20.4 %collective-permute-start.38 = (bf16[384,512]{1,0:T(8,128)(2,1)}, bf16[384,512]{1,0:T(8,128)(2,1)}, u32[]{:S(2)}, u32[]{:S(2)}) collective-permute-start(bf16[384,512]{1,0:T(8,128)(2,1)} %get-tuple-element.48.g0), channel_id=1, source_target_pairs={{0,2},{1,3},{2,4},{3,5},{4,6},{5,7},{6,0},{7,1},{8,10},{9,11},{10,... | collective-permute-start | bytes 1179656 | tf_op jit(solution)/shard_map/ppermute | solution.py:100
  183.3 17.7 %collective-permute-start.37 = (bf16[384,512]{1,0:T(8,128)(2,1)}, bf16[384,512]{1,0:T(8,128)(2,1)}, u32[]{:S(2)}, u32[]{:S(2)}) collective-permute-start(bf16[384,512]{1,0:T(8,128)(2,1)} %collective-permute-done.36.g1), channel_id=1, source_target_pairs={{0,6},{1,7},{2,0},{3,1},{4,2},{5,3},{6,4},{7,5},{8,14},{9,15},{10,... | collective-permute-start | bytes 1179656 | tf_op jit(solution)/shard_map/ppermute | solution.py:100
  186.2 21.3 %collective-permute-start.20 = (bf16[384,512]{1,0:T(8,128)(2,1)}, bf16[384,512]{1,0:T(8,128)(2,1)}, u32[]{:S(2)}, u32[]{:S(2)}) collective-permute-start(bf16[384,512]{1,0:T(8,128)(2,1)} %get-tuple-element.44.g0), channel_id=1, source_target_pairs={{0,6},{1,7},{2,0},{3,1},{4,2},{5,3},{6,4},{7,5},{8,14},{9,15},{10,... | collective-permute-start | bytes 1179656 | tf_op jit(solution)/shard_map/ppermute | solution.py:100
  186.3 21.1 %collective-permute-start.22 = (bf16[384,512]{1,0:T(8,128)(2,1)}, bf16[384,512]{1,0:T(8,128)(2,1)}, u32[]{:S(2)}, u32[]{:S(2)}) collective-permute-start(bf16[384,512]{1,0:T(8,128)(2,1)} %collective-permute-done.21.g3), channel_id=1, source_target_pairs={{0,2},{1,3},{2,4},{3,5},{4,6},{5,7},{6,0},{7,1},{8,10},{9,11},{10,... | collective-permute-start | bytes 1179656 | tf_op jit(solution)/shard_map/ppermute | solution.py:100
  197.8 16.9 %collective-permute-start.43 = (bf16[256,512]{1,0:T(8,128)(2,1)S(1)}, bf16[256,512]{1,0:T(8,128)(2,1)S(1)}, u32[]{:S(2)}, u32[]{:S(2)}) collective-permute-start(bf16[256,512]{1,0:T(8,128)(2,1)S(1)} %get-tuple-element.53), channel_id=1, source_target_pairs={{0,1},{1,0},{2,3},{3,2},{4,5},{5,4},{6,7},{7,6},{8,9},{9,8},{10,11... | collective-permute-start | bytes 786440 | tf_op jit(solution)/shard_map/ppermute | solution.py:104
  206.7 13.7 %collective-permute-start.39 = (bf16[384,512]{1,0:T(8,128)(2,1)}, bf16[384,512]{1,0:T(8,128)(2,1)S(1)}, u32[]{:S(2)}, u32[]{:S(2)}) collective-permute-start(bf16[384,512]{1,0:T(8,128)(2,1)} %get-tuple-element.50), channel_id=1, source_target_pairs={{0,1},{1,0},{2,3},{3,2},{4,5},{5,4},{6,7},{7,6},{8,9},{9,8},{10,11... | collective-permute-start | bytes 1179656 | tf_op jit(solution)/shard_map/ppermute | solution.py:104
  211.8 13.6 %collective-permute-start.35 = (bf16[384,512]{1,0:T(8,128)(2,1)S(1)}, bf16[384,512]{1,0:T(8,128)(2,1)S(1)}, u32[]{:S(2)}, u32[]{:S(2)}) collective-permute-start(bf16[384,512]{1,0:T(8,128)(2,1)S(1)} %get-tuple-element.47), channel_id=1, source_target_pairs={{0,1},{1,0},{2,3},{3,2},{4,5},{5,4},{6,7},{7,6},{8,9},{9,8},{10,11... | collective-permute-start | bytes 1179656 | tf_op jit(solution)/shard_map/ppermute | solution.py:104
  (47 other events, 553.1 us)
